TPU v7x, 32 devices: a whole 2x2x4 slice. The times are simulated.
32 devices in a mesh: group: 2 (over x), expert: 8 (over z, y), dp: 2 (over core).
Axes of the slice: x: 2, y: 2, z: 4, core: 2. Of those that a mesh axis runs over, the one named last changes fastest.
Arguments:
- tokens: bfloat16 [4096, 2048], P(('group', 'expert', 'dp')), parts along dimension 0, may hold values from -30 to 30
- expert_choice: int32 [4096, 2], P(('group', 'expert', 'dp')), parts along dimension 0, may hold values from 0 to 3, all different within a row; in each aligned block of 128 rows (0 to 127, 128 to 255, ...) at most 70 rows name the same one
- gate_weights: float32 [4096, 2], P(('group', 'expert', 'dp')), parts along dimension 0, may hold values from 0.1 to 1
- attention_gain: float32 [2048], replicated, may hold values from 0.1 to 1.9
- query_weight: bfloat16 [2048, 2048], P('dp'), may hold values from -0.13258252 to 0.13258252
- key_value_weight: bfloat16 [2048, 1024], P('dp'), may hold values from -3.2040776022515436 to 3.2040776022515436
- output_weight: bfloat16 [2048, 2048], P('dp'), may hold values from -0.125 to 0.125
- feedforward_gain: float32 [2048], replicated, may hold values from 0.1 to 1.9
- expert_gate: bfloat16 [2048, 28672], P(None, ('expert', 'dp')), may hold values from -0.125 to 0.125
- expert_up: bfloat16 [2048, 28672], P(None, ('expert', 'dp')), may hold values from -0.125 to 0.125
- expert_down: bfloat16 [28672, 2048], P(('expert', 'dp')), may hold values from -0.0625 to 0.0625
Outputs:
- layer_output: bfloat16 [4096, 2048], P(('group', 'expert', 'dp')), parts along dimension 0
There are 2 independent parts, one for each index of `group`. A program takes and returns all parts, laid end to end along the dimension named above; an argument that names none is the same for every part. Nothing has to cross between parts.
Inputs may be any that keep to these rules, and one draw needn't show every extreme that they name: `expert_choice`: each row names 2 different experts; within the rows of one device no expert is named more than 70 times, and some device's expert is named exactly 70 times.
All inputs are finite; a program needn't handle non-finite values.
Results may differ from a plain program's by a relative error of at most 0.012.
Values may be sent and summed in bfloat16 or wider, within the bound.
No kernel may reach another device: no remote copies, remote signals or barrier semaphores. Data moves between devices by JAX's collectives and lax.ppermute only.
A program may use at most 128 MiB of HBM per device.

v0:
```python
import functools
import math

import jax
import jax.numpy as jnp
from jax import lax
from jax.experimental import pallas as pl
from jax.experimental.pallas import tpu as pltpu
from jax.sharding import PartitionSpec as P


HEAD_DIM = 128
EXPERTS = 4
CAP = 70
ROWS = -(-CAP // 8) * 8

HIDDEN_STEP = 256
DOWN_STEP = 256
ORDER = (0, 1, 2, 3)

epsilon = 1e-05
base_theta = 1000000.0
masked_score = -1e30

VMEM = pl.BlockSpec(memory_space=pltpu.VMEM)
f32 = jnp.float32
bf16 = jnp.bfloat16


def dot(a, b):
    return jnp.dot(a, b, preferred_element_type=f32)


def call(kernel, outs, operands, scratch=(), flops=0, moved=0, limit=16 << 20):
    return pl.pallas_call(
        kernel,
        out_shape=outs,
        in_specs=[VMEM] * len(operands),
        out_specs=jax.tree.map(lambda _: VMEM, outs),
        scratch_shapes=list(scratch),
        compiler_params=pltpu.CompilerParams(vmem_limit_bytes=limit),
        cost_estimate=pl.CostEstimate(flops=flops, bytes_accessed=moved, transcendentals=0),
    )(*operands)


def normalized(widened, gain):
    spread = jnp.mean(widened * widened, axis=-1, keepdims=True)
    return (widened * lax.rsqrt(spread + epsilon) * gain).astype(bf16)


def norm_kernel(tokens_ref, gain_ref, keep_ref, send_ref, whole_ref):
    half = keep_ref.shape[1]
    whole_ref[...] = normalized(tokens_ref[...].astype(f32), gain_ref[...])
    core = lax.axis_index("dp")
    keep_ref[...] = whole_ref[:, pl.ds(pl.multiple_of(core * half, half), half)]
    send_ref[...] = whole_ref[:, pl.ds(pl.multiple_of((1 - core) * half, half), half)]


def keyval_kernel(mine_ref, theirs_ref, weight_ref, keep_ref, send_ref):
    rows = jnp.concatenate([mine_ref[...], theirs_ref[...]], axis=0)
    width = keep_ref.shape[1] // 2
    core = lax.axis_index("dp")
    for out_ref, owner in ((send_ref, 1 - core), (keep_ref, core)):
        for part in range(2):
            start = pl.multiple_of((part * 2 + owner) * width, width)
            out_ref[:, part * width : (part + 1) * width] = dot(
                rows, weight_ref[:, pl.ds(start, width)]
            )


def query_kernel(mine_ref, theirs_ref, weight_ref, keep_ref, send_ref):
    rows = jnp.concatenate([mine_ref[...], theirs_ref[...]], axis=0)
    width = keep_ref.shape[1]
    step = min(512, width)
    core = lax.axis_index("dp")
    for out_ref, owner in ((send_ref, 1 - core), (keep_ref, core)):
        for offset in range(0, width, step):
            start = pl.multiple_of(owner * width + offset, step)
            out_ref[:, offset : offset + step] = dot(rows, weight_ref[:, pl.ds(start, step)])


def summed(keep_ref, came_ref, columns):
    half = keep_ref.shape[0] // 2
    came = came_ref[:, columns]
    return keep_ref[:, columns] + jnp.concatenate([came[half:], came[:half]], axis=0)


def turned(vectors, cosine, sine):
    return vectors * cosine + pltpu.roll(vectors, HEAD_DIM // 2, 1) * sine


def keyval_turn_kernel(keep_ref, came_ref, cosine_ref, sine_ref, out_ref):
    width = out_ref.shape[1]
    for start in range(0, width, HEAD_DIM):
        columns = slice(start, start + HEAD_DIM)
        total = summed(keep_ref, came_ref, columns)
        if start < width // 2:
            total = turned(total, cosine_ref[...], sine_ref[...])
        out_ref[:, columns] = total.astype(bf16)


def query_turn_kernel(keep_ref, came_ref, cosine_ref, sine_ref, out_ref):
    for head in range(out_ref.shape[0]):
        columns = slice(head * HEAD_DIM, (head + 1) * HEAD_DIM)
        total = summed(keep_ref, came_ref, columns)
        out_ref[head] = turned(total, cosine_ref[...], sine_ref[...]).astype(bf16)


def attention_kernel(places, along, query_ref, weight_ref, *refs):
    keyval_refs = refs[: len(places)]
    send_ref, keep_ref, score_ref, context_ref = refs[len(places) :]
    heads, rows, _ = query_ref.shape
    half = rows // 2
    shared = keyval_refs[0].shape[1] // (2 * HEAD_DIM)
    sharing = heads // shared
    core = lax.axis_index("dp")
    chip = lax.axis_index("expert")
    plane, place = chip // along, chip % along

    def position(shape, axis):
        row = lax.broadcasted_iota(jnp.int32, shape, axis)
        return jnp.where(core == 0, row, jnp.where(row < half, row + half, row - half))

    own_visible = position((rows, rows), 1) <= position((rows, rows), 0)
    seen = []
    for back, turn in places:
        if back == 0:
            seen.append((place ^ turn) < place)
        else:
            seen.append(plane >= back)
    factor = HEAD_DIM ** (-0.5) * math.log2(math.e)

    for group in range(shared):
        key_columns = slice(group * HEAD_DIM, (group + 1) * HEAD_DIM)
        value_columns = slice((shared + group) * HEAD_DIM, (shared + group + 1) * HEAD_DIM)

        def one_head(member, _):
            head = group * sharing + member
            query = query_ref[head]
            highest = jnp.full((rows, HEAD_DIM), masked_score, f32)
            for index, keyval_ref in enumerate(keyval_refs):
                score = lax.dot_general(
                    query,
                    keyval_ref[:, key_columns],
                    (((1,), (1,)), ((), ())),
                    preferred_element_type=f32,
                ) * factor
                if index == 0:
                    score = jnp.where(own_visible, score, masked_score)
                score_ref[:, index * rows : (index + 1) * rows] = score
                most = score[:, :HEAD_DIM]
                for start in range(HEAD_DIM, rows, HEAD_DIM):
                    most = jnp.maximum(most, score[:, start : start + HEAD_DIM])
                if index > 0:
                    most = jnp.where(seen[index], most, masked_score)
                highest = jnp.maximum(highest, most)
            highest = jnp.max(highest, axis=-1, keepdims=True)
            totals = jnp.zeros((rows, HEAD_DIM), f32)
            mixed = jnp.zeros((rows, HEAD_DIM), f32)
            for index, keyval_ref in enumerate(keyval_refs):
                ceiling = highest
                if index > 0:
                    ceiling = jnp.where(seen[index], highest, -masked_score)
                expo = jnp.exp2(score_ref[:, index * rows : (index + 1) * rows] - ceiling)
                for start in range(0, rows, HEAD_DIM):
                    totals = totals + expo[:, start : start + HEAD_DIM]
                mixed = mixed + dot(expo.astype(bf16), keyval_ref[:, value_columns])
            total = jnp.sum(totals, axis=-1, keepdims=True)
            context_ref[head] = (mixed / total).astype(bf16)
            return 0

        lax.fori_loop(0, sharing, one_head, 0)

    context = jnp.concatenate([context_ref[head] for head in range(heads)], axis=1)
    step = min(512, send_ref.shape[1])
    for start in range(0, send_ref.shape[1], step):
        columns = slice(start, start + step)
        out = dot(context, weight_ref[:, columns])
        keep_ref[:, columns] = out[:half]
        send_ref[:, columns] = out[half:].astype(bf16)


def as_columns(rows_ref):
    count = rows_ref.shape[1]
    same = (
        lax.broadcasted_iota(jnp.int32, (count, count), 0)
        == lax.broadcasted_iota(jnp.int32, (count, count), 1)
    )
    return lax.dot_general(
        same.astype(f32),
        rows_ref[...].astype(f32),
        (((1,), (1,)), ((), ())),
        precision=lax.Precision.HIGHEST,
        preferred_element_type=f32,
    )


def placed(choice, plane):
    rows = choice.shape[0]
    first, second = choice[:, 0:1], choice[:, 1:2]
    lane = lax.broadcasted_iota(jnp.int32, (rows, 128), 1)
    goes = jnp.zeros((rows, 128), jnp.bool_)
    for step in range(EXPERTS):
        expert = plane ^ step
        goes = goes | ((lane == step) & ((first == expert) | (second == expert)))
    earlier = (
        lax.broadcasted_iota(jnp.int32, (rows, rows), 1)
        < lax.broadcasted_iota(jnp.int32, (rows, rows), 0)
    )
    slots = dot(earlier.astype(bf16), goes.astype(bf16)).astype(jnp.int32)
    slots = jnp.where(goes, slots, -1)
    return [
        (lane[:, :ROWS] == slots[:, step : step + 1]).astype(bf16) for step in range(EXPERTS)
    ]


def pack_kernel(along, keep_ref, came_ref, tokens_ref, gain_ref, choice_ref, residual_ref, *out_refs):
    attention = keep_ref[...] + came_ref[...].astype(f32)
    residual = (tokens_ref[...].astype(f32) + attention).astype(bf16)
    residual_ref[...] = residual
    mixed_in = normalized(residual.astype(f32), gain_ref[...])
    plane = lax.axis_index("expert") // along
    choice = as_columns(choice_ref).astype(jnp.int32)
    for out_ref, routing in zip(out_refs, placed(choice, plane)):
        out_ref[...] = lax.dot_general(
            routing, mixed_in, (((0,), (0,)), ((), ())), preferred_element_type=f32
        ).astype(bf16)


def fetch_kernel(parts, from_ref, to_ref, sem):
    rows = from_ref.shape[0] // parts
    copies = []
    for part in range(parts):
        block = pl.ds(part * rows, rows)
        copies.append(
            pltpu.make_async_copy(from_ref.at[block], to_ref.at[block], sem.at[part])
        )
    for copy in copies:
        copy.start()
    for copy in copies:
        copy.wait()


def fetched(weight):
    parts = 4
    return pl.pallas_call(
        functools.partial(fetch_kernel, parts),
        out_shape=jax.ShapeDtypeStruct(weight.shape, weight.dtype),
        in_specs=[pl.BlockSpec(memory_space=pltpu.HBM)],
        out_specs=VMEM,
        scratch_shapes=[pltpu.SemaphoreType.DMA((parts,))],
        compiler_params=pltpu.CompilerParams(vmem_limit_bytes=2 << 20),
        cost_estimate=pl.CostEstimate(
            flops=0, bytes_accessed=4 * weight.size, transcendentals=0
        ),
        name="fetch",
    )(weight)


def expert_kernel(count, gate_ref, up_ref, down_ref, *refs):
    row_refs, out_refs, hidden_ref = refs[:count], refs[count : 2 * count], refs[2 * count]
    rows = jnp.concatenate([row_ref[...] for row_ref in row_refs], axis=0)
    for start in range(0, hidden_ref.shape[1], HIDDEN_STEP):
        columns = slice(start, start + HIDDEN_STEP)
        gate = dot(rows, gate_ref[:, columns])
        upward = dot(rows, up_ref[:, columns])
        hidden_ref[:, columns] = (gate / (1.0 + jnp.exp(-gate)) * upward).astype(bf16)
    hidden = hidden_ref[...]
    for start in range(0, down_ref.shape[1], DOWN_STEP):
        columns = slice(start, start + DOWN_STEP)
        out = dot(hidden, down_ref[:, columns]).astype(bf16)
        for index, out_ref in enumerate(out_refs):
            out_ref[:, columns] = out[index * ROWS : (index + 1) * ROWS]


def experts(rows, expert_gate, expert_up, expert_down):
    width, hidden = expert_gate.shape
    count = len(rows)
    return call(
        functools.partial(expert_kernel, count),
        [jax.ShapeDtypeStruct((ROWS, width), bf16)] * count,
        (expert_gate, expert_up, expert_down, *rows),
        scratch=[pltpu.VMEM((count * ROWS, hidden), bf16)],
        flops=6 * count * ROWS * width * hidden,
        moved=6 * width * hidden,
        limit=12 << 20,
    )


def combine_kernel(along, residual_ref, choice_ref, weight_ref, *refs):
    row_refs, out_ref = refs[:-1], refs[-1]
    plane = lax.axis_index("expert") // along
    choice = as_columns(choice_ref).astype(jnp.int32)
    weights = as_columns(weight_ref)
    total = residual_ref[...].astype(f32)
    for step, routing in enumerate(placed(choice, plane)):
        expert = plane ^ step
        weight = jnp.sum(jnp.where(choice == expert, weights, 0.0), axis=1, keepdims=True)
        total = total + weight * dot(routing, row_refs[step][...])
    out_ref[...] = total.astype(bf16)


def add(*terms):
    return sum(term.astype(f32) for term in terms).astype(bf16)


def body(
    tokens,
    expert_choice,
    gate_weights,
    attention_gain,
    query_weight,
    key_value_weight,
    output_weight,
    feedforward_gain,
    expert_gate,
    expert_up,
    expert_down,
):
    local_rows, model_width = tokens.shape
    share = query_weight.shape[0]
    cores = lax.axis_size("dp")
    chips = lax.axis_size("expert")
    along = chips // EXPERTS
    query_width = query_weight.shape[1] // cores
    keyval_width = key_value_weight.shape[1] // cores
    heads = query_width // HEAD_DIM
    pair_rows = local_rows * cores
    chip = lax.axis_index("expert")
    core = lax.axis_index("dp")

    def across(x):
        return lax.ppermute(x, "dp", [(i, i ^ 1) for i in range(cores)])

    def beside(x, turn):
        return lax.ppermute(x, "expert", [(i, i ^ turn) for i in range(chips)])

    def upward(x):
        return lax.ppermute(x, "expert", [(i, (i + along) % chips) for i in range(chips)])

    def planes(x, step):
        return lax.ppermute(x, "expert", [(i, i ^ (step * along)) for i in range(chips)])

    order = jnp.arange(pair_rows, dtype=jnp.int32)
    order = (order + core * local_rows) % pair_rows
    positions = chip * pair_rows + order
    halfway = HEAD_DIM // 2
    powers = jnp.arange(halfway, dtype=f32) * (2.0 / HEAD_DIM)
    inverse = base_theta ** (-powers)
    angles = positions.astype(f32)[:, None] * inverse[None, :]
    cosine, sine = jnp.cos(angles), jnp.sin(angles)
    cosine = jnp.concatenate([cosine, cosine], axis=1)
    sine = jnp.concatenate([-sine, sine], axis=1)

    shape = jax.ShapeDtypeStruct
    mine, outgoing = call(
        norm_kernel,
        [shape((local_rows, share), bf16)] * 2,
        (tokens, attention_gain.reshape(1, -1)),
        scratch=[pltpu.VMEM((local_rows, model_width), bf16)],
        flops=8 * local_rows * model_width,
        moved=4 * local_rows * model_width,
    )
    theirs = across(outgoing)
    keyval_keep, keyval_send = call(
        keyval_kernel,
        [shape((pair_rows, keyval_width), f32)] * 2,
        (mine, theirs, key_value_weight),
        flops=4 * pair_rows * share * keyval_width,
        moved=4 * share * keyval_width,
    )
    keyval_came = across(keyval_send)
    query_keep, query_send = call(
        query_kernel,
        [shape((pair_rows, query_width), f32)] * 2,
        (mine, theirs, query_weight),
        flops=4 * pair_rows * share * query_width,
        moved=4 * share * query_width,
    )
    query_came = across(query_send)
    keyval = call(
        keyval_turn_kernel,
        shape((pair_rows, keyval_width), bf16),
        (keyval_keep, keyval_came, cosine, sine),
        flops=8 * pair_rows * keyval_width,
        moved=10 * pair_rows * keyval_width,
    )
    queries = call(
        query_turn_kernel,
        shape((heads, pair_rows, HEAD_DIM), bf16),
        (query_keep, query_came, cosine, sine),
        flops=8 * pair_rows * query_width,
        moved=10 * pair_rows * query_width,
    )
    blocks, places = [], []
    line = keyval
    for back in range(EXPERTS):
        if back:
            line = upward(line)
        for turn in range(along):
            blocks.append(beside(line, turn) if turn else line)
            places.append((back, turn))
    attention_send, attention_keep = call(
        functools.partial(attention_kernel, tuple(places), along),
        [shape((local_rows, model_width), bf16), shape((local_rows, model_width), f32)],
        (queries, output_weight, *blocks),
        scratch=[
            pltpu.VMEM((pair_rows, pair_rows * len(blocks)), f32),
            pltpu.VMEM((heads, pair_rows, HEAD_DIM), bf16),
        ],
        flops=4 * pair_rows * pair_rows * len(blocks) * query_width
        + 2 * pair_rows * query_width * model_width,
        moved=2 * query_width * model_width,
        limit=20 << 20,
    )
    attention_came = across(attention_send)
    residual, *packed = call(
        functools.partial(pack_kernel, along),
        [shape((local_rows, model_width), bf16)] + [shape((ROWS, model_width), bf16)] * EXPERTS,
        (
            attention_keep,
            attention_came,
            tokens,
            feedforward_gain.reshape(1, -1),
            expert_choice.T,
        ),
        flops=2 * EXPERTS * ROWS * local_rows * model_width,
        moved=12 * local_rows * model_width,
    )
    expert_gate = fetched(expert_gate)
    expert_up = fetched(expert_up)
    expert_down = fetched(expert_down)
    arrived = {}
    for step in ORDER:
        arrived[step] = planes(packed[step], step) if step else packed[step]
    collected = [None] * EXPERTS
    for step in ORDER:
        line = [arrived[step]] + [beside(arrived[step], turn) for turn in range(1, along)]
        line = line + [across(x) for x in line]
        outs = experts(line, expert_gate, expert_up, expert_down)
        others = [across(x) for x in outs[along:]]
        near = [add(own, other) for own, other in zip(outs[:along], others)]
        others = [beside(near[turn], turn) for turn in range(1, along)]
        reduced = add(near[0], *others)
        collected[step] = planes(reduced, step) if step else reduced
    return call(
        functools.partial(combine_kernel, along),
        shape((local_rows, model_width), bf16),
        (residual, expert_choice.T, gate_weights.T, *collected),
        flops=2 * EXPERTS * ROWS * local_rows * model_width,
        moved=8 * local_rows * model_width,
    )


def solution(mesh):
    assert mesh.shape["dp"] == 2 and mesh.shape["expert"] % EXPERTS == 0
    in_specs = (
        P(("group", "expert", "dp"), None),
        P(("group", "expert", "dp"), None),
        P(("group", "expert", "dp"), None),
        P(),
        P("dp", None),
        P("dp", None),
        P("dp", None),
        P(),
        P(None, ("expert", "dp")),
        P(None, ("expert", "dp")),
        P(("expert", "dp"), None),
    )
    out_specs = P(("group", "expert", "dp"), None)

    return jax.shard_map(body, mesh=mesh, in_specs=in_specs, out_specs=out_specs, check_vma=False)
```

profile of v0, /device:TPU:1, one launch (start us, length us, event | category | flops | bytes accessed | tf_op | source)
XLA Modules:
  0.0 180.8 jit_solution(13408968785035083043)
XLA Ops:
  6.8 2.2 %copy-done = bf16[1024,2048]{1,0:T(8,128)(2,1)S(1)} copy-done((bf16[1024,2048]{1,0:T(8,128)(2,1)S(1)}, bf16[1024,2048]{1,0:T(8,128)(2,1)}, u32[]{:S(2)}) %copy-start) | copy-done | bytes 4194328
  10.9 2.5 %collective-permute-start.4 = (bf16[256,512]{1,0:T(8,128)(2,1)S(1)}, bf16[256,512]{1,0:T(8,128)(2,1)S(1)}, u32[]{:S(2)}, u32[]{:S(2)}) collective-permute-start(bf16[256,512]{1,0:T(8,128)(2,1)S(1)} %shard_map.113.refs_0_), channel_id=1, source_target_pairs={{0,4},{2,6},{4,8},{6,10},{8,12},{10,14},{12,0},{14,2},{1,5},{3,7},... | collective-permute-start | bytes 786440 | tf_op jit(solution)/shard_map/ppermute | solution.py:339
  13.4 8.3 %collective-permute-done.4.refs_2_ = bf16[256,512]{1,0:T(8,128)(2,1)S(1)} collective-permute-done((bf16[256,512]{1,0:T(8,128)(2,1)S(1)}, bf16[256,512]{1,0:T(8,128)(2,1)S(1)}, u32[]{:S(2)}, u32[]{:S(2)}) %collective-permute-start.4) | collective-permute-done | bytes 262176 | tf_op jit(solution)/shard_map/ppermute | solution.py:339
  21.7 8.7 %collective-permute-done.6.refs_4_ = bf16[256,512]{1,0:T(8,128)(2,1)S(1)} collective-permute-done((bf16[256,512]{1,0:T(8,128)(2,1)S(1)}, bf16[256,512]{1,0:T(8,128)(2,1)S(1)}, u32[]{:S(2)}, u32[]{:S(2)}) %collective-permute-start.6) | collective-permute-done | bytes 262176 | tf_op jit(solution)/shard_map/ppermute | solution.py:339
  32.8 5.5 %collective-permute-done.8.refs_6_ = bf16[256,512]{1,0:T(8,128)(2,1)S(1)} collective-permute-done((bf16[256,512]{1,0:T(8,128)(2,1)S(1)}, bf16[256,512]{1,0:T(8,128)(2,1)S(1)}, u32[]{:S(2)}, u32[]{:S(2)}) %collective-permute-start.8) | collective-permute-done | bytes 262176 | tf_op jit(solution)/shard_map/ppermute | solution.py:339
  39.4 2.7 %collective-permute-done.5.refs_3_ = bf16[256,512]{1,0:T(8,128)(2,1)S(1)} collective-permute-done((bf16[256,512]{1,0:T(8,128)(2,1)S(1)}, bf16[256,512]{1,0:T(8,128)(2,1)S(1)}, u32[]{:S(2)}, u32[]{:S(2)}) %collective-permute-start.5) | collective-permute-done | bytes 262176 | tf_op jit(solution)/shard_map/ppermute | solution.py:336
  42.1 5.6 %collective-permute-done.7.refs_5_ = bf16[256,512]{1,0:T(8,128)(2,1)S(1)} collective-permute-done((bf16[256,512]{1,0:T(8,128)(2,1)S(1)}, bf16[256,512]{1,0:T(8,128)(2,1)S(1)}, u32[]{:S(2)}, u32[]{:S(2)}) %collective-permute-start.7) | collective-permute-done | bytes 262176 | tf_op jit(solution)/shard_map/ppermute | solution.py:336
  47.8 5.6 %collective-permute-done.9.refs_7_ = bf16[256,512]{1,0:T(8,128)(2,1)S(1)} collective-permute-done((bf16[256,512]{1,0:T(8,128)(2,1)S(1)}, bf16[256,512]{1,0:T(8,128)(2,1)S(1)}, u32[]{:S(2)}, u32[]{:S(2)}) %collective-permute-start.9) | collective-permute-done | bytes 262176 | tf_op jit(solution)/shard_map/ppermute | solution.py:336
  53.4 9.9 %shard_map.114 = (bf16[128,2048]{1,0:T(8,128)(2,1)S(1)}, f32[128,2048]{1,0:T(8,128)S(1)}) custom-call(bf16[8,256,128]{2,1,0:T(8,128)(2,1)S(1)} %shard_map.111.query_ref, bf16[1024,2048]{1,0:T(8,128)(2,1)S(1)} %copy-done.8, bf16[256,512]{1,0:T(8,128)(2,1)S(1)} %shard_map.113.refs_0_, bf16[256,512]{1,0:T(8,128)(2,1)S(1)} %collective-permute-done.3.refs_1_, ...), custom_call_target="tpu_custom_call" | custom-call | flops 3221225472 | bytes 4194304 | tf_op jit(solution)/shard_map/pallas_call | solution.py:35
  63.2 2.7 %collective-permute-start.10 = (bf16[128,2048]{1,0:T(8,128)(2,1)S(1)}, bf16[128,2048]{1,0:T(8,128)(2,1)S(1)}, u32[]{:S(2)}, u32[]{:S(2)}) collective-permute-start(bf16[128,2048]{1,0:T(8,128)(2,1)S(1)} %get-tuple-element.41), channel_id=1, source_target_pairs={{0,1},{1,0},{2,3},{3,2},{4,5},{5,4},{6,7},{7,6},{8,9},{9,8},{10,11... | collective-permute-start | bytes 1572872 | tf_op jit(solution)/shard_map/ppermute | solution.py:333
  68.8 3.3 %collective-permute-start.33 = (bf16[72,2048]{1,0:T(8,128)(2,1)S(1)}, bf16[72,2048]{1,0:T(8,128)(2,1)S(1)}, u32[]{:S(2)}, u32[]{:S(2)}) collective-permute-start(bf16[72,2048]{1,0:T(8,128)(2,1)S(1)} %get-tuple-element.58), channel_id=1, source_target_pairs={{0,12},{2,14},{4,8},{6,10},{8,4},{10,6},{12,0},{14,2},{1,13},{3,15... | collective-permute-start | bytes 884744 | tf_op jit(solution)/shard_map/ppermute | solution.py:342
  74.8 4.2 %collective-permute-done.33.refs_0_ = bf16[72,2048]{1,0:T(8,128)(2,1)S(1)} collective-permute-done((bf16[72,2048]{1,0:T(8,128)(2,1)S(1)}, bf16[72,2048]{1,0:T(8,128)(2,1)S(1)}, u32[]{:S(2)}, u32[]{:S(2)}) %collective-permute-start.33) | collective-permute-done | bytes 294944 | tf_op jit(solution)/shard_map/ppermute | solution.py:342
  80.0 2.2 %collective-permute-start.13 = (bf16[72,2048]{1,0:T(8,128)(2,1)S(1)}, bf16[72,2048]{1,0:T(8,128)(2,1)S(1)}, u32[]{:S(2)}, u32[]{:S(2)}) collective-permute-start(bf16[72,2048]{1,0:T(8,128)(2,1)S(1)} %collective-permute-done.11.refs_1_), channel_id=1, source_target_pairs={{0,1},{1,0},{2,3},{3,2},{4,5},{5,4},{6,7},{7,6},{8,9},{9,8},{10,11... | collective-permute-start | bytes 884744 | tf_op jit(solution)/shard_map/ppermute | solution.py:333
  84.1 10.1 %collective-permute-done.25.refs_0_ = bf16[72,2048]{1,0:T(8,128)(2,1)S(1)} collective-permute-done((bf16[72,2048]{1,0:T(8,128)(2,1)S(1)}, bf16[72,2048]{1,0:T(8,128)(2,1)S(1)}, u32[]{:S(2)}, u32[]{:S(2)}) %collective-permute-start.25) | collective-permute-done | bytes 294944 | tf_op jit(solution)/shard_map/ppermute | solution.py:342
  97.7 6.6 %shard_map.116 = (bf16[72,2048]{1,0:T(8,128)(2,1)S(1)}, bf16[72,2048]{1,0:T(8,128)(2,1)S(1)}, bf16[72,2048]{1,0:T(8,128)(2,1)S(1)}, bf16[72,2048]{1,0:T(8,128)(2,1)S(1)}) custom-call(bf16[2048,1792]{1,0:T(8,128)(2,1)S(1)} %fetch.3.gate_ref, bf16[2048,1792]{1,0:T(8,128)(2,1)S(1)} %fetch.4.up_ref, bf16[1792,2048]{1,0:T(8,128)(2,1)S(1)} %fetch.5.down_ref, ...), custom_call_target="tpu_custom_call" | custom-call | flops 6341787648 | bytes 22020096 | tf_op jit(solution)/shard_map/pallas_call | solution.py:35
  105.3 6.6 %shard_map.119 = (bf16[72,2048]{1,0:T(8,128)(2,1)S(1)}, bf16[72,2048]{1,0:T(8,128)(2,1)S(1)}, bf16[72,2048]{1,0:T(8,128)(2,1)S(1)}, bf16[72,2048]{1,0:T(8,128)(2,1)S(1)}) custom-call(bf16[2048,1792]{1,0:T(8,128)(2,1)S(1)} %fetch.3.gate_ref, bf16[2048,1792]{1,0:T(8,128)(2,1)S(1)} %fetch.4.up_ref, bf16[1792,2048]{1,0:T(8,128)(2,1)S(1)} %fetch.5.down_ref, ...), custom_call_target="tpu_custom_call" | custom-call | flops 6341787648 | bytes 22020096 | tf_op jit(solution)/shard_map/pallas_call | solution.py:35
  113.0 6.8 %shard_map.118 = (bf16[72,2048]{1,0:T(8,128)(2,1)S(1)}, bf16[72,2048]{1,0:T(8,128)(2,1)S(1)}, bf16[72,2048]{1,0:T(8,128)(2,1)S(1)}, bf16[72,2048]{1,0:T(8,128)(2,1)S(1)}) custom-call(bf16[2048,1792]{1,0:T(8,128)(2,1)S(1)} %fetch.3.gate_ref, bf16[2048,1792]{1,0:T(8,128)(2,1)S(1)} %fetch.4.up_ref, bf16[1792,2048]{1,0:T(8,128)(2,1)S(1)} %fetch.5.down_ref, ...), custom_call_target="tpu_custom_call" | custom-call | flops 6341787648 | bytes 22020096 | tf_op jit(solution)/shard_map/pallas_call | solution.py:35
  120.5 6.6 %shard_map.117 = (bf16[72,2048]{1,0:T(8,128)(2,1)S(1)}, bf16[72,2048]{1,0:T(8,128)(2,1)S(1)}, bf16[72,2048]{1,0:T(8,128)(2,1)S(1)}, bf16[72,2048]{1,0:T(8,128)(2,1)S(1)}) custom-call(bf16[2048,1792]{1,0:T(8,128)(2,1)S(1)} %fetch.3.gate_ref, bf16[2048,1792]{1,0:T(8,128)(2,1)S(1)} %fetch.4.up_ref, bf16[1792,2048]{1,0:T(8,128)(2,1)S(1)} %fetch.5.down_ref, ...), custom_call_target="tpu_custom_call" | custom-call | flops 6341787648 | bytes 22020096 | tf_op jit(solution)/shard_map/pallas_call | solution.py:35
  130.8 6.7 %collective-permute-done.39 = bf16[72,2048]{1,0:T(8,128)(2,1)S(1)} collective-permute-done((bf16[72,2048]{1,0:T(8,128)(2,1)S(1)}, bf16[72,2048]{1,0:T(8,128)(2,1)S(1)}, u32[]{:S(2)}, u32[]{:S(2)}) %collective-permute-start.39) | collective-permute-done | bytes 294944 | tf_op jit(solution)/shard_map/ppermute | solution.py:336
  139.1 11.0 %collective-permute-done.31 = bf16[72,2048]{1,0:T(8,128)(2,1)S(1)} collective-permute-done((bf16[72,2048]{1,0:T(8,128)(2,1)S(1)}, bf16[72,2048]{1,0:T(8,128)(2,1)S(1)}, u32[]{:S(2)}, u32[]{:S(2)}) %collective-permute-start.31) | collective-permute-done | bytes 294944 | tf_op jit(solution)/shard_map/ppermute | solution.py:336
  150.1 2.2 %collective-permute-start.40 = (bf16[72,2048]{1,0:T(8,128)(2,1)S(1)}, bf16[72,2048]{1,0:T(8,128)(2,1)S(1)}, u32[]{:S(2)}, u32[]{:S(2)}) collective-permute-start(bf16[72,2048]{1,0:T(8,128)(2,1)S(1)} %add_convert_fusion), channel_id=1, source_target_pairs={{0,12},{2,14},{4,8},{6,10},{8,4},{10,6},{12,0},{14,2},{1,13},{3,15... | collective-permute-start | bytes 884744 | tf_op jit(solution)/shard_map/ppermute | solution.py:342
  153.0 3.5 %collective-permute-done.23 = bf16[72,2048]{1,0:T(8,128)(2,1)S(1)} collective-permute-done((bf16[72,2048]{1,0:T(8,128)(2,1)S(1)}, bf16[72,2048]{1,0:T(8,128)(2,1)S(1)}, u32[]{:S(2)}, u32[]{:S(2)}) %collective-permute-start.23) | collective-permute-done | bytes 294944 | tf_op jit(solution)/shard_map/ppermute | solution.py:336
  158.8 19.8 %collective-permute-done.32.refs_2_ = bf16[72,2048]{1,0:T(8,128)(2,1)S(1)} collective-permute-done((bf16[72,2048]{1,0:T(8,128)(2,1)S(1)}, bf16[72,2048]{1,0:T(8,128)(2,1)S(1)}, u32[]{:S(2)}, u32[]{:S(2)}) %collective-permute-start.32) | collective-permute-done | bytes 294944 | tf_op jit(solution)/shard_map/ppermute | solution.py:342
  178.6 2.2 %shard_map.120 = bf16[128,2048]{1,0:T(8,128)(2,1)} custom-call(bf16[128,2048]{1,0:T(8,128)(2,1)S(1)} %get-tuple-element.42.residual_ref, s32[2,128]{1,0:T(2,128)S(1)} %bitcast.13, f32[2,128]{1,0:T(2,128)S(1)} %bitcast.14, bf16[72,2048]{1,0:T(8,128)(2,1)S(1)} %add_convert_fusion.9.refs_0_, bf16[72,2048]{1,0:T(8,128)(2,1)S(1)} %collective-permute-done.24.refs_1_, ...), custom_call_target="tpu_custom_call" | custom-call | flops 150994944 | bytes 2097152 | tf_op jit(solution)/shard_map/pallas_call | solution.py:35
  (118 shorter events, 34.8 us)
Async XLA Ops:
  10.3 28.7 %collective-permute-start.1 = (f32[256,1024]{1,0:T(8,128)S(1)}, f32[256,1024]{1,0:T(8,128)S(1)}, u32[]{:S(2)}, u32[]{:S(2)}) collective-permute-start(f32[256,1024]{1,0:T(8,128)S(1)} %get-tuple-element.37), channel_id=1, source_target_pairs={{0,1},{1,0},{2,3},{3,2},{4,5},{5,4},{6,7},{7,6},{8,9},{9,8},{10,11... | collective-permute-start | bytes 3145736 | tf_op jit(solution)/shard_map/ppermute | solution.py:333
  10.9 10.8 %collective-permute-start.4 = (bf16[256,512]{1,0:T(8,128)(2,1)S(1)}, bf16[256,512]{1,0:T(8,128)(2,1)S(1)}, u32[]{:S(2)}, u32[]{:S(2)}) collective-permute-start(bf16[256,512]{1,0:T(8,128)(2,1)S(1)} %shard_map.113.refs_0_), channel_id=1, source_target_pairs={{0,4},{2,6},{4,8},{6,10},{8,12},{10,14},{12,0},{14,2},{1,5},{3,7},... | collective-permute-start | bytes 786440 | tf_op jit(solution)/shard_map/ppermute | solution.py:339
  31.3 10.8 %collective-permute-start.5 = (bf16[256,512]{1,0:T(8,128)(2,1)S(1)}, bf16[256,512]{1,0:T(8,128)(2,1)S(1)}, u32[]{:S(2)}, u32[]{:S(2)}) collective-permute-start(bf16[256,512]{1,0:T(8,128)(2,1)S(1)} %collective-permute-done.4.refs_2_), channel_id=1, source_target_pairs={{0,2},{2,0},{4,6},{6,4},{8,10},{10,8},{12,14},{14,12},{1,3},{3,1},... | collective-permute-start | bytes 786440 | tf_op jit(solution)/shard_map/ppermute | solution.py:336
  31.9 15.8 %collective-permute-start.7 = (bf16[256,512]{1,0:T(8,128)(2,1)S(1)}, bf16[256,512]{1,0:T(8,128)(2,1)S(1)}, u32[]{:S(2)}, u32[]{:S(2)}) collective-permute-start(bf16[256,512]{1,0:T(8,128)(2,1)S(1)} %collective-permute-done.6.refs_4_), channel_id=1, source_target_pairs={{0,2},{2,0},{4,6},{6,4},{8,10},{10,8},{12,14},{14,12},{1,3},{3,1},... | collective-permute-start | bytes 786440 | tf_op jit(solution)/shard_map/ppermute | solution.py:336
  38.3 15.1 %collective-permute-start.9 = (bf16[256,512]{1,0:T(8,128)(2,1)S(1)}, bf16[256,512]{1,0:T(8,128)(2,1)S(1)}, u32[]{:S(2)}, u32[]{:S(2)}) collective-permute-start(bf16[256,512]{1,0:T(8,128)(2,1)S(1)} %collective-permute-done.8.refs_6_), channel_id=1, source_target_pairs={{0,2},{2,0},{4,6},{6,4},{8,10},{10,8},{12,14},{14,12},{1,3},{3,1},... | collective-permute-start | bytes 786440 | tf_op jit(solution)/shard_map/ppermute | solution.py:336
  73.0 21.2 %collective-permute-start.25 = (bf16[72,2048]{1,0:T(8,128)(2,1)S(1)}, bf16[72,2048]{1,0:T(8,128)(2,1)S(1)}, u32[]{:S(2)}, u32[]{:S(2)}) collective-permute-start(bf16[72,2048]{1,0:T(8,128)(2,1)S(1)} %get-tuple-element.53), channel_id=1, source_target_pairs={{0,8},{2,10},{4,12},{6,14},{8,0},{10,2},{12,4},{14,6},{1,9},{3,11}... | collective-permute-start | bytes 884744 | tf_op jit(solution)/shard_map/ppermute | solution.py:342
  73.0 22.5 %collective-permute-start.17 = (bf16[72,2048]{1,0:T(8,128)(2,1)S(1)}, bf16[72,2048]{1,0:T(8,128)(2,1)S(1)}, u32[]{:S(2)}, u32[]{:S(2)}) collective-permute-start(bf16[72,2048]{1,0:T(8,128)(2,1)S(1)} %get-tuple-element.48), channel_id=1, source_target_pairs={{0,4},{2,6},{4,0},{6,2},{8,12},{10,14},{12,8},{14,10},{1,5},{3,7},... | collective-permute-start | bytes 884744 | tf_op jit(solution)/shard_map/ppermute | solution.py:342
  73.3 23.2 %collective-permute-start.12 = (bf16[72,2048]{1,0:T(8,128)(2,1)S(1)}, bf16[72,2048]{1,0:T(8,128)(2,1)S(1)}, u32[]{:S(2)}, u32[]{:S(2)}) collective-permute-start(bf16[72,2048]{1,0:T(8,128)(2,1)S(1)} %get-tuple-element.43.refs_0_), channel_id=1, source_target_pairs={{0,1},{1,0},{2,3},{3,2},{4,5},{5,4},{6,7},{7,6},{8,9},{9,8},{10,11... | collective-permute-start | bytes 884744 | tf_op jit(solution)/shard_map/ppermute | solution.py:333
  78.9 17.9 %collective-permute-start.34 = (bf16[72,2048]{1,0:T(8,128)(2,1)S(1)}, bf16[72,2048]{1,0:T(8,128)(2,1)S(1)}, u32[]{:S(2)}, u32[]{:S(2)}) collective-permute-start(bf16[72,2048]{1,0:T(8,128)(2,1)S(1)} %collective-permute-done.33.refs_0_), channel_id=1, source_target_pairs={{0,2},{2,0},{4,6},{6,4},{8,10},{10,8},{12,14},{14,12},{1,3},{3,1},... | collective-permute-start | bytes 884744 | tf_op jit(solution)/shard_map/ppermute | solution.py:336
  80.0 17.2 %collective-permute-start.13 = (bf16[72,2048]{1,0:T(8,128)(2,1)S(1)}, bf16[72,2048]{1,0:T(8,128)(2,1)S(1)}, u32[]{:S(2)}, u32[]{:S(2)}) collective-permute-start(bf16[72,2048]{1,0:T(8,128)(2,1)S(1)} %collective-permute-done.11.refs_1_), channel_id=1, source_target_pairs={{0,1},{1,0},{2,3},{3,2},{4,5},{5,4},{6,7},{7,6},{8,9},{9,8},{10,11... | collective-permute-start | bytes 884744 | tf_op jit(solution)/shard_map/ppermute | solution.py:333
  96.6 15.4 %collective-permute-start.27 = (bf16[72,2048]{1,0:T(8,128)(2,1)S(1)}, bf16[72,2048]{1,0:T(8,128)(2,1)S(1)}, u32[]{:S(2)}, u32[]{:S(2)}) collective-permute-start(bf16[72,2048]{1,0:T(8,128)(2,1)S(1)} %collective-permute-done.25.refs_0_), channel_id=1, source_target_pairs={{0,1},{1,0},{2,3},{3,2},{4,5},{5,4},{6,7},{7,6},{8,9},{9,8},{10,11... | collective-permute-start | bytes 884744 | tf_op jit(solution)/shard_map/ppermute | solution.py:333
  96.9 15.7 %collective-permute-start.18 = (bf16[72,2048]{1,0:T(8,128)(2,1)S(1)}, bf16[72,2048]{1,0:T(8,128)(2,1)S(1)}, u32[]{:S(2)}, u32[]{:S(2)}) collective-permute-start(bf16[72,2048]{1,0:T(8,128)(2,1)S(1)} %collective-permute-done.17.refs_0_), channel_id=1, source_target_pairs={{0,2},{2,0},{4,6},{6,4},{8,10},{10,8},{12,14},{14,12},{1,3},{3,1},... | collective-permute-start | bytes 884744 | tf_op jit(solution)/shard_map/ppermute | solution.py:336
  104.3 15.5 %collective-permute-start.19 = (bf16[72,2048]{1,0:T(8,128)(2,1)S(1)}, bf16[72,2048]{1,0:T(8,128)(2,1)S(1)}, u32[]{:S(2)}, u32[]{:S(2)}) collective-permute-start(bf16[72,2048]{1,0:T(8,128)(2,1)S(1)} %collective-permute-done.17.refs_0_), channel_id=1, source_target_pairs={{0,1},{1,0},{2,3},{3,2},{4,5},{5,4},{6,7},{7,6},{8,9},{9,8},{10,11... | collective-permute-start | bytes 884744 | tf_op jit(solution)/shard_map/ppermute | solution.py:333
  104.4 22.7 %collective-permute-start.15 = (bf16[72,2048]{1,0:T(8,128)(2,1)S(1)}, bf16[72,2048]{1,0:T(8,128)(2,1)S(1)}, u32[]{:S(2)}, u32[]{:S(2)}) collective-permute-start(bf16[72,2048]{1,0:T(8,128)(2,1)S(1)} %get-tuple-element.47), channel_id=1, source_target_pairs={{0,1},{1,0},{2,3},{3,2},{4,5},{5,4},{6,7},{7,6},{8,9},{9,8},{10,11... | collective-permute-start | bytes 884744 | tf_op jit(solution)/shard_map/ppermute | solution.py:333
  111.9 45.5 %collective-permute-start.14 = (bf16[72,2048]{1,0:T(8,128)(2,1)S(1)}, bf16[72,2048]{1,0:T(8,128)(2,1)S(1)}, u32[]{:S(2)}, u32[]{:S(2)}) collective-permute-start(bf16[72,2048]{1,0:T(8,128)(2,1)S(1)} %get-tuple-element.45), channel_id=1, source_target_pairs={{0,1},{1,0},{2,3},{3,2},{4,5},{5,4},{6,7},{7,6},{8,9},{9,8},{10,11... | collective-permute-start | bytes 884744 | tf_op jit(solution)/shard_map/ppermute | solution.py:333
  112.6 14.7 %collective-permute-start.38 = (bf16[72,2048]{1,0:T(8,128)(2,1)S(1)}, bf16[72,2048]{1,0:T(8,128)(2,1)S(1)}, u32[]{:S(2)}, u32[]{:S(2)}) collective-permute-start(bf16[72,2048]{1,0:T(8,128)(2,1)S(1)} %get-tuple-element.62), channel_id=1, source_target_pairs={{0,1},{1,0},{2,3},{3,2},{4,5},{5,4},{6,7},{7,6},{8,9},{9,8},{10,11... | collective-permute-start | bytes 884744 | tf_op jit(solution)/shard_map/ppermute | solution.py:333
  119.9 10.5 %collective-permute-start.37 = (bf16[72,2048]{1,0:T(8,128)(2,1)S(1)}, bf16[72,2048]{1,0:T(8,128)(2,1)S(1)}, u32[]{:S(2)}, u32[]{:S(2)}) collective-permute-start(bf16[72,2048]{1,0:T(8,128)(2,1)S(1)} %get-tuple-element.60), channel_id=1, source_target_pairs={{0,1},{1,0},{2,3},{3,2},{4,5},{5,4},{6,7},{7,6},{8,9},{9,8},{10,11... | collective-permute-start | bytes 884744 | tf_op jit(solution)/shard_map/ppermute | solution.py:333
  127.1 11.6 %collective-permute-start.29 = (bf16[72,2048]{1,0:T(8,128)(2,1)S(1)}, bf16[72,2048]{1,0:T(8,128)(2,1)S(1)}, u32[]{:S(2)}, u32[]{:S(2)}) collective-permute-start(bf16[72,2048]{1,0:T(8,128)(2,1)S(1)} %get-tuple-element.55), channel_id=1, source_target_pairs={{0,1},{1,0},{2,3},{3,2},{4,5},{5,4},{6,7},{7,6},{8,9},{9,8},{10,11... | collective-permute-start | bytes 884744 | tf_op jit(solution)/shard_map/ppermute | solution.py:333
  127.9 24.6 %collective-permute-start.21 = (bf16[72,2048]{1,0:T(8,128)(2,1)S(1)}, bf16[72,2048]{1,0:T(8,128)(2,1)S(1)}, u32[]{:S(2)}, u32[]{:S(2)}) collective-permute-start(bf16[72,2048]{1,0:T(8,128)(2,1)S(1)} %get-tuple-element.50), channel_id=1, source_target_pairs={{0,1},{1,0},{2,3},{3,2},{4,5},{5,4},{6,7},{7,6},{8,9},{9,8},{10,11... | collective-permute-start | bytes 884744 | tf_op jit(solution)/shard_map/ppermute | solution.py:333
  130.4 27.1 %collective-permute-start.16 = (bf16[72,2048]{1,0:T(8,128)(2,1)S(1)}, bf16[72,2048]{1,0:T(8,128)(2,1)S(1)}, u32[]{:S(2)}, u32[]{:S(2)}) collective-permute-start(bf16[72,2048]{1,0:T(8,128)(2,1)S(1)} %add_convert_fusion.10), channel_id=1, source_target_pairs={{0,2},{2,0},{4,6},{6,4},{8,10},{10,8},{12,14},{14,12},{1,3},{3,1},... | collective-permute-start | bytes 884744 | tf_op jit(solution)/shard_map/ppermute | solution.py:336
  137.5 12.6 %collective-permute-start.31 = (bf16[72,2048]{1,0:T(8,128)(2,1)S(1)}, bf16[72,2048]{1,0:T(8,128)(2,1)S(1)}, u32[]{:S(2)}, u32[]{:S(2)}) collective-permute-start(bf16[72,2048]{1,0:T(8,128)(2,1)S(1)} %add_convert_fusion.4), channel_id=1, source_target_pairs={{0,2},{2,0},{4,6},{6,4},{8,10},{10,8},{12,14},{14,12},{1,3},{3,1},... | collective-permute-start | bytes 884744 | tf_op jit(solution)/shard_map/ppermute | solution.py:336
  138.7 17.7 %collective-permute-start.23 = (bf16[72,2048]{1,0:T(8,128)(2,1)S(1)}, bf16[72,2048]{1,0:T(8,128)(2,1)S(1)}, u32[]{:S(2)}, u32[]{:S(2)}) collective-permute-start(bf16[72,2048]{1,0:T(8,128)(2,1)S(1)} %add_convert_fusion.7), channel_id=1, source_target_pairs={{0,2},{2,0},{4,6},{6,4},{8,10},{10,8},{12,14},{14,12},{1,3},{3,1},... | collective-permute-start | bytes 884744 | tf_op jit(solution)/shard_map/ppermute | solution.py:336
  152.5 26.1 %collective-permute-start.32 = (bf16[72,2048]{1,0:T(8,128)(2,1)S(1)}, bf16[72,2048]{1,0:T(8,128)(2,1)S(1)}, u32[]{:S(2)}, u32[]{:S(2)}) collective-permute-start(bf16[72,2048]{1,0:T(8,128)(2,1)S(1)} %add_convert_fusion.3), channel_id=1, source_target_pairs={{0,8},{2,10},{4,12},{6,14},{8,0},{10,2},{12,4},{14,6},{1,9},{3,11}... | collective-permute-start | bytes 884744 | tf_op jit(solution)/shard_map/ppermute | solution.py:342
  156.5 22.1 %collective-permute-start.24 = (bf16[72,2048]{1,0:T(8,128)(2,1)S(1)}, bf16[72,2048]{1,0:T(8,128)(2,1)S(1)}, u32[]{:S(2)}, u32[]{:S(2)}) collective-permute-start(bf16[72,2048]{1,0:T(8,128)(2,1)S(1)} %add_convert_fusion.6), channel_id=1, source_target_pairs={{0,4},{2,6},{4,0},{6,2},{8,12},{10,14},{12,8},{14,10},{1,5},{3,7},... | collective-permute-start | bytes 884744 | tf_op jit(solution)/shard_map/ppermute | solution.py:342
  (32 other events, 441.6 us)
where the time goes:
time: 182 us; the launch traced here: 181 us
  waiting for transfers between devices  97.4 us (54%)
  Pallas kernels  44.5 us (24%)
  starting transfers between devices  31.5 us (17%)
  local copies, waits for them, and re-layouts  5.56 us (3%)
    pallas_call x12, Pallas kernels, call(): pl.pallas_call(kernel, out_shape=outs, in_specs=[VMEM] * len(operands), o...  42.7 us
    ppermute x12, waiting for transfers between devices, beside(): return lax.ppermute(x, 'expert', [(i, i ^ turn) for i in range(chips)])  35.4 us
    ppermute x6, waiting for transfers between devices, planes(): lax.ppermute(x, 'expert', [(i, i ^ step * along) for i in range(chips)])  35.3 us
    ppermute x3, waiting for transfers between devices, upward(): lax.ppermute(x, 'expert', [(i, (i + along) % chips) for i in range(chips)])  22.6 us
    ppermute x20, starting transfers between devices, across(): return lax.ppermute(x, 'dp', [(i, i ^ 1) for i in range(cores)])  12.5 us
    ppermute x12, starting transfers between devices, beside(): return lax.ppermute(x, 'expert', [(i, i ^ turn) for i in range(chips)])  9.21 us
    ppermute x6, starting transfers between devices, planes(): lax.ppermute(x, 'expert', [(i, i ^ step * along) for i in range(chips)])  7.32 us
    unnamed x30, local copies, waits for them, and re-layouts  5.56 us
  transfers between devices with their start and end apart: 41, of which 17 were waited for; matrix products, arithmetic and copies ran while one was open for 1% of the time, Pallas kernels for 17%

commit v1 on v0

--- a/solution.py
+++ b/solution.py
@@ -16,7 +16,7 @@
 
 HIDDEN_STEP = 256
 DOWN_STEP = 256
-ORDER = (0, 1, 2, 3)
+ORDER = (0, 2, 1, 3)
 
 epsilon = 1e-05
 base_theta = 1000000.0
@@ -106,9 +106,14 @@
         out_ref[head] = turned(total, cosine_ref[...], sine_ref[...]).astype(bf16)
 
 
-def attention_kernel(places, along, query_ref, weight_ref, *refs):
-    keyval_refs = refs[: len(places)]
-    send_ref, keep_ref, score_ref, context_ref = refs[len(places) :]
+def attention_kernel(places, along, first, last, query_ref, *refs):
+    refs = list(refs)
+    keyval_refs = [refs.pop(0) for _ in places]
+    before = [] if first else [refs.pop(0) for _ in range(3)]
+    weight_ref = refs.pop(0) if last else None
+    after = [refs.pop(0) for _ in range(2 if last else 3)]
+    score_ref = refs.pop(0)
+    context_ref = refs.pop(0) if last else None
     heads, rows, _ = query_ref.shape
     half = rows // 2
     shared = keyval_refs[0].shape[1] // (2 * HEAD_DIM)
@@ -121,7 +126,8 @@
         row = lax.broadcasted_iota(jnp.int32, shape, axis)
         return jnp.where(core == 0, row, jnp.where(row < half, row + half, row - half))
 
-    own_visible = position((rows, rows), 1) <= position((rows, rows), 0)
+    if first:
+        own_visible = position((rows, rows), 1) <= position((rows, rows), 0)
     seen = []
     for back, turn in places:
         if back == 0:
@@ -145,39 +151,54 @@
                     (((1,), (1,)), ((), ())),
                     preferred_element_type=f32,
                 ) * factor
-                if index == 0:
+                own = first and index == 0
+                if own:
                     score = jnp.where(own_visible, score, masked_score)
                 score_ref[:, index * rows : (index + 1) * rows] = score
                 most = score[:, :HEAD_DIM]
                 for start in range(HEAD_DIM, rows, HEAD_DIM):
                     most = jnp.maximum(most, score[:, start : start + HEAD_DIM])
-                if index > 0:
+                if not own:
                     most = jnp.where(seen[index], most, masked_score)
                 highest = jnp.maximum(highest, most)
             highest = jnp.max(highest, axis=-1, keepdims=True)
-            totals = jnp.zeros((rows, HEAD_DIM), f32)
-            mixed = jnp.zeros((rows, HEAD_DIM), f32)
+            if first:
+                totals = jnp.zeros((rows, HEAD_DIM), f32)
+                mixed = jnp.zeros((rows, HEAD_DIM), f32)
+            else:
+                earlier = before[0][head][:, :1]
+                highest = jnp.maximum(highest, earlier)
+                shrink = jnp.exp2(earlier - highest)
+                totals = before[1][head] * shrink
+                mixed = before[2][head] * shrink
             for index, keyval_ref in enumerate(keyval_refs):
                 ceiling = highest
-                if index > 0:
+                if not (first and index == 0):
                     ceiling = jnp.where(seen[index], highest, -masked_score)
                 expo = jnp.exp2(score_ref[:, index * rows : (index + 1) * rows] - ceiling)
                 for start in range(0, rows, HEAD_DIM):
                     totals = totals + expo[:, start : start + HEAD_DIM]
                 mixed = mixed + dot(expo.astype(bf16), keyval_ref[:, value_columns])
-            total = jnp.sum(totals, axis=-1, keepdims=True)
-            context_ref[head] = (mixed / total).astype(bf16)
+            if last:
+                total = jnp.sum(totals, axis=-1, keepdims=True)
+                context_ref[head] = (mixed / total).astype(bf16)
+            else:
+                after[0][head] = jnp.broadcast_to(highest, (rows, HEAD_DIM))
+                after[1][head] = totals
+                after[2][head] = mixed
             return 0
 
         lax.fori_loop(0, sharing, one_head, 0)
 
-    context = jnp.concatenate([context_ref[head] for head in range(heads)], axis=1)
-    step = min(512, send_ref.shape[1])
-    for start in range(0, send_ref.shape[1], step):
-        columns = slice(start, start + step)
-        out = dot(context, weight_ref[:, columns])
-        keep_ref[:, columns] = out[:half]
-        send_ref[:, columns] = out[half:].astype(bf16)
+    if last:
+        send_ref, keep_ref = after
+        context = jnp.concatenate([context_ref[head] for head in range(heads)], axis=1)
+        step = min(512, send_ref.shape[1])
+        for start in range(0, send_ref.shape[1], step):
+            columns = slice(start, start + step)
+            out = dot(context, weight_ref[:, columns])
+            keep_ref[:, columns] = out[:half]
+            send_ref[:, columns] = out[half:].astype(bf16)
 
 
 def as_columns(rows_ref):
@@ -287,17 +308,18 @@
     )
 
 
-def combine_kernel(along, residual_ref, choice_ref, weight_ref, *refs):
+def combine_kernel(along, steps, base_ref, choice_ref, weight_ref, *refs):
     row_refs, out_ref = refs[:-1], refs[-1]
     plane = lax.axis_index("expert") // along
     choice = as_columns(choice_ref).astype(jnp.int32)
     weights = as_columns(weight_ref)
-    total = residual_ref[...].astype(f32)
-    for step, routing in enumerate(placed(choice, plane)):
+    total = base_ref[...].astype(f32)
+    routings = placed(choice, plane)
+    for step, row_ref in zip(steps, row_refs):
         expert = plane ^ step
         weight = jnp.sum(jnp.where(choice == expert, weights, 0.0), axis=1, keepdims=True)
-        total = total + weight * dot(routing, row_refs[step][...])
-    out_ref[...] = total.astype(bf16)
+        total = total + weight * dot(routings[step], row_ref[...])
+    out_ref[...] = total.astype(out_ref.dtype)
 
 
 def add(*terms):
@@ -362,6 +384,7 @@
         moved=4 * local_rows * model_width,
     )
     theirs = across(outgoing)
+    key_value_weight = fetched(key_value_weight)
     keyval_keep, keyval_send = call(
         keyval_kernel,
         [shape((pair_rows, keyval_width), f32)] * 2,
@@ -392,27 +415,37 @@
         flops=8 * pair_rows * query_width,
         moved=10 * pair_rows * query_width,
     )
-    blocks, places = [], []
+    parts, part = [], []
     line = keyval
     for back in range(EXPERTS):
         if back:
             line = upward(line)
-        for turn in range(along):
-            blocks.append(beside(line, turn) if turn else line)
-            places.append((back, turn))
-    attention_send, attention_keep = call(
-        functools.partial(attention_kernel, tuple(places), along),
-        [shape((local_rows, model_width), bf16), shape((local_rows, model_width), f32)],
-        (queries, output_weight, *blocks),
-        scratch=[
-            pltpu.VMEM((pair_rows, pair_rows * len(blocks)), f32),
-            pltpu.VMEM((heads, pair_rows, HEAD_DIM), bf16),
-        ],
-        flops=4 * pair_rows * pair_rows * len(blocks) * query_width
-        + 2 * pair_rows * query_width * model_width,
-        moved=2 * query_width * model_width,
-        limit=20 << 20,
-    )
+        part.append((line, (back, 0)))
+        if back:
+            parts.append(part)
+            part = []
+        part += [(beside(line, turn), (back, turn)) for turn in range(1, along)]
+    parts.append(part)
+    state = []
+    for index, part in enumerate(parts):
+        blocks, places = zip(*part) if part else ((), ())
+        last = index == len(parts) - 1
+        outs = [shape((heads, pair_rows, HEAD_DIM), f32)] * 3
+        scratch = [pltpu.VMEM((pair_rows, pair_rows * max(1, len(blocks))), f32)]
+        if last:
+            outs = [shape((local_rows, model_width), bf16), shape((local_rows, model_width), f32)]
+            scratch.append(pltpu.VMEM((heads, pair_rows, HEAD_DIM), bf16))
+        state = call(
+            functools.partial(attention_kernel, places, along, index == 0, last),
+            outs,
+            (queries, *blocks, *state, *([output_weight] if last else [])),
+            scratch=scratch,
+            flops=4 * pair_rows * pair_rows * len(blocks) * query_width
+            + 2 * pair_rows * query_width * model_width * last,
+            moved=8 * pair_rows * query_width,
+            limit=8 << 20,
+        )
+    attention_send, attention_keep = state
     attention_came = across(attention_send)
     residual, *packed = call(
         functools.partial(pack_kernel, along),
@@ -443,13 +476,19 @@
         others = [beside(near[turn], turn) for turn in range(1, along)]
         reduced = add(near[0], *others)
         collected[step] = planes(reduced, step) if step else reduced
-    return call(
-        functools.partial(combine_kernel, along),
-        shape((local_rows, model_width), bf16),
-        (residual, expert_choice.T, gate_weights.T, *collected),
-        flops=2 * EXPERTS * ROWS * local_rows * model_width,
-        moved=8 * local_rows * model_width,
-    )
+
+    def combined(base, steps, kind):
+        return call(
+            functools.partial(combine_kernel, along, steps),
+            shape((local_rows, model_width), kind),
+            (base, expert_choice.T, gate_weights.T, *[collected[step] for step in steps]),
+            flops=2 * len(steps) * ROWS * local_rows * model_width,
+            moved=8 * local_rows * model_width,
+        )
+
+    a, b, c, d = ORDER
+    early = combined(residual, (a, b), f32)
+    return combined(early, (c, d), bf16)
 
 
 def solution(mesh):

time: 182 us -> 178 us (0.978); the launches traced: 181 us -> 175 us
  waiting for transfers between devices: 97.4 us -> 78.5 us
  Pallas kernels: 44.5 us -> 55.3 us
  local copies, waits for them, and re-layouts: 5.56 us -> 7.74 us
    ppermute x12, waiting for transfers between devices: 35.4 us -> 21.7 us  [beside(): return lax.ppermute(x, 'expert', [(i, i ^ turn) for i in range(chips)])]
    pallas_call x12 -> x16, Pallas kernels: 42.7 us -> 53.3 us  [call(): pl.pallas_call(kernel, out_shape=outs, in_specs=[VMEM] * len(operands), o...]
    ppermute x6, waiting for transfers between devices: 35.3 us -> 30.5 us  [planes(): lax.ppermute(x, 'expert', [(i, i ^ step * along) for i in range(chips)])]
    unnamed x30, local copies, waits for them, and re-layouts: 5.56 us -> 7.74 us
  transfers between devices with their start and end apart: 41 -> 41, of which waited for: 17 -> 12; matrix products, arithmetic and copies ran while one was open for 1% -> 1% of each run, Pallas kernels for 17% -> 26%
where the time goes in v1:
time: 178 us; the launch traced here: 175 us
  waiting for transfers between devices  78.5 us (44%)
  Pallas kernels  55.3 us (31%)
  starting transfers between devices  31.3 us (18%)
  local copies, waits for them, and re-layouts  7.74 us (4%)
    pallas_call x16, Pallas kernels, call(): pl.pallas_call(kernel, out_shape=outs, in_specs=[VMEM] * len(operands), o...  53.3 us
    ppermute x6, waiting for transfers between devices, planes(): lax.ppermute(x, 'expert', [(i, i ^ step * along) for i in range(chips)])  30.5 us
    ppermute x3, waiting for transfers between devices, upward(): lax.ppermute(x, 'expert', [(i, (i + along) % chips) for i in range(chips)])  23.7 us
    ppermute x12, waiting for transfers between devices, beside(): return lax.ppermute(x, 'expert', [(i, i ^ turn) for i in range(chips)])  21.7 us
    ppermute x20, starting transfers between devices, across(): return lax.ppermute(x, 'dp', [(i, i ^ 1) for i in range(cores)])  12.9 us
    ppermute x12, starting transfers between devices, beside(): return lax.ppermute(x, 'expert', [(i, i ^ turn) for i in range(chips)])  9.36 us
    unnamed x30, local copies, waits for them, and re-layouts  7.74 us
    ppermute x6, starting transfers between devices, planes(): lax.ppermute(x, 'expert', [(i, i ^ step * along) for i in range(chips)])  6.27 us
  transfers between devices with their start and end apart: 41, of which 12 were waited for; matrix products, arithmetic and copies ran while one was open for 1% of the time, Pallas kernels for 26%

profile of v1, /device:TPU:1, one launch (start us, length us, event | category | flops | bytes accessed | tf_op | source)
XLA Modules:
  0.0 174.8 jit_solution(770102478824763872)
XLA Ops:
  5.2 2.2 %copy-done = bf16[1024,2048]{1,0:T(8,128)(2,1)S(1)} copy-done((bf16[1024,2048]{1,0:T(8,128)(2,1)S(1)}, bf16[1024,2048]{1,0:T(8,128)(2,1)}, u32[]{:S(2)}) %copy-start) | copy-done | bytes 4194328
  9.7 2.8 %collective-permute-start.3 = (bf16[256,512]{1,0:T(8,128)(2,1)S(1)}, bf16[256,512]{1,0:T(8,128)(2,1)S(1)}, u32[]{:S(2)}, u32[]{:S(2)}) collective-permute-start(bf16[256,512]{1,0:T(8,128)(2,1)S(1)} %shard_map.113.refs_0_), channel_id=1, source_target_pairs={{0,4},{2,6},{4,8},{6,10},{8,12},{10,14},{12,0},{14,2},{1,5},{3,7},... | collective-permute-start | bytes 786440 | tf_op jit(solution)/shard_map/ppermute | solution.py:361
  12.5 8.7 %collective-permute-done.3.refs_2_ = bf16[256,512]{1,0:T(8,128)(2,1)S(1)} collective-permute-done((bf16[256,512]{1,0:T(8,128)(2,1)S(1)}, bf16[256,512]{1,0:T(8,128)(2,1)S(1)}, u32[]{:S(2)}, u32[]{:S(2)}) %collective-permute-start.3) | collective-permute-done | bytes 262176 | tf_op jit(solution)/shard_map/ppermute | solution.py:361
  21.2 9.1 %collective-permute-done.4.refs_1_ = bf16[256,512]{1,0:T(8,128)(2,1)S(1)} collective-permute-done((bf16[256,512]{1,0:T(8,128)(2,1)S(1)}, bf16[256,512]{1,0:T(8,128)(2,1)S(1)}, u32[]{:S(2)}, u32[]{:S(2)}) %collective-permute-start.4) | collective-permute-done | bytes 262176 | tf_op jit(solution)/shard_map/ppermute | solution.py:361
  32.5 6.0 %collective-permute-done.5.refs_1_ = bf16[256,512]{1,0:T(8,128)(2,1)S(1)} collective-permute-done((bf16[256,512]{1,0:T(8,128)(2,1)S(1)}, bf16[256,512]{1,0:T(8,128)(2,1)S(1)}, u32[]{:S(2)}, u32[]{:S(2)}) %collective-permute-start.5) | collective-permute-done | bytes 262176 | tf_op jit(solution)/shard_map/ppermute | solution.py:361
  39.4 5.0 %shard_map.114 = (f32[8,256,128]{2,1,0:T(8,128)S(1)}, f32[8,256,128]{2,1,0:T(8,128)S(1)}, f32[8,256,128]{2,1,0:T(8,128)S(1)}) custom-call(bf16[8,256,128]{2,1,0:T(8,128)(2,1)S(1)} %shard_map.111.query_ref, bf16[256,512]{1,0:T(8,128)(2,1)S(1)} %shard_map.113.refs_0_, bf16[256,512]{1,0:T(8,128)(2,1)S(1)} %collective-permute-done.9.refs_1_, ...), custom_call_target="tpu_custom_call" | custom-call | flops 805306368 | bytes 2097152 | tf_op jit(solution)/shard_map/pallas_call | solution.py:35
  44.5 4.5 %shard_map.115 = (f32[8,256,128]{2,1,0:T(8,128)S(1)}, f32[8,256,128]{2,1,0:T(8,128)S(1)}, f32[8,256,128]{2,1,0:T(8,128)S(1)}) custom-call(bf16[8,256,128]{2,1,0:T(8,128)(2,1)S(1)} %shard_map.111.query_ref, bf16[256,512]{1,0:T(8,128)(2,1)S(1)} %collective-permute-done.8.refs_0_, bf16[256,512]{1,0:T(8,128)(2,1)S(1)} %collective-permute-done.4.refs_1_, ...), custom_call_target="tpu_custom_call" | custom-call | flops 536870912 | bytes 2097152 | tf_op jit(solution)/shard_map/pallas_call | solution.py:35
  49.0 4.5 %shard_map.116 = (f32[8,256,128]{2,1,0:T(8,128)S(1)}, f32[8,256,128]{2,1,0:T(8,128)S(1)}, f32[8,256,128]{2,1,0:T(8,128)S(1)}) custom-call(bf16[8,256,128]{2,1,0:T(8,128)(2,1)S(1)} %shard_map.111.query_ref, bf16[256,512]{1,0:T(8,128)(2,1)S(1)} %collective-permute-done.7.refs_0_, bf16[256,512]{1,0:T(8,128)(2,1)S(1)} %collective-permute-done.5.refs_1_, ...), custom_call_target="tpu_custom_call" | custom-call | flops 536870912 | bytes 2097152 | tf_op jit(solution)/shard_map/pallas_call | solution.py:35
  53.6 5.7 %shard_map.117 = (bf16[128,2048]{1,0:T(8,128)(2,1)S(1)}, f32[128,2048]{1,0:T(8,128)S(1)}) custom-call(bf16[8,256,128]{2,1,0:T(8,128)(2,1)S(1)} %shard_map.111.query_ref, bf16[256,512]{1,0:T(8,128)(2,1)S(1)} %collective-permute-done.6.refs_0_, f32[8,256,128]{2,1,0:T(8,128)S(1)} %get-tuple-element.55.refs_1_, f32[8,256,128]{2,1,0:T(8,128)S(1)} %get-tuple-element.56.refs_2_, ...), custom_call_target="tpu_custom_call" | custom-call | flops 1342177280 | bytes 2097152 | tf_op jit(solution)/shard_map/pallas_call | solution.py:35
  59.3 3.2 %collective-permute-start.10 = (bf16[128,2048]{1,0:T(8,128)(2,1)S(1)}, bf16[128,2048]{1,0:T(8,128)(2,1)S(1)}, u32[]{:S(2)}, u32[]{:S(2)}) collective-permute-start(bf16[128,2048]{1,0:T(8,128)(2,1)S(1)} %get-tuple-element.59), channel_id=1, source_target_pairs={{0,1},{1,0},{2,3},{3,2},{4,5},{5,4},{6,7},{7,6},{8,9},{9,8},{10,11... | collective-permute-start | bytes 1572872 | tf_op jit(solution)/shard_map/ppermute | solution.py:355
  65.3 3.6 %collective-permute-start.33 = (bf16[72,2048]{1,0:T(8,128)(2,1)S(1)}, bf16[72,2048]{1,0:T(8,128)(2,1)S(1)}, u32[]{:S(2)}, u32[]{:S(2)}) collective-permute-start(bf16[72,2048]{1,0:T(8,128)(2,1)S(1)} %get-tuple-element.76), channel_id=1, source_target_pairs={{0,12},{2,14},{4,8},{6,10},{8,4},{10,6},{12,0},{14,2},{1,13},{3,15... | collective-permute-start | bytes 884744 | tf_op jit(solution)/shard_map/ppermute | solution.py:364
  71.5 4.5 %collective-permute-done.33.refs_0_ = bf16[72,2048]{1,0:T(8,128)(2,1)S(1)} collective-permute-done((bf16[72,2048]{1,0:T(8,128)(2,1)S(1)}, bf16[72,2048]{1,0:T(8,128)(2,1)S(1)}, u32[]{:S(2)}, u32[]{:S(2)}) %collective-permute-start.33) | collective-permute-done | bytes 294944 | tf_op jit(solution)/shard_map/ppermute | solution.py:364
  82.8 3.5 %collective-permute-done.25.refs_0_ = bf16[72,2048]{1,0:T(8,128)(2,1)S(1)} collective-permute-done((bf16[72,2048]{1,0:T(8,128)(2,1)S(1)}, bf16[72,2048]{1,0:T(8,128)(2,1)S(1)}, u32[]{:S(2)}, u32[]{:S(2)}) %collective-permute-start.25) | collective-permute-done | bytes 294944 | tf_op jit(solution)/shard_map/ppermute | solution.py:364
  86.9 4.3 %collective-permute-done.17.refs_0_ = bf16[72,2048]{1,0:T(8,128)(2,1)S(1)} collective-permute-done((bf16[72,2048]{1,0:T(8,128)(2,1)S(1)}, bf16[72,2048]{1,0:T(8,128)(2,1)S(1)}, u32[]{:S(2)}, u32[]{:S(2)}) %collective-permute-start.17) | collective-permute-done | bytes 294944 | tf_op jit(solution)/shard_map/ppermute | solution.py:364
  94.5 6.6 %shard_map.119 = (bf16[72,2048]{1,0:T(8,128)(2,1)S(1)}, bf16[72,2048]{1,0:T(8,128)(2,1)S(1)}, bf16[72,2048]{1,0:T(8,128)(2,1)S(1)}, bf16[72,2048]{1,0:T(8,128)(2,1)S(1)}) custom-call(bf16[2048,1792]{1,0:T(8,128)(2,1)S(1)} %fetch.5.gate_ref, bf16[2048,1792]{1,0:T(8,128)(2,1)S(1)} %fetch.6.up_ref, bf16[1792,2048]{1,0:T(8,128)(2,1)S(1)} %fetch.7.down_ref, ...), custom_call_target="tpu_custom_call" | custom-call | flops 6341787648 | bytes 22020096 | tf_op jit(solution)/shard_map/pallas_call | solution.py:35
  102.3 6.6 %shard_map.123 = (bf16[72,2048]{1,0:T(8,128)(2,1)S(1)}, bf16[72,2048]{1,0:T(8,128)(2,1)S(1)}, bf16[72,2048]{1,0:T(8,128)(2,1)S(1)}, bf16[72,2048]{1,0:T(8,128)(2,1)S(1)}) custom-call(bf16[2048,1792]{1,0:T(8,128)(2,1)S(1)} %fetch.5.gate_ref, bf16[2048,1792]{1,0:T(8,128)(2,1)S(1)} %fetch.6.up_ref, bf16[1792,2048]{1,0:T(8,128)(2,1)S(1)} %fetch.7.down_ref, ...), custom_call_target="tpu_custom_call" | custom-call | flops 6341787648 | bytes 22020096 | tf_op jit(solution)/shard_map/pallas_call | solution.py:35
  110.0 6.8 %shard_map.122 = (bf16[72,2048]{1,0:T(8,128)(2,1)S(1)}, bf16[72,2048]{1,0:T(8,128)(2,1)S(1)}, bf16[72,2048]{1,0:T(8,128)(2,1)S(1)}, bf16[72,2048]{1,0:T(8,128)(2,1)S(1)}) custom-call(bf16[2048,1792]{1,0:T(8,128)(2,1)S(1)} %fetch.5.gate_ref, bf16[2048,1792]{1,0:T(8,128)(2,1)S(1)} %fetch.6.up_ref, bf16[1792,2048]{1,0:T(8,128)(2,1)S(1)} %fetch.7.down_ref, ...), custom_call_target="tpu_custom_call" | custom-call | flops 6341787648 | bytes 22020096 | tf_op jit(solution)/shard_map/pallas_call | solution.py:35
  117.4 6.6 %shard_map.120 = (bf16[72,2048]{1,0:T(8,128)(2,1)S(1)}, bf16[72,2048]{1,0:T(8,128)(2,1)S(1)}, bf16[72,2048]{1,0:T(8,128)(2,1)S(1)}, bf16[72,2048]{1,0:T(8,128)(2,1)S(1)}) custom-call(bf16[2048,1792]{1,0:T(8,128)(2,1)S(1)} %fetch.5.gate_ref, bf16[2048,1792]{1,0:T(8,128)(2,1)S(1)} %fetch.6.up_ref, bf16[1792,2048]{1,0:T(8,128)(2,1)S(1)} %fetch.7.down_ref, ...), custom_call_target="tpu_custom_call" | custom-call | flops 6341787648 | bytes 22020096 | tf_op jit(solution)/shard_map/pallas_call | solution.py:35
  127.7 6.7 %collective-permute-done.39 = bf16[72,2048]{1,0:T(8,128)(2,1)S(1)} collective-permute-done((bf16[72,2048]{1,0:T(8,128)(2,1)S(1)}, bf16[72,2048]{1,0:T(8,128)(2,1)S(1)}, u32[]{:S(2)}, u32[]{:S(2)}) %collective-permute-start.39) | collective-permute-done | bytes 294944 | tf_op jit(solution)/shard_map/ppermute | solution.py:358
  136.1 11.0 %collective-permute-done.31 = bf16[72,2048]{1,0:T(8,128)(2,1)S(1)} collective-permute-done((bf16[72,2048]{1,0:T(8,128)(2,1)S(1)}, bf16[72,2048]{1,0:T(8,128)(2,1)S(1)}, u32[]{:S(2)}, u32[]{:S(2)}) %collective-permute-start.31) | collective-permute-done | bytes 294944 | tf_op jit(solution)/shard_map/ppermute | solution.py:358
  147.0 2.2 %collective-permute-start.40 = (bf16[72,2048]{1,0:T(8,128)(2,1)S(1)}, bf16[72,2048]{1,0:T(8,128)(2,1)S(1)}, u32[]{:S(2)}, u32[]{:S(2)}) collective-permute-start(bf16[72,2048]{1,0:T(8,128)(2,1)S(1)} %add_convert_fusion), channel_id=1, source_target_pairs={{0,12},{2,14},{4,8},{6,10},{8,4},{10,6},{12,0},{14,2},{1,13},{3,15... | collective-permute-start | bytes 884744 | tf_op jit(solution)/shard_map/ppermute | solution.py:364
  149.4 4.0 %collective-permute-done.23 = bf16[72,2048]{1,0:T(8,128)(2,1)S(1)} collective-permute-done((bf16[72,2048]{1,0:T(8,128)(2,1)S(1)}, bf16[72,2048]{1,0:T(8,128)(2,1)S(1)}, u32[]{:S(2)}, u32[]{:S(2)}) %collective-permute-start.23) | collective-permute-done | bytes 294944 | tf_op jit(solution)/shard_map/ppermute | solution.py:358
  153.7 18.1 %collective-permute-done.24.refs_1_ = bf16[72,2048]{1,0:T(8,128)(2,1)S(1)} collective-permute-done((bf16[72,2048]{1,0:T(8,128)(2,1)S(1)}, bf16[72,2048]{1,0:T(8,128)(2,1)S(1)}, u32[]{:S(2)}, u32[]{:S(2)}) %collective-permute-start.24) | collective-permute-done | bytes 294944 | tf_op jit(solution)/shard_map/ppermute | solution.py:364
  172.9 1.9 %shard_map.124 = bf16[128,2048]{1,0:T(8,128)(2,1)} custom-call(f32[128,2048]{1,0:T(8,128)S(1)} %shard_map.121.base_ref, s32[2,128]{1,0:T(2,128)S(1)} %bitcast.12, f32[2,128]{1,0:T(2,128)S(1)} %bitcast.16, bf16[72,2048]{1,0:T(8,128)(2,1)S(1)} %collective-permute-done.32.refs_0_, bf16[72,2048]{1,0:T(8,128)(2,1)S(1)} %collective-permute-done.40.refs_1_), custom_call_target="tpu_custom_call" | custom-call | flops 75497472 | bytes 2097152 | tf_op jit(solution)/shard_map/pallas_call | solution.py:35
  (123 shorter events, 36.3 us)
Async XLA Ops:
  8.7 30.3 %collective-permute-start.1 = (f32[256,1024]{1,0:T(8,128)S(1)}, f32[256,1024]{1,0:T(8,128)S(1)}, u32[]{:S(2)}, u32[]{:S(2)}) collective-permute-start(f32[256,1024]{1,0:T(8,128)S(1)} %get-tuple-element.46), channel_id=1, source_target_pairs={{0,1},{1,0},{2,3},{3,2},{4,5},{5,4},{6,7},{7,6},{8,9},{9,8},{10,11... | collective-permute-start | bytes 3145736 | tf_op jit(solution)/shard_map/ppermute | solution.py:355
  31.0 13.4 %collective-permute-start.8 = (bf16[256,512]{1,0:T(8,128)(2,1)S(1)}, bf16[256,512]{1,0:T(8,128)(2,1)S(1)}, u32[]{:S(2)}, u32[]{:S(2)}) collective-permute-start(bf16[256,512]{1,0:T(8,128)(2,1)S(1)} %collective-permute-done.3.refs_2_), channel_id=1, source_target_pairs={{0,2},{2,0},{4,6},{6,4},{8,10},{10,8},{12,14},{14,12},{1,3},{3,1},... | collective-permute-start | bytes 786440 | tf_op jit(solution)/shard_map/ppermute | solution.py:358
  31.7 17.3 %collective-permute-start.7 = (bf16[256,512]{1,0:T(8,128)(2,1)S(1)}, bf16[256,512]{1,0:T(8,128)(2,1)S(1)}, u32[]{:S(2)}, u32[]{:S(2)}) collective-permute-start(bf16[256,512]{1,0:T(8,128)(2,1)S(1)} %collective-permute-done.4.refs_1_), channel_id=1, source_target_pairs={{0,2},{2,0},{4,6},{6,4},{8,10},{10,8},{12,14},{14,12},{1,3},{3,1},... | collective-permute-start | bytes 786440 | tf_op jit(solution)/shard_map/ppermute | solution.py:358
  38.5 15.1 %collective-permute-start.6 = (bf16[256,512]{1,0:T(8,128)(2,1)S(1)}, bf16[256,512]{1,0:T(8,128)(2,1)S(1)}, u32[]{:S(2)}, u32[]{:S(2)}) collective-permute-start(bf16[256,512]{1,0:T(8,128)(2,1)S(1)} %collective-permute-done.5.refs_1_), channel_id=1, source_target_pairs={{0,2},{2,0},{4,6},{6,4},{8,10},{10,8},{12,14},{14,12},{1,3},{3,1},... | collective-permute-start | bytes 786440 | tf_op jit(solution)/shard_map/ppermute | solution.py:358
  69.9 16.5 %collective-permute-start.25 = (bf16[72,2048]{1,0:T(8,128)(2,1)S(1)}, bf16[72,2048]{1,0:T(8,128)(2,1)S(1)}, u32[]{:S(2)}, u32[]{:S(2)}) collective-permute-start(bf16[72,2048]{1,0:T(8,128)(2,1)S(1)} %get-tuple-element.71), channel_id=1, source_target_pairs={{0,4},{2,6},{4,0},{6,2},{8,12},{10,14},{12,8},{14,10},{1,5},{3,7},... | collective-permute-start | bytes 884744 | tf_op jit(solution)/shard_map/ppermute | solution.py:364
  69.9 21.3 %collective-permute-start.17 = (bf16[72,2048]{1,0:T(8,128)(2,1)S(1)}, bf16[72,2048]{1,0:T(8,128)(2,1)S(1)}, u32[]{:S(2)}, u32[]{:S(2)}) collective-permute-start(bf16[72,2048]{1,0:T(8,128)(2,1)S(1)} %get-tuple-element.66), channel_id=1, source_target_pairs={{0,8},{2,10},{4,12},{6,14},{8,0},{10,2},{12,4},{14,6},{1,9},{3,11}... | collective-permute-start | bytes 884744 | tf_op jit(solution)/shard_map/ppermute | solution.py:364
  70.3 22.2 %collective-permute-start.12 = (bf16[72,2048]{1,0:T(8,128)(2,1)S(1)}, bf16[72,2048]{1,0:T(8,128)(2,1)S(1)}, u32[]{:S(2)}, u32[]{:S(2)}) collective-permute-start(bf16[72,2048]{1,0:T(8,128)(2,1)S(1)} %get-tuple-element.61.refs_0_), channel_id=1, source_target_pairs={{0,1},{1,0},{2,3},{3,2},{4,5},{5,4},{6,7},{7,6},{8,9},{9,8},{10,11... | collective-permute-start | bytes 884744 | tf_op jit(solution)/shard_map/ppermute | solution.py:355
  76.0 18.0 %collective-permute-start.34 = (bf16[72,2048]{1,0:T(8,128)(2,1)S(1)}, bf16[72,2048]{1,0:T(8,128)(2,1)S(1)}, u32[]{:S(2)}, u32[]{:S(2)}) collective-permute-start(bf16[72,2048]{1,0:T(8,128)(2,1)S(1)} %collective-permute-done.33.refs_0_), channel_id=1, source_target_pairs={{0,2},{2,0},{4,6},{6,4},{8,10},{10,8},{12,14},{14,12},{1,3},{3,1},... | collective-permute-start | bytes 884744 | tf_op jit(solution)/shard_map/ppermute | solution.py:358
  77.0 17.2 %collective-permute-start.13 = (bf16[72,2048]{1,0:T(8,128)(2,1)S(1)}, bf16[72,2048]{1,0:T(8,128)(2,1)S(1)}, u32[]{:S(2)}, u32[]{:S(2)}) collective-permute-start(bf16[72,2048]{1,0:T(8,128)(2,1)S(1)} %collective-permute-done.11.refs_1_), channel_id=1, source_target_pairs={{0,1},{1,0},{2,3},{3,2},{4,5},{5,4},{6,7},{7,6},{8,9},{9,8},{10,11... | collective-permute-start | bytes 884744 | tf_op jit(solution)/shard_map/ppermute | solution.py:355
  86.4 14.8 %collective-permute-start.35 = (bf16[72,2048]{1,0:T(8,128)(2,1)S(1)}, bf16[72,2048]{1,0:T(8,128)(2,1)S(1)}, u32[]{:S(2)}, u32[]{:S(2)}) collective-permute-start(bf16[72,2048]{1,0:T(8,128)(2,1)S(1)} %collective-permute-done.33.refs_0_), channel_id=1, source_target_pairs={{0,1},{1,0},{2,3},{3,2},{4,5},{5,4},{6,7},{7,6},{8,9},{9,8},{10,11... | collective-permute-start | bytes 884744 | tf_op jit(solution)/shard_map/ppermute | solution.py:355
  92.4 16.5 %collective-permute-start.27 = (bf16[72,2048]{1,0:T(8,128)(2,1)S(1)}, bf16[72,2048]{1,0:T(8,128)(2,1)S(1)}, u32[]{:S(2)}, u32[]{:S(2)}) collective-permute-start(bf16[72,2048]{1,0:T(8,128)(2,1)S(1)} %collective-permute-done.25.refs_0_), channel_id=1, source_target_pairs={{0,1},{1,0},{2,3},{3,2},{4,5},{5,4},{6,7},{7,6},{8,9},{9,8},{10,11... | collective-permute-start | bytes 884744 | tf_op jit(solution)/shard_map/ppermute | solution.py:355
  94.0 15.5 %collective-permute-start.18 = (bf16[72,2048]{1,0:T(8,128)(2,1)S(1)}, bf16[72,2048]{1,0:T(8,128)(2,1)S(1)}, u32[]{:S(2)}, u32[]{:S(2)}) collective-permute-start(bf16[72,2048]{1,0:T(8,128)(2,1)S(1)} %collective-permute-done.17.refs_0_), channel_id=1, source_target_pairs={{0,2},{2,0},{4,6},{6,4},{8,10},{10,8},{12,14},{14,12},{1,3},{3,1},... | collective-permute-start | bytes 884744 | tf_op jit(solution)/shard_map/ppermute | solution.py:358
  101.1 15.7 %collective-permute-start.19 = (bf16[72,2048]{1,0:T(8,128)(2,1)S(1)}, bf16[72,2048]{1,0:T(8,128)(2,1)S(1)}, u32[]{:S(2)}, u32[]{:S(2)}) collective-permute-start(bf16[72,2048]{1,0:T(8,128)(2,1)S(1)} %collective-permute-done.17.refs_0_), channel_id=1, source_target_pairs={{0,1},{1,0},{2,3},{3,2},{4,5},{5,4},{6,7},{7,6},{8,9},{9,8},{10,11... | collective-permute-start | bytes 884744 | tf_op jit(solution)/shard_map/ppermute | solution.py:355
  101.4 22.6 %collective-permute-start.15 = (bf16[72,2048]{1,0:T(8,128)(2,1)S(1)}, bf16[72,2048]{1,0:T(8,128)(2,1)S(1)}, u32[]{:S(2)}, u32[]{:S(2)}) collective-permute-start(bf16[72,2048]{1,0:T(8,128)(2,1)S(1)} %get-tuple-element.65), channel_id=1, source_target_pairs={{0,1},{1,0},{2,3},{3,2},{4,5},{5,4},{6,7},{7,6},{8,9},{9,8},{10,11... | collective-permute-start | bytes 884744 | tf_op jit(solution)/shard_map/ppermute | solution.py:355
  108.9 44.7 %collective-permute-start.14 = (bf16[72,2048]{1,0:T(8,128)(2,1)S(1)}, bf16[72,2048]{1,0:T(8,128)(2,1)S(1)}, u32[]{:S(2)}, u32[]{:S(2)}) collective-permute-start(bf16[72,2048]{1,0:T(8,128)(2,1)S(1)} %get-tuple-element.63), channel_id=1, source_target_pairs={{0,1},{1,0},{2,3},{3,2},{4,5},{5,4},{6,7},{7,6},{8,9},{9,8},{10,11... | collective-permute-start | bytes 884744 | tf_op jit(solution)/shard_map/ppermute | solution.py:355
  109.6 14.7 %collective-permute-start.38 = (bf16[72,2048]{1,0:T(8,128)(2,1)S(1)}, bf16[72,2048]{1,0:T(8,128)(2,1)S(1)}, u32[]{:S(2)}, u32[]{:S(2)}) collective-permute-start(bf16[72,2048]{1,0:T(8,128)(2,1)S(1)} %get-tuple-element.80), channel_id=1, source_target_pairs={{0,1},{1,0},{2,3},{3,2},{4,5},{5,4},{6,7},{7,6},{8,9},{9,8},{10,11... | collective-permute-start | bytes 884744 | tf_op jit(solution)/shard_map/ppermute | solution.py:355
  124.0 11.8 %collective-permute-start.29 = (bf16[72,2048]{1,0:T(8,128)(2,1)S(1)}, bf16[72,2048]{1,0:T(8,128)(2,1)S(1)}, u32[]{:S(2)}, u32[]{:S(2)}) collective-permute-start(bf16[72,2048]{1,0:T(8,128)(2,1)S(1)} %get-tuple-element.73), channel_id=1, source_target_pairs={{0,1},{1,0},{2,3},{3,2},{4,5},{5,4},{6,7},{7,6},{8,9},{9,8},{10,11... | collective-permute-start | bytes 884744 | tf_op jit(solution)/shard_map/ppermute | solution.py:355
  124.8 24.5 %collective-permute-start.21 = (bf16[72,2048]{1,0:T(8,128)(2,1)S(1)}, bf16[72,2048]{1,0:T(8,128)(2,1)S(1)}, u32[]{:S(2)}, u32[]{:S(2)}) collective-permute-start(bf16[72,2048]{1,0:T(8,128)(2,1)S(1)} %get-tuple-element.68), channel_id=1, source_target_pairs={{0,1},{1,0},{2,3},{3,2},{4,5},{5,4},{6,7},{7,6},{8,9},{9,8},{10,11... | collective-permute-start | bytes 884744 | tf_op jit(solution)/shard_map/ppermute | solution.py:355
  127.4 26.2 %collective-permute-start.16 = (bf16[72,2048]{1,0:T(8,128)(2,1)S(1)}, bf16[72,2048]{1,0:T(8,128)(2,1)S(1)}, u32[]{:S(2)}, u32[]{:S(2)}) collective-permute-start(bf16[72,2048]{1,0:T(8,128)(2,1)S(1)} %add_convert_fusion.10), channel_id=1, source_target_pairs={{0,2},{2,0},{4,6},{6,4},{8,10},{10,8},{12,14},{14,12},{1,3},{3,1},... | collective-permute-start | bytes 884744 | tf_op jit(solution)/shard_map/ppermute | solution.py:358
  134.4 12.6 %collective-permute-start.31 = (bf16[72,2048]{1,0:T(8,128)(2,1)S(1)}, bf16[72,2048]{1,0:T(8,128)(2,1)S(1)}, u32[]{:S(2)}, u32[]{:S(2)}) collective-permute-start(bf16[72,2048]{1,0:T(8,128)(2,1)S(1)} %add_convert_fusion.4), channel_id=1, source_target_pairs={{0,2},{2,0},{4,6},{6,4},{8,10},{10,8},{12,14},{14,12},{1,3},{3,1},... | collective-permute-start | bytes 884744 | tf_op jit(solution)/shard_map/ppermute | solution.py:358
  135.8 17.6 %collective-permute-start.23 = (bf16[72,2048]{1,0:T(8,128)(2,1)S(1)}, bf16[72,2048]{1,0:T(8,128)(2,1)S(1)}, u32[]{:S(2)}, u32[]{:S(2)}) collective-permute-start(bf16[72,2048]{1,0:T(8,128)(2,1)S(1)} %add_convert_fusion.7), channel_id=1, source_target_pairs={{0,2},{2,0},{4,6},{6,4},{8,10},{10,8},{12,14},{14,12},{1,3},{3,1},... | collective-permute-start | bytes 884744 | tf_op jit(solution)/shard_map/ppermute | solution.py:358
  147.0 25.9 %collective-permute-start.40 = (bf16[72,2048]{1,0:T(8,128)(2,1)S(1)}, bf16[72,2048]{1,0:T(8,128)(2,1)S(1)}, u32[]{:S(2)}, u32[]{:S(2)}) collective-permute-start(bf16[72,2048]{1,0:T(8,128)(2,1)S(1)} %add_convert_fusion), channel_id=1, source_target_pairs={{0,12},{2,14},{4,8},{6,10},{8,4},{10,6},{12,0},{14,2},{1,13},{3,15... | collective-permute-start | bytes 884744 | tf_op jit(solution)/shard_map/ppermute | solution.py:364
  149.3 23.6 %collective-permute-start.32 = (bf16[72,2048]{1,0:T(8,128)(2,1)S(1)}, bf16[72,2048]{1,0:T(8,128)(2,1)S(1)}, u32[]{:S(2)}, u32[]{:S(2)}) collective-permute-start(bf16[72,2048]{1,0:T(8,128)(2,1)S(1)} %add_convert_fusion.3), channel_id=1, source_target_pairs={{0,4},{2,6},{4,0},{6,2},{8,12},{10,14},{12,8},{14,10},{1,5},{3,7},... | collective-permute-start | bytes 884744 | tf_op jit(solution)/shard_map/ppermute | solution.py:364
  153.5 18.4 %collective-permute-start.24 = (bf16[72,2048]{1,0:T(8,128)(2,1)S(1)}, bf16[72,2048]{1,0:T(8,128)(2,1)S(1)}, u32[]{:S(2)}, u32[]{:S(2)}) collective-permute-start(bf16[72,2048]{1,0:T(8,128)(2,1)S(1)} %add_convert_fusion.6), channel_id=1, source_target_pairs={{0,8},{2,10},{4,12},{6,14},{8,0},{10,2},{12,4},{14,6},{1,9},{3,11}... | collective-permute-start | bytes 884744 | tf_op jit(solution)/shard_map/ppermute | solution.py:364
  (32 other events, 364.3 us)

commit v2 on v1

--- a/solution.py
+++ b/solution.py
@@ -136,14 +136,16 @@
             seen.append(plane >= back)
     factor = HEAD_DIM ** (-0.5) * math.log2(math.e)
 
-    for group in range(shared):
-        key_columns = slice(group * HEAD_DIM, (group + 1) * HEAD_DIM)
-        value_columns = slice((shared + group) * HEAD_DIM, (shared + group + 1) * HEAD_DIM)
-
-        def one_head(member, _):
+    def one_group(group, _):
+        key_columns = pl.ds(pl.multiple_of(group * HEAD_DIM, HEAD_DIM), HEAD_DIM)
+        value_columns = pl.ds(
+            pl.multiple_of((shared + group) * HEAD_DIM, HEAD_DIM), HEAD_DIM
+        )
+
+        def one_head(member):
             head = group * sharing + member
             query = query_ref[head]
-            highest = jnp.full((rows, HEAD_DIM), masked_score, f32)
+            highest = None
             for index, keyval_ref in enumerate(keyval_refs):
                 score = lax.dot_general(
                     query,
@@ -154,19 +156,21 @@
                 own = first and index == 0
                 if own:
                     score = jnp.where(own_visible, score, masked_score)
-                score_ref[:, index * rows : (index + 1) * rows] = score
+                score_ref[member, :, index * rows : (index + 1) * rows] = score
                 most = score[:, :HEAD_DIM]
                 for start in range(HEAD_DIM, rows, HEAD_DIM):
                     most = jnp.maximum(most, score[:, start : start + HEAD_DIM])
                 if not own:
                     most = jnp.where(seen[index], most, masked_score)
-                highest = jnp.maximum(highest, most)
-            highest = jnp.max(highest, axis=-1, keepdims=True)
+                highest = most if highest is None else jnp.maximum(highest, most)
+            highest = jnp.broadcast_to(
+                jnp.max(highest, axis=-1, keepdims=True), (rows, HEAD_DIM)
+            )
             if first:
                 totals = jnp.zeros((rows, HEAD_DIM), f32)
                 mixed = jnp.zeros((rows, HEAD_DIM), f32)
             else:
-                earlier = before[0][head][:, :1]
+                earlier = before[0][head]
                 highest = jnp.maximum(highest, earlier)
                 shrink = jnp.exp2(earlier - highest)
                 totals = before[1][head] * shrink
@@ -175,20 +179,25 @@
                 ceiling = highest
                 if not (first and index == 0):
                     ceiling = jnp.where(seen[index], highest, -masked_score)
-                expo = jnp.exp2(score_ref[:, index * rows : (index + 1) * rows] - ceiling)
-                for start in range(0, rows, HEAD_DIM):
-                    totals = totals + expo[:, start : start + HEAD_DIM]
-                mixed = mixed + dot(expo.astype(bf16), keyval_ref[:, value_columns])
+                probs = []
+                for start in range(index * rows, (index + 1) * rows, HEAD_DIM):
+                    expo = jnp.exp2(score_ref[member, :, start : start + HEAD_DIM] - ceiling)
+                    totals = totals + expo
+                    probs.append(expo.astype(bf16))
+                mixed = mixed + dot(jnp.concatenate(probs, axis=1), keyval_ref[:, value_columns])
             if last:
                 total = jnp.sum(totals, axis=-1, keepdims=True)
                 context_ref[head] = (mixed / total).astype(bf16)
             else:
-                after[0][head] = jnp.broadcast_to(highest, (rows, HEAD_DIM))
+                after[0][head] = highest
                 after[1][head] = totals
                 after[2][head] = mixed
-            return 0
-
-        lax.fori_loop(0, sharing, one_head, 0)
+
+        for member in range(sharing):
+            one_head(member)
+        return 0
+
+    lax.fori_loop(0, shared, one_group, 0)
 
     if last:
         send_ref, keep_ref = after
@@ -347,6 +356,7 @@
     query_width = query_weight.shape[1] // cores
     keyval_width = key_value_weight.shape[1] // cores
     heads = query_width // HEAD_DIM
+    sharing = query_weight.shape[1] * 2 // key_value_weight.shape[1]
     pair_rows = local_rows * cores
     chip = lax.axis_index("expert")
     core = lax.axis_index("dp")
@@ -431,7 +441,9 @@
         blocks, places = zip(*part) if part else ((), ())
         last = index == len(parts) - 1
         outs = [shape((heads, pair_rows, HEAD_DIM), f32)] * 3
-        scratch = [pltpu.VMEM((pair_rows, pair_rows * max(1, len(blocks))), f32)]
+        scratch = [
+            pltpu.VMEM((sharing, pair_rows, pair_rows * max(1, len(blocks))), f32)
+        ]
         if last:
             outs = [shape((local_rows, model_width), bf16), shape((local_rows, model_width), f32)]
             scratch.append(pltpu.VMEM((heads, pair_rows, HEAD_DIM), bf16))
@@ -443,7 +455,7 @@
             flops=4 * pair_rows * pair_rows * len(blocks) * query_width
             + 2 * pair_rows * query_width * model_width * last,
             moved=8 * pair_rows * query_width,
-            limit=8 << 20,
+            limit=14 << 20,
         )
     attention_send, attention_keep = state
     attention_came = across(attention_send)

time: 178 us -> 174 us (0.978)
  Pallas kernels: 55.3 us -> 47.9 us
  waiting for transfers between devices: 78.5 us -> 82.9 us
    pallas_call x16, Pallas kernels: 53.3 us -> 45.9 us  [call(): pl.pallas_call(kernel, out_shape=outs, in_specs=[VMEM] * len(operands), o...]
    ppermute x12, waiting for transfers between devices: 21.7 us -> 26.5 us  [beside(): return lax.ppermute(x, 'expert', [(i, i ^ turn) for i in range(chips)])]
  transfers between devices with their start and end apart: 41 -> 41, of which waited for: 12 -> 15; matrix products, arithmetic and copies ran while one was open for 1% -> 1% of each run, Pallas kernels for 26% -> 24%
where the time goes in v2:
time: 174 us; the launch traced here: 171 us
  waiting for transfers between devices  82.9 us (48%)
  Pallas kernels  47.9 us (28%)
  starting transfers between devices  30.3 us (17%)
  local copies, waits for them, and re-layouts  7.75 us (4%)
    pallas_call x16, Pallas kernels, call(): pl.pallas_call(kernel, out_shape=outs, in_specs=[VMEM] * len(operands), o...  45.9 us
    ppermute x6, waiting for transfers between devices, planes(): lax.ppermute(x, 'expert', [(i, i ^ step * along) for i in range(chips)])  30.1 us
    ppermute x12, waiting for transfers between devices, beside(): return lax.ppermute(x, 'expert', [(i, i ^ turn) for i in range(chips)])  26.5 us
    ppermute x3, waiting for transfers between devices, upward(): lax.ppermute(x, 'expert', [(i, (i + along) % chips) for i in range(chips)])  23.7 us
    ppermute x20, starting transfers between devices, across(): return lax.ppermute(x, 'dp', [(i, i ^ 1) for i in range(cores)])  12.5 us
    ppermute x12, starting transfers between devices, beside(): return lax.ppermute(x, 'expert', [(i, i ^ turn) for i in range(chips)])  8.91 us
    unnamed x30, local copies, waits for them, and re-layouts  7.75 us
    ppermute x6, starting transfers between devices, planes(): lax.ppermute(x, 'expert', [(i, i ^ step * along) for i in range(chips)])  6.04 us
  transfers between devices with their start and end apart: 41, of which 15 were waited for; matrix products, arithmetic and copies ran while one was open for 1% of the time, Pallas kernels for 24%

profile of v2, /device:TPU:1, one launch (start us, length us, event | category | flops | bytes accessed | tf_op | source)
XLA Modules:
  0.0 170.8 jit_solution(17430218196313490398)
XLA Ops:
  5.2 2.2 %copy-done = bf16[1024,2048]{1,0:T(8,128)(2,1)S(1)} copy-done((bf16[1024,2048]{1,0:T(8,128)(2,1)S(1)}, bf16[1024,2048]{1,0:T(8,128)(2,1)}, u32[]{:S(2)}) %copy-start) | copy-done | bytes 4194328
  9.7 2.8 %collective-permute-start.3 = (bf16[256,512]{1,0:T(8,128)(2,1)S(1)}, bf16[256,512]{1,0:T(8,128)(2,1)S(1)}, u32[]{:S(2)}, u32[]{:S(2)}) collective-permute-start(bf16[256,512]{1,0:T(8,128)(2,1)S(1)} %shard_map.113.refs_0_), channel_id=1, source_target_pairs={{0,4},{2,6},{4,8},{6,10},{8,12},{10,14},{12,0},{14,2},{1,5},{3,7},... | collective-permute-start | bytes 786440 | tf_op jit(solution)/shard_map/ppermute | solution.py:371
  12.5 8.7 %collective-permute-done.3.refs_2_ = bf16[256,512]{1,0:T(8,128)(2,1)S(1)} collective-permute-done((bf16[256,512]{1,0:T(8,128)(2,1)S(1)}, bf16[256,512]{1,0:T(8,128)(2,1)S(1)}, u32[]{:S(2)}, u32[]{:S(2)}) %collective-permute-start.3) | collective-permute-done | bytes 262176 | tf_op jit(solution)/shard_map/ppermute | solution.py:371
  21.2 9.1 %collective-permute-done.4.refs_1_ = bf16[256,512]{1,0:T(8,128)(2,1)S(1)} collective-permute-done((bf16[256,512]{1,0:T(8,128)(2,1)S(1)}, bf16[256,512]{1,0:T(8,128)(2,1)S(1)}, u32[]{:S(2)}, u32[]{:S(2)}) %collective-permute-start.4) | collective-permute-done | bytes 262176 | tf_op jit(solution)/shard_map/ppermute | solution.py:371
  32.5 6.0 %collective-permute-done.5.refs_1_ = bf16[256,512]{1,0:T(8,128)(2,1)S(1)} collective-permute-done((bf16[256,512]{1,0:T(8,128)(2,1)S(1)}, bf16[256,512]{1,0:T(8,128)(2,1)S(1)}, u32[]{:S(2)}, u32[]{:S(2)}) %collective-permute-start.5) | collective-permute-done | bytes 262176 | tf_op jit(solution)/shard_map/ppermute | solution.py:371
  39.4 3.6 %shard_map.114 = (f32[8,256,128]{2,1,0:T(8,128)S(1)}, f32[8,256,128]{2,1,0:T(8,128)S(1)}, f32[8,256,128]{2,1,0:T(8,128)S(1)}) custom-call(bf16[8,256,128]{2,1,0:T(8,128)(2,1)S(1)} %shard_map.111.query_ref, bf16[256,512]{1,0:T(8,128)(2,1)S(1)} %shard_map.113.refs_0_, bf16[256,512]{1,0:T(8,128)(2,1)S(1)} %collective-permute-done.9.refs_1_, ...), custom_call_target="tpu_custom_call" | custom-call | flops 805306368 | bytes 2097152 | tf_op jit(solution)/shard_map/pallas_call | solution.py:35
  43.1 2.9 %shard_map.115 = (f32[8,256,128]{2,1,0:T(8,128)S(1)}, f32[8,256,128]{2,1,0:T(8,128)S(1)}, f32[8,256,128]{2,1,0:T(8,128)S(1)}) custom-call(bf16[8,256,128]{2,1,0:T(8,128)(2,1)S(1)} %shard_map.111.query_ref, bf16[256,512]{1,0:T(8,128)(2,1)S(1)} %collective-permute-done.8.refs_0_, bf16[256,512]{1,0:T(8,128)(2,1)S(1)} %collective-permute-done.4.refs_1_, ...), custom_call_target="tpu_custom_call" | custom-call | flops 536870912 | bytes 2097152 | tf_op jit(solution)/shard_map/pallas_call | solution.py:35
  47.9 2.9 %shard_map.116 = (f32[8,256,128]{2,1,0:T(8,128)S(1)}, f32[8,256,128]{2,1,0:T(8,128)S(1)}, f32[8,256,128]{2,1,0:T(8,128)S(1)}) custom-call(bf16[8,256,128]{2,1,0:T(8,128)(2,1)S(1)} %shard_map.111.query_ref, bf16[256,512]{1,0:T(8,128)(2,1)S(1)} %collective-permute-done.7.refs_0_, bf16[256,512]{1,0:T(8,128)(2,1)S(1)} %collective-permute-done.5.refs_1_, ...), custom_call_target="tpu_custom_call" | custom-call | flops 536870912 | bytes 2097152 | tf_op jit(solution)/shard_map/pallas_call | solution.py:35
  50.8 2.7 %collective-permute-done.6.refs_0_ = bf16[256,512]{1,0:T(8,128)(2,1)S(1)} collective-permute-done((bf16[256,512]{1,0:T(8,128)(2,1)S(1)}, bf16[256,512]{1,0:T(8,128)(2,1)S(1)}, u32[]{:S(2)}, u32[]{:S(2)}) %collective-permute-start.6) | collective-permute-done | bytes 262176 | tf_op jit(solution)/shard_map/ppermute | solution.py:368
  53.5 3.0 %shard_map.117 = (bf16[128,2048]{1,0:T(8,128)(2,1)S(1)}, f32[128,2048]{1,0:T(8,128)S(1)}) custom-call(bf16[8,256,128]{2,1,0:T(8,128)(2,1)S(1)} %shard_map.111.query_ref, bf16[256,512]{1,0:T(8,128)(2,1)S(1)} %collective-permute-done.6.refs_0_, f32[8,256,128]{2,1,0:T(8,128)S(1)} %get-tuple-element.55.refs_1_, f32[8,256,128]{2,1,0:T(8,128)S(1)} %get-tuple-element.56.refs_2_, ...), custom_call_target="tpu_custom_call" | custom-call | flops 1342177280 | bytes 2097152 | tf_op jit(solution)/shard_map/pallas_call | solution.py:35
  56.5 2.4 %collective-permute-start.10 = (bf16[128,2048]{1,0:T(8,128)(2,1)S(1)}, bf16[128,2048]{1,0:T(8,128)(2,1)S(1)}, u32[]{:S(2)}, u32[]{:S(2)}) collective-permute-start(bf16[128,2048]{1,0:T(8,128)(2,1)S(1)} %get-tuple-element.59), channel_id=1, source_target_pairs={{0,1},{1,0},{2,3},{3,2},{4,5},{5,4},{6,7},{7,6},{8,9},{9,8},{10,11... | collective-permute-start | bytes 1572872 | tf_op jit(solution)/shard_map/ppermute | solution.py:365
  61.7 3.3 %collective-permute-start.33 = (bf16[72,2048]{1,0:T(8,128)(2,1)S(1)}, bf16[72,2048]{1,0:T(8,128)(2,1)S(1)}, u32[]{:S(2)}, u32[]{:S(2)}) collective-permute-start(bf16[72,2048]{1,0:T(8,128)(2,1)S(1)} %get-tuple-element.76), channel_id=1, source_target_pairs={{0,12},{2,14},{4,8},{6,10},{8,4},{10,6},{12,0},{14,2},{1,13},{3,15... | collective-permute-start | bytes 884744 | tf_op jit(solution)/shard_map/ppermute | solution.py:374
  67.6 4.3 %collective-permute-done.33.refs_0_ = bf16[72,2048]{1,0:T(8,128)(2,1)S(1)} collective-permute-done((bf16[72,2048]{1,0:T(8,128)(2,1)S(1)}, bf16[72,2048]{1,0:T(8,128)(2,1)S(1)}, u32[]{:S(2)}, u32[]{:S(2)}) %collective-permute-start.33) | collective-permute-done | bytes 294944 | tf_op jit(solution)/shard_map/ppermute | solution.py:374
  79.0 3.6 %collective-permute-done.25.refs_0_ = bf16[72,2048]{1,0:T(8,128)(2,1)S(1)} collective-permute-done((bf16[72,2048]{1,0:T(8,128)(2,1)S(1)}, bf16[72,2048]{1,0:T(8,128)(2,1)S(1)}, u32[]{:S(2)}, u32[]{:S(2)}) %collective-permute-start.25) | collective-permute-done | bytes 294944 | tf_op jit(solution)/shard_map/ppermute | solution.py:374
  83.1 4.0 %collective-permute-done.17.refs_0_ = bf16[72,2048]{1,0:T(8,128)(2,1)S(1)} collective-permute-done((bf16[72,2048]{1,0:T(8,128)(2,1)S(1)}, bf16[72,2048]{1,0:T(8,128)(2,1)S(1)}, u32[]{:S(2)}, u32[]{:S(2)}) %collective-permute-start.17) | collective-permute-done | bytes 294944 | tf_op jit(solution)/shard_map/ppermute | solution.py:374
  90.5 6.6 %shard_map.119 = (bf16[72,2048]{1,0:T(8,128)(2,1)S(1)}, bf16[72,2048]{1,0:T(8,128)(2,1)S(1)}, bf16[72,2048]{1,0:T(8,128)(2,1)S(1)}, bf16[72,2048]{1,0:T(8,128)(2,1)S(1)}) custom-call(bf16[2048,1792]{1,0:T(8,128)(2,1)S(1)} %fetch.5.gate_ref, bf16[2048,1792]{1,0:T(8,128)(2,1)S(1)} %fetch.6.up_ref, bf16[1792,2048]{1,0:T(8,128)(2,1)S(1)} %fetch.7.down_ref, ...), custom_call_target="tpu_custom_call" | custom-call | flops 6341787648 | bytes 22020096 | tf_op jit(solution)/shard_map/pallas_call | solution.py:35
  98.3 6.6 %shard_map.123 = (bf16[72,2048]{1,0:T(8,128)(2,1)S(1)}, bf16[72,2048]{1,0:T(8,128)(2,1)S(1)}, bf16[72,2048]{1,0:T(8,128)(2,1)S(1)}, bf16[72,2048]{1,0:T(8,128)(2,1)S(1)}) custom-call(bf16[2048,1792]{1,0:T(8,128)(2,1)S(1)} %fetch.5.gate_ref, bf16[2048,1792]{1,0:T(8,128)(2,1)S(1)} %fetch.6.up_ref, bf16[1792,2048]{1,0:T(8,128)(2,1)S(1)} %fetch.7.down_ref, ...), custom_call_target="tpu_custom_call" | custom-call | flops 6341787648 | bytes 22020096 | tf_op jit(solution)/shard_map/pallas_call | solution.py:35
  105.9 6.8 %shard_map.122 = (bf16[72,2048]{1,0:T(8,128)(2,1)S(1)}, bf16[72,2048]{1,0:T(8,128)(2,1)S(1)}, bf16[72,2048]{1,0:T(8,128)(2,1)S(1)}, bf16[72,2048]{1,0:T(8,128)(2,1)S(1)}) custom-call(bf16[2048,1792]{1,0:T(8,128)(2,1)S(1)} %fetch.5.gate_ref, bf16[2048,1792]{1,0:T(8,128)(2,1)S(1)} %fetch.6.up_ref, bf16[1792,2048]{1,0:T(8,128)(2,1)S(1)} %fetch.7.down_ref, ...), custom_call_target="tpu_custom_call" | custom-call | flops 6341787648 | bytes 22020096 | tf_op jit(solution)/shard_map/pallas_call | solution.py:35
  113.4 6.6 %shard_map.120 = (bf16[72,2048]{1,0:T(8,128)(2,1)S(1)}, bf16[72,2048]{1,0:T(8,128)(2,1)S(1)}, bf16[72,2048]{1,0:T(8,128)(2,1)S(1)}, bf16[72,2048]{1,0:T(8,128)(2,1)S(1)}) custom-call(bf16[2048,1792]{1,0:T(8,128)(2,1)S(1)} %fetch.5.gate_ref, bf16[2048,1792]{1,0:T(8,128)(2,1)S(1)} %fetch.6.up_ref, bf16[1792,2048]{1,0:T(8,128)(2,1)S(1)} %fetch.7.down_ref, ...), custom_call_target="tpu_custom_call" | custom-call | flops 6341787648 | bytes 22020096 | tf_op jit(solution)/shard_map/pallas_call | solution.py:35
  123.7 6.7 %collective-permute-done.39 = bf16[72,2048]{1,0:T(8,128)(2,1)S(1)} collective-permute-done((bf16[72,2048]{1,0:T(8,128)(2,1)S(1)}, bf16[72,2048]{1,0:T(8,128)(2,1)S(1)}, u32[]{:S(2)}, u32[]{:S(2)}) %collective-permute-start.39) | collective-permute-done | bytes 294944 | tf_op jit(solution)/shard_map/ppermute | solution.py:368
  132.0 11.0 %collective-permute-done.31 = bf16[72,2048]{1,0:T(8,128)(2,1)S(1)} collective-permute-done((bf16[72,2048]{1,0:T(8,128)(2,1)S(1)}, bf16[72,2048]{1,0:T(8,128)(2,1)S(1)}, u32[]{:S(2)}, u32[]{:S(2)}) %collective-permute-start.31) | collective-permute-done | bytes 294944 | tf_op jit(solution)/shard_map/ppermute | solution.py:368
  143.0 2.2 %collective-permute-start.40 = (bf16[72,2048]{1,0:T(8,128)(2,1)S(1)}, bf16[72,2048]{1,0:T(8,128)(2,1)S(1)}, u32[]{:S(2)}, u32[]{:S(2)}) collective-permute-start(bf16[72,2048]{1,0:T(8,128)(2,1)S(1)} %add_convert_fusion), channel_id=1, source_target_pairs={{0,12},{2,14},{4,8},{6,10},{8,4},{10,6},{12,0},{14,2},{1,13},{3,15... | collective-permute-start | bytes 884744 | tf_op jit(solution)/shard_map/ppermute | solution.py:374
  145.4 3.9 %collective-permute-done.23 = bf16[72,2048]{1,0:T(8,128)(2,1)S(1)} collective-permute-done((bf16[72,2048]{1,0:T(8,128)(2,1)S(1)}, bf16[72,2048]{1,0:T(8,128)(2,1)S(1)}, u32[]{:S(2)}, u32[]{:S(2)}) %collective-permute-start.23) | collective-permute-done | bytes 294944 | tf_op jit(solution)/shard_map/ppermute | solution.py:368
  149.7 18.2 %collective-permute-done.24.refs_1_ = bf16[72,2048]{1,0:T(8,128)(2,1)S(1)} collective-permute-done((bf16[72,2048]{1,0:T(8,128)(2,1)S(1)}, bf16[72,2048]{1,0:T(8,128)(2,1)S(1)}, u32[]{:S(2)}, u32[]{:S(2)}) %collective-permute-start.24) | collective-permute-done | bytes 294944 | tf_op jit(solution)/shard_map/ppermute | solution.py:374
  (123 shorter events, 40.3 us)
Async XLA Ops:
  8.7 30.3 %collective-permute-start.1 = (f32[256,1024]{1,0:T(8,128)S(1)}, f32[256,1024]{1,0:T(8,128)S(1)}, u32[]{:S(2)}, u32[]{:S(2)}) collective-permute-start(f32[256,1024]{1,0:T(8,128)S(1)} %get-tuple-element.46), channel_id=1, source_target_pairs={{0,1},{1,0},{2,3},{3,2},{4,5},{5,4},{6,7},{7,6},{8,9},{9,8},{10,11... | collective-permute-start | bytes 3145736 | tf_op jit(solution)/shard_map/ppermute | solution.py:365
  31.0 12.0 %collective-permute-start.8 = (bf16[256,512]{1,0:T(8,128)(2,1)S(1)}, bf16[256,512]{1,0:T(8,128)(2,1)S(1)}, u32[]{:S(2)}, u32[]{:S(2)}) collective-permute-start(bf16[256,512]{1,0:T(8,128)(2,1)S(1)} %collective-permute-done.3.refs_2_), channel_id=1, source_target_pairs={{0,2},{2,0},{4,6},{6,4},{8,10},{10,8},{12,14},{14,12},{1,3},{3,1},... | collective-permute-start | bytes 786440 | tf_op jit(solution)/shard_map/ppermute | solution.py:368
  31.7 16.2 %collective-permute-start.7 = (bf16[256,512]{1,0:T(8,128)(2,1)S(1)}, bf16[256,512]{1,0:T(8,128)(2,1)S(1)}, u32[]{:S(2)}, u32[]{:S(2)}) collective-permute-start(bf16[256,512]{1,0:T(8,128)(2,1)S(1)} %collective-permute-done.4.refs_1_), channel_id=1, source_target_pairs={{0,2},{2,0},{4,6},{6,4},{8,10},{10,8},{12,14},{14,12},{1,3},{3,1},... | collective-permute-start | bytes 786440 | tf_op jit(solution)/shard_map/ppermute | solution.py:368
  38.5 15.1 %collective-permute-start.6 = (bf16[256,512]{1,0:T(8,128)(2,1)S(1)}, bf16[256,512]{1,0:T(8,128)(2,1)S(1)}, u32[]{:S(2)}, u32[]{:S(2)}) collective-permute-start(bf16[256,512]{1,0:T(8,128)(2,1)S(1)} %collective-permute-done.5.refs_1_), channel_id=1, source_target_pairs={{0,2},{2,0},{4,6},{6,4},{8,10},{10,8},{12,14},{14,12},{1,3},{3,1},... | collective-permute-start | bytes 786440 | tf_op jit(solution)/shard_map/ppermute | solution.py:368
  65.8 16.9 %collective-permute-start.25 = (bf16[72,2048]{1,0:T(8,128)(2,1)S(1)}, bf16[72,2048]{1,0:T(8,128)(2,1)S(1)}, u32[]{:S(2)}, u32[]{:S(2)}) collective-permute-start(bf16[72,2048]{1,0:T(8,128)(2,1)S(1)} %get-tuple-element.71), channel_id=1, source_target_pairs={{0,4},{2,6},{4,0},{6,2},{8,12},{10,14},{12,8},{14,10},{1,5},{3,7},... | collective-permute-start | bytes 884744 | tf_op jit(solution)/shard_map/ppermute | solution.py:374
  65.8 21.3 %collective-permute-start.17 = (bf16[72,2048]{1,0:T(8,128)(2,1)S(1)}, bf16[72,2048]{1,0:T(8,128)(2,1)S(1)}, u32[]{:S(2)}, u32[]{:S(2)}) collective-permute-start(bf16[72,2048]{1,0:T(8,128)(2,1)S(1)} %get-tuple-element.66), channel_id=1, source_target_pairs={{0,8},{2,10},{4,12},{6,14},{8,0},{10,2},{12,4},{14,6},{1,9},{3,11}... | collective-permute-start | bytes 884744 | tf_op jit(solution)/shard_map/ppermute | solution.py:374
  66.2 22.1 %collective-permute-start.12 = (bf16[72,2048]{1,0:T(8,128)(2,1)S(1)}, bf16[72,2048]{1,0:T(8,128)(2,1)S(1)}, u32[]{:S(2)}, u32[]{:S(2)}) collective-permute-start(bf16[72,2048]{1,0:T(8,128)(2,1)S(1)} %get-tuple-element.61.refs_0_), channel_id=1, source_target_pairs={{0,1},{1,0},{2,3},{3,2},{4,5},{5,4},{6,7},{7,6},{8,9},{9,8},{10,11... | collective-permute-start | bytes 884744 | tf_op jit(solution)/shard_map/ppermute | solution.py:365
  71.8 18.0 %collective-permute-start.34 = (bf16[72,2048]{1,0:T(8,128)(2,1)S(1)}, bf16[72,2048]{1,0:T(8,128)(2,1)S(1)}, u32[]{:S(2)}, u32[]{:S(2)}) collective-permute-start(bf16[72,2048]{1,0:T(8,128)(2,1)S(1)} %collective-permute-done.33.refs_0_), channel_id=1, source_target_pairs={{0,2},{2,0},{4,6},{6,4},{8,10},{10,8},{12,14},{14,12},{1,3},{3,1},... | collective-permute-start | bytes 884744 | tf_op jit(solution)/shard_map/ppermute | solution.py:368
  72.9 17.2 %collective-permute-start.13 = (bf16[72,2048]{1,0:T(8,128)(2,1)S(1)}, bf16[72,2048]{1,0:T(8,128)(2,1)S(1)}, u32[]{:S(2)}, u32[]{:S(2)}) collective-permute-start(bf16[72,2048]{1,0:T(8,128)(2,1)S(1)} %collective-permute-done.11.refs_1_), channel_id=1, source_target_pairs={{0,1},{1,0},{2,3},{3,2},{4,5},{5,4},{6,7},{7,6},{8,9},{9,8},{10,11... | collective-permute-start | bytes 884744 | tf_op jit(solution)/shard_map/ppermute | solution.py:365
  82.7 14.4 %collective-permute-start.35 = (bf16[72,2048]{1,0:T(8,128)(2,1)S(1)}, bf16[72,2048]{1,0:T(8,128)(2,1)S(1)}, u32[]{:S(2)}, u32[]{:S(2)}) collective-permute-start(bf16[72,2048]{1,0:T(8,128)(2,1)S(1)} %collective-permute-done.33.refs_0_), channel_id=1, source_target_pairs={{0,1},{1,0},{2,3},{3,2},{4,5},{5,4},{6,7},{7,6},{8,9},{9,8},{10,11... | collective-permute-start | bytes 884744 | tf_op jit(solution)/shard_map/ppermute | solution.py:365
  88.3 16.6 %collective-permute-start.27 = (bf16[72,2048]{1,0:T(8,128)(2,1)S(1)}, bf16[72,2048]{1,0:T(8,128)(2,1)S(1)}, u32[]{:S(2)}, u32[]{:S(2)}) collective-permute-start(bf16[72,2048]{1,0:T(8,128)(2,1)S(1)} %collective-permute-done.25.refs_0_), channel_id=1, source_target_pairs={{0,1},{1,0},{2,3},{3,2},{4,5},{5,4},{6,7},{7,6},{8,9},{9,8},{10,11... | collective-permute-start | bytes 884744 | tf_op jit(solution)/shard_map/ppermute | solution.py:365
  89.8 15.6 %collective-permute-start.18 = (bf16[72,2048]{1,0:T(8,128)(2,1)S(1)}, bf16[72,2048]{1,0:T(8,128)(2,1)S(1)}, u32[]{:S(2)}, u32[]{:S(2)}) collective-permute-start(bf16[72,2048]{1,0:T(8,128)(2,1)S(1)} %collective-permute-done.17.refs_0_), channel_id=1, source_target_pairs={{0,2},{2,0},{4,6},{6,4},{8,10},{10,8},{12,14},{14,12},{1,3},{3,1},... | collective-permute-start | bytes 884744 | tf_op jit(solution)/shard_map/ppermute | solution.py:368
  97.1 15.7 %collective-permute-start.19 = (bf16[72,2048]{1,0:T(8,128)(2,1)S(1)}, bf16[72,2048]{1,0:T(8,128)(2,1)S(1)}, u32[]{:S(2)}, u32[]{:S(2)}) collective-permute-start(bf16[72,2048]{1,0:T(8,128)(2,1)S(1)} %collective-permute-done.17.refs_0_), channel_id=1, source_target_pairs={{0,1},{1,0},{2,3},{3,2},{4,5},{5,4},{6,7},{7,6},{8,9},{9,8},{10,11... | collective-permute-start | bytes 884744 | tf_op jit(solution)/shard_map/ppermute | solution.py:365
  97.3 22.7 %collective-permute-start.15 = (bf16[72,2048]{1,0:T(8,128)(2,1)S(1)}, bf16[72,2048]{1,0:T(8,128)(2,1)S(1)}, u32[]{:S(2)}, u32[]{:S(2)}) collective-permute-start(bf16[72,2048]{1,0:T(8,128)(2,1)S(1)} %get-tuple-element.65), channel_id=1, source_target_pairs={{0,1},{1,0},{2,3},{3,2},{4,5},{5,4},{6,7},{7,6},{8,9},{9,8},{10,11... | collective-permute-start | bytes 884744 | tf_op jit(solution)/shard_map/ppermute | solution.py:365
  104.9 44.7 %collective-permute-start.14 = (bf16[72,2048]{1,0:T(8,128)(2,1)S(1)}, bf16[72,2048]{1,0:T(8,128)(2,1)S(1)}, u32[]{:S(2)}, u32[]{:S(2)}) collective-permute-start(bf16[72,2048]{1,0:T(8,128)(2,1)S(1)} %get-tuple-element.63), channel_id=1, source_target_pairs={{0,1},{1,0},{2,3},{3,2},{4,5},{5,4},{6,7},{7,6},{8,9},{9,8},{10,11... | collective-permute-start | bytes 884744 | tf_op jit(solution)/shard_map/ppermute | solution.py:365
  105.5 14.7 %collective-permute-start.38 = (bf16[72,2048]{1,0:T(8,128)(2,1)S(1)}, bf16[72,2048]{1,0:T(8,128)(2,1)S(1)}, u32[]{:S(2)}, u32[]{:S(2)}) collective-permute-start(bf16[72,2048]{1,0:T(8,128)(2,1)S(1)} %get-tuple-element.80), channel_id=1, source_target_pairs={{0,1},{1,0},{2,3},{3,2},{4,5},{5,4},{6,7},{7,6},{8,9},{9,8},{10,11... | collective-permute-start | bytes 884744 | tf_op jit(solution)/shard_map/ppermute | solution.py:365
  120.0 11.7 %collective-permute-start.29 = (bf16[72,2048]{1,0:T(8,128)(2,1)S(1)}, bf16[72,2048]{1,0:T(8,128)(2,1)S(1)}, u32[]{:S(2)}, u32[]{:S(2)}) collective-permute-start(bf16[72,2048]{1,0:T(8,128)(2,1)S(1)} %get-tuple-element.73), channel_id=1, source_target_pairs={{0,1},{1,0},{2,3},{3,2},{4,5},{5,4},{6,7},{7,6},{8,9},{9,8},{10,11... | collective-permute-start | bytes 884744 | tf_op jit(solution)/shard_map/ppermute | solution.py:365
  120.8 24.6 %collective-permute-start.21 = (bf16[72,2048]{1,0:T(8,128)(2,1)S(1)}, bf16[72,2048]{1,0:T(8,128)(2,1)S(1)}, u32[]{:S(2)}, u32[]{:S(2)}) collective-permute-start(bf16[72,2048]{1,0:T(8,128)(2,1)S(1)} %get-tuple-element.68), channel_id=1, source_target_pairs={{0,1},{1,0},{2,3},{3,2},{4,5},{5,4},{6,7},{7,6},{8,9},{9,8},{10,11... | collective-permute-start | bytes 884744 | tf_op jit(solution)/shard_map/ppermute | solution.py:365
  123.3 26.3 %collective-permute-start.16 = (bf16[72,2048]{1,0:T(8,128)(2,1)S(1)}, bf16[72,2048]{1,0:T(8,128)(2,1)S(1)}, u32[]{:S(2)}, u32[]{:S(2)}) collective-permute-start(bf16[72,2048]{1,0:T(8,128)(2,1)S(1)} %add_convert_fusion.10), channel_id=1, source_target_pairs={{0,2},{2,0},{4,6},{6,4},{8,10},{10,8},{12,14},{14,12},{1,3},{3,1},... | collective-permute-start | bytes 884744 | tf_op jit(solution)/shard_map/ppermute | solution.py:368
  130.4 12.6 %collective-permute-start.31 = (bf16[72,2048]{1,0:T(8,128)(2,1)S(1)}, bf16[72,2048]{1,0:T(8,128)(2,1)S(1)}, u32[]{:S(2)}, u32[]{:S(2)}) collective-permute-start(bf16[72,2048]{1,0:T(8,128)(2,1)S(1)} %add_convert_fusion.4), channel_id=1, source_target_pairs={{0,2},{2,0},{4,6},{6,4},{8,10},{10,8},{12,14},{14,12},{1,3},{3,1},... | collective-permute-start | bytes 884744 | tf_op jit(solution)/shard_map/ppermute | solution.py:368
  131.6 17.7 %collective-permute-start.23 = (bf16[72,2048]{1,0:T(8,128)(2,1)S(1)}, bf16[72,2048]{1,0:T(8,128)(2,1)S(1)}, u32[]{:S(2)}, u32[]{:S(2)}) collective-permute-start(bf16[72,2048]{1,0:T(8,128)(2,1)S(1)} %add_convert_fusion.7), channel_id=1, source_target_pairs={{0,2},{2,0},{4,6},{6,4},{8,10},{10,8},{12,14},{14,12},{1,3},{3,1},... | collective-permute-start | bytes 884744 | tf_op jit(solution)/shard_map/ppermute | solution.py:368
  143.0 25.9 %collective-permute-start.40 = (bf16[72,2048]{1,0:T(8,128)(2,1)S(1)}, bf16[72,2048]{1,0:T(8,128)(2,1)S(1)}, u32[]{:S(2)}, u32[]{:S(2)}) collective-permute-start(bf16[72,2048]{1,0:T(8,128)(2,1)S(1)} %add_convert_fusion), channel_id=1, source_target_pairs={{0,12},{2,14},{4,8},{6,10},{8,4},{10,6},{12,0},{14,2},{1,13},{3,15... | collective-permute-start | bytes 884744 | tf_op jit(solution)/shard_map/ppermute | solution.py:374
  145.3 23.6 %collective-permute-start.32 = (bf16[72,2048]{1,0:T(8,128)(2,1)S(1)}, bf16[72,2048]{1,0:T(8,128)(2,1)S(1)}, u32[]{:S(2)}, u32[]{:S(2)}) collective-permute-start(bf16[72,2048]{1,0:T(8,128)(2,1)S(1)} %add_convert_fusion.3), channel_id=1, source_target_pairs={{0,4},{2,6},{4,0},{6,2},{8,12},{10,14},{12,8},{14,10},{1,5},{3,7},... | collective-permute-start | bytes 884744 | tf_op jit(solution)/shard_map/ppermute | solution.py:374
  149.5 18.4 %collective-permute-start.24 = (bf16[72,2048]{1,0:T(8,128)(2,1)S(1)}, bf16[72,2048]{1,0:T(8,128)(2,1)S(1)}, u32[]{:S(2)}, u32[]{:S(2)}) collective-permute-start(bf16[72,2048]{1,0:T(8,128)(2,1)S(1)} %add_convert_fusion.6), channel_id=1, source_target_pairs={{0,8},{2,10},{4,12},{6,14},{8,0},{10,2},{12,4},{14,6},{1,9},{3,11}... | collective-permute-start | bytes 884744 | tf_op jit(solution)/shard_map/ppermute | solution.py:374
  (32 other events, 352.2 us)

commit v3 on v2

--- a/solution.py
+++ b/solution.py
@@ -16,7 +16,7 @@
 
 HIDDEN_STEP = 256
 DOWN_STEP = 256
-ORDER = (0, 2, 1, 3)
+ORDER = (0, 1, 2, 3)
 
 epsilon = 1e-05
 base_theta = 1000000.0
@@ -499,8 +499,8 @@
         )
 
     a, b, c, d = ORDER
-    early = combined(residual, (a, b), f32)
-    return combined(early, (c, d), bf16)
+    early = combined(residual, (a, c), f32)
+    return combined(early, (b, d), bf16)
 
 
 def solution(mesh):

time: 174 us -> 174 us (level)
  no operation moved by 1% of the time
where the time goes in v3:
time: 174 us; the launch traced here: 171 us
  waiting for transfers between devices  82.9 us (48%)
  Pallas kernels  47.9 us (28%)
  starting transfers between devices  30.3 us (17%)
  local copies, waits for them, and re-layouts  7.75 us (4%)
    pallas_call x16, Pallas kernels, call(): pl.pallas_call(kernel, out_shape=outs, in_specs=[VMEM] * len(operands), o...  45.9 us
    ppermute x6, waiting for transfers between devices, planes(): lax.ppermute(x, 'expert', [(i, i ^ step * along) for i in range(chips)])  30.1 us
    ppermute x12, waiting for transfers between devices, beside(): return lax.ppermute(x, 'expert', [(i, i ^ turn) for i in range(chips)])  26.5 us
    ppermute x3, waiting for transfers between devices, upward(): lax.ppermute(x, 'expert', [(i, (i + along) % chips) for i in range(chips)])  23.7 us
    ppermute x20, starting transfers between devices, across(): return lax.ppermute(x, 'dp', [(i, i ^ 1) for i in range(cores)])  12.5 us
    ppermute x12, starting transfers between devices, beside(): return lax.ppermute(x, 'expert', [(i, i ^ turn) for i in range(chips)])  8.91 us
    unnamed x30, local copies, waits for them, and re-layouts  7.75 us
    ppermute x6, starting transfers between devices, planes(): lax.ppermute(x, 'expert', [(i, i ^ step * along) for i in range(chips)])  6.04 us
  transfers between devices with their start and end apart: 41, of which 15 were waited for; matrix products, arithmetic and copies ran while one was open for 1% of the time, Pallas kernels for 24%

profile of v3, /device:TPU:1, one launch (start us, length us, event | category | flops | bytes accessed | tf_op | source)
XLA Modules:
  0.0 170.8 jit_solution(17430218196313490398)
XLA Ops:
  5.2 2.2 %copy-done = bf16[1024,2048]{1,0:T(8,128)(2,1)S(1)} copy-done((bf16[1024,2048]{1,0:T(8,128)(2,1)S(1)}, bf16[1024,2048]{1,0:T(8,128)(2,1)}, u32[]{:S(2)}) %copy-start) | copy-done | bytes 4194328
  9.7 2.8 %collective-permute-start.3 = (bf16[256,512]{1,0:T(8,128)(2,1)S(1)}, bf16[256,512]{1,0:T(8,128)(2,1)S(1)}, u32[]{:S(2)}, u32[]{:S(2)}) collective-permute-start(bf16[256,512]{1,0:T(8,128)(2,1)S(1)} %shard_map.113.refs_0_), channel_id=1, source_target_pairs={{0,4},{2,6},{4,8},{6,10},{8,12},{10,14},{12,0},{14,2},{1,5},{3,7},... | collective-permute-start | bytes 786440 | tf_op jit(solution)/shard_map/ppermute | solution.py:371
  12.5 8.7 %collective-permute-done.3.refs_2_ = bf16[256,512]{1,0:T(8,128)(2,1)S(1)} collective-permute-done((bf16[256,512]{1,0:T(8,128)(2,1)S(1)}, bf16[256,512]{1,0:T(8,128)(2,1)S(1)}, u32[]{:S(2)}, u32[]{:S(2)}) %collective-permute-start.3) | collective-permute-done | bytes 262176 | tf_op jit(solution)/shard_map/ppermute | solution.py:371
  21.2 9.1 %collective-permute-done.4.refs_1_ = bf16[256,512]{1,0:T(8,128)(2,1)S(1)} collective-permute-done((bf16[256,512]{1,0:T(8,128)(2,1)S(1)}, bf16[256,512]{1,0:T(8,128)(2,1)S(1)}, u32[]{:S(2)}, u32[]{:S(2)}) %collective-permute-start.4) | collective-permute-done | bytes 262176 | tf_op jit(solution)/shard_map/ppermute | solution.py:371
  32.5 6.0 %collective-permute-done.5.refs_1_ = bf16[256,512]{1,0:T(8,128)(2,1)S(1)} collective-permute-done((bf16[256,512]{1,0:T(8,128)(2,1)S(1)}, bf16[256,512]{1,0:T(8,128)(2,1)S(1)}, u32[]{:S(2)}, u32[]{:S(2)}) %collective-permute-start.5) | collective-permute-done | bytes 262176 | tf_op jit(solution)/shard_map/ppermute | solution.py:371
  39.4 3.6 %shard_map.114 = (f32[8,256,128]{2,1,0:T(8,128)S(1)}, f32[8,256,128]{2,1,0:T(8,128)S(1)}, f32[8,256,128]{2,1,0:T(8,128)S(1)}) custom-call(bf16[8,256,128]{2,1,0:T(8,128)(2,1)S(1)} %shard_map.111.query_ref, bf16[256,512]{1,0:T(8,128)(2,1)S(1)} %shard_map.113.refs_0_, bf16[256,512]{1,0:T(8,128)(2,1)S(1)} %collective-permute-done.9.refs_1_, ...), custom_call_target="tpu_custom_call" | custom-call | flops 805306368 | bytes 2097152 | tf_op jit(solution)/shard_map/pallas_call | solution.py:35
  43.1 2.9 %shard_map.115 = (f32[8,256,128]{2,1,0:T(8,128)S(1)}, f32[8,256,128]{2,1,0:T(8,128)S(1)}, f32[8,256,128]{2,1,0:T(8,128)S(1)}) custom-call(bf16[8,256,128]{2,1,0:T(8,128)(2,1)S(1)} %shard_map.111.query_ref, bf16[256,512]{1,0:T(8,128)(2,1)S(1)} %collective-permute-done.8.refs_0_, bf16[256,512]{1,0:T(8,128)(2,1)S(1)} %collective-permute-done.4.refs_1_, ...), custom_call_target="tpu_custom_call" | custom-call | flops 536870912 | bytes 2097152 | tf_op jit(solution)/shard_map/pallas_call | solution.py:35
  47.9 2.9 %shard_map.116 = (f32[8,256,128]{2,1,0:T(8,128)S(1)}, f32[8,256,128]{2,1,0:T(8,128)S(1)}, f32[8,256,128]{2,1,0:T(8,128)S(1)}) custom-call(bf16[8,256,128]{2,1,0:T(8,128)(2,1)S(1)} %shard_map.111.query_ref, bf16[256,512]{1,0:T(8,128)(2,1)S(1)} %collective-permute-done.7.refs_0_, bf16[256,512]{1,0:T(8,128)(2,1)S(1)} %collective-permute-done.5.refs_1_, ...), custom_call_target="tpu_custom_call" | custom-call | flops 536870912 | bytes 2097152 | tf_op jit(solution)/shard_map/pallas_call | solution.py:35
  50.8 2.7 %collective-permute-done.6.refs_0_ = bf16[256,512]{1,0:T(8,128)(2,1)S(1)} collective-permute-done((bf16[256,512]{1,0:T(8,128)(2,1)S(1)}, bf16[256,512]{1,0:T(8,128)(2,1)S(1)}, u32[]{:S(2)}, u32[]{:S(2)}) %collective-permute-start.6) | collective-permute-done | bytes 262176 | tf_op jit(solution)/shard_map/ppermute | solution.py:368
  53.5 3.0 %shard_map.117 = (bf16[128,2048]{1,0:T(8,128)(2,1)S(1)}, f32[128,2048]{1,0:T(8,128)S(1)}) custom-call(bf16[8,256,128]{2,1,0:T(8,128)(2,1)S(1)} %shard_map.111.query_ref, bf16[256,512]{1,0:T(8,128)(2,1)S(1)} %collective-permute-done.6.refs_0_, f32[8,256,128]{2,1,0:T(8,128)S(1)} %get-tuple-element.55.refs_1_, f32[8,256,128]{2,1,0:T(8,128)S(1)} %get-tuple-element.56.refs_2_, ...), custom_call_target="tpu_custom_call" | custom-call | flops 1342177280 | bytes 2097152 | tf_op jit(solution)/shard_map/pallas_call | solution.py:35
  56.5 2.4 %collective-permute-start.10 = (bf16[128,2048]{1,0:T(8,128)(2,1)S(1)}, bf16[128,2048]{1,0:T(8,128)(2,1)S(1)}, u32[]{:S(2)}, u32[]{:S(2)}) collective-permute-start(bf16[128,2048]{1,0:T(8,128)(2,1)S(1)} %get-tuple-element.59), channel_id=1, source_target_pairs={{0,1},{1,0},{2,3},{3,2},{4,5},{5,4},{6,7},{7,6},{8,9},{9,8},{10,11... | collective-permute-start | bytes 1572872 | tf_op jit(solution)/shard_map/ppermute | solution.py:365
  61.7 3.3 %collective-permute-start.33 = (bf16[72,2048]{1,0:T(8,128)(2,1)S(1)}, bf16[72,2048]{1,0:T(8,128)(2,1)S(1)}, u32[]{:S(2)}, u32[]{:S(2)}) collective-permute-start(bf16[72,2048]{1,0:T(8,128)(2,1)S(1)} %get-tuple-element.76), channel_id=1, source_target_pairs={{0,12},{2,14},{4,8},{6,10},{8,4},{10,6},{12,0},{14,2},{1,13},{3,15... | collective-permute-start | bytes 884744 | tf_op jit(solution)/shard_map/ppermute | solution.py:374
  67.6 4.3 %collective-permute-done.33.refs_0_ = bf16[72,2048]{1,0:T(8,128)(2,1)S(1)} collective-permute-done((bf16[72,2048]{1,0:T(8,128)(2,1)S(1)}, bf16[72,2048]{1,0:T(8,128)(2,1)S(1)}, u32[]{:S(2)}, u32[]{:S(2)}) %collective-permute-start.33) | collective-permute-done | bytes 294944 | tf_op jit(solution)/shard_map/ppermute | solution.py:374
  79.0 3.6 %collective-permute-done.25.refs_0_ = bf16[72,2048]{1,0:T(8,128)(2,1)S(1)} collective-permute-done((bf16[72,2048]{1,0:T(8,128)(2,1)S(1)}, bf16[72,2048]{1,0:T(8,128)(2,1)S(1)}, u32[]{:S(2)}, u32[]{:S(2)}) %collective-permute-start.25) | collective-permute-done | bytes 294944 | tf_op jit(solution)/shard_map/ppermute | solution.py:374
  83.1 4.0 %collective-permute-done.17.refs_0_ = bf16[72,2048]{1,0:T(8,128)(2,1)S(1)} collective-permute-done((bf16[72,2048]{1,0:T(8,128)(2,1)S(1)}, bf16[72,2048]{1,0:T(8,128)(2,1)S(1)}, u32[]{:S(2)}, u32[]{:S(2)}) %collective-permute-start.17) | collective-permute-done | bytes 294944 | tf_op jit(solution)/shard_map/ppermute | solution.py:374
  90.5 6.6 %shard_map.119 = (bf16[72,2048]{1,0:T(8,128)(2,1)S(1)}, bf16[72,2048]{1,0:T(8,128)(2,1)S(1)}, bf16[72,2048]{1,0:T(8,128)(2,1)S(1)}, bf16[72,2048]{1,0:T(8,128)(2,1)S(1)}) custom-call(bf16[2048,1792]{1,0:T(8,128)(2,1)S(1)} %fetch.5.gate_ref, bf16[2048,1792]{1,0:T(8,128)(2,1)S(1)} %fetch.6.up_ref, bf16[1792,2048]{1,0:T(8,128)(2,1)S(1)} %fetch.7.down_ref, ...), custom_call_target="tpu_custom_call" | custom-call | flops 6341787648 | bytes 22020096 | tf_op jit(solution)/shard_map/pallas_call | solution.py:35
  98.3 6.6 %shard_map.123 = (bf16[72,2048]{1,0:T(8,128)(2,1)S(1)}, bf16[72,2048]{1,0:T(8,128)(2,1)S(1)}, bf16[72,2048]{1,0:T(8,128)(2,1)S(1)}, bf16[72,2048]{1,0:T(8,128)(2,1)S(1)}) custom-call(bf16[2048,1792]{1,0:T(8,128)(2,1)S(1)} %fetch.5.gate_ref, bf16[2048,1792]{1,0:T(8,128)(2,1)S(1)} %fetch.6.up_ref, bf16[1792,2048]{1,0:T(8,128)(2,1)S(1)} %fetch.7.down_ref, ...), custom_call_target="tpu_custom_call" | custom-call | flops 6341787648 | bytes 22020096 | tf_op jit(solution)/shard_map/pallas_call | solution.py:35
  105.9 6.8 %shard_map.122 = (bf16[72,2048]{1,0:T(8,128)(2,1)S(1)}, bf16[72,2048]{1,0:T(8,128)(2,1)S(1)}, bf16[72,2048]{1,0:T(8,128)(2,1)S(1)}, bf16[72,2048]{1,0:T(8,128)(2,1)S(1)}) custom-call(bf16[2048,1792]{1,0:T(8,128)(2,1)S(1)} %fetch.5.gate_ref, bf16[2048,1792]{1,0:T(8,128)(2,1)S(1)} %fetch.6.up_ref, bf16[1792,2048]{1,0:T(8,128)(2,1)S(1)} %fetch.7.down_ref, ...), custom_call_target="tpu_custom_call" | custom-call | flops 6341787648 | bytes 22020096 | tf_op jit(solution)/shard_map/pallas_call | solution.py:35
  113.4 6.6 %shard_map.120 = (bf16[72,2048]{1,0:T(8,128)(2,1)S(1)}, bf16[72,2048]{1,0:T(8,128)(2,1)S(1)}, bf16[72,2048]{1,0:T(8,128)(2,1)S(1)}, bf16[72,2048]{1,0:T(8,128)(2,1)S(1)}) custom-call(bf16[2048,1792]{1,0:T(8,128)(2,1)S(1)} %fetch.5.gate_ref, bf16[2048,1792]{1,0:T(8,128)(2,1)S(1)} %fetch.6.up_ref, bf16[1792,2048]{1,0:T(8,128)(2,1)S(1)} %fetch.7.down_ref, ...), custom_call_target="tpu_custom_call" | custom-call | flops 6341787648 | bytes 22020096 | tf_op jit(solution)/shard_map/pallas_call | solution.py:35
  123.7 6.7 %collective-permute-done.39 = bf16[72,2048]{1,0:T(8,128)(2,1)S(1)} collective-permute-done((bf16[72,2048]{1,0:T(8,128)(2,1)S(1)}, bf16[72,2048]{1,0:T(8,128)(2,1)S(1)}, u32[]{:S(2)}, u32[]{:S(2)}) %collective-permute-start.39) | collective-permute-done | bytes 294944 | tf_op jit(solution)/shard_map/ppermute | solution.py:368
  132.0 11.0 %collective-permute-done.31 = bf16[72,2048]{1,0:T(8,128)(2,1)S(1)} collective-permute-done((bf16[72,2048]{1,0:T(8,128)(2,1)S(1)}, bf16[72,2048]{1,0:T(8,128)(2,1)S(1)}, u32[]{:S(2)}, u32[]{:S(2)}) %collective-permute-start.31) | collective-permute-done | bytes 294944 | tf_op jit(solution)/shard_map/ppermute | solution.py:368
  143.0 2.2 %collective-permute-start.40 = (bf16[72,2048]{1,0:T(8,128)(2,1)S(1)}, bf16[72,2048]{1,0:T(8,128)(2,1)S(1)}, u32[]{:S(2)}, u32[]{:S(2)}) collective-permute-start(bf16[72,2048]{1,0:T(8,128)(2,1)S(1)} %add_convert_fusion), channel_id=1, source_target_pairs={{0,12},{2,14},{4,8},{6,10},{8,4},{10,6},{12,0},{14,2},{1,13},{3,15... | collective-permute-start | bytes 884744 | tf_op jit(solution)/shard_map/ppermute | solution.py:374
  145.4 3.9 %collective-permute-done.23 = bf16[72,2048]{1,0:T(8,128)(2,1)S(1)} collective-permute-done((bf16[72,2048]{1,0:T(8,128)(2,1)S(1)}, bf16[72,2048]{1,0:T(8,128)(2,1)S(1)}, u32[]{:S(2)}, u32[]{:S(2)}) %collective-permute-start.23) | collective-permute-done | bytes 294944 | tf_op jit(solution)/shard_map/ppermute | solution.py:368
  149.7 18.2 %collective-permute-done.24.refs_1_ = bf16[72,2048]{1,0:T(8,128)(2,1)S(1)} collective-permute-done((bf16[72,2048]{1,0:T(8,128)(2,1)S(1)}, bf16[72,2048]{1,0:T(8,128)(2,1)S(1)}, u32[]{:S(2)}, u32[]{:S(2)}) %collective-permute-start.24) | collective-permute-done | bytes 294944 | tf_op jit(solution)/shard_map/ppermute | solution.py:374
  (123 shorter events, 40.3 us)
Async XLA Ops:
  8.7 30.3 %collective-permute-start.1 = (f32[256,1024]{1,0:T(8,128)S(1)}, f32[256,1024]{1,0:T(8,128)S(1)}, u32[]{:S(2)}, u32[]{:S(2)}) collective-permute-start(f32[256,1024]{1,0:T(8,128)S(1)} %get-tuple-element.46), channel_id=1, source_target_pairs={{0,1},{1,0},{2,3},{3,2},{4,5},{5,4},{6,7},{7,6},{8,9},{9,8},{10,11... | collective-permute-start | bytes 3145736 | tf_op jit(solution)/shard_map/ppermute | solution.py:365
  31.0 12.0 %collective-permute-start.8 = (bf16[256,512]{1,0:T(8,128)(2,1)S(1)}, bf16[256,512]{1,0:T(8,128)(2,1)S(1)}, u32[]{:S(2)}, u32[]{:S(2)}) collective-permute-start(bf16[256,512]{1,0:T(8,128)(2,1)S(1)} %collective-permute-done.3.refs_2_), channel_id=1, source_target_pairs={{0,2},{2,0},{4,6},{6,4},{8,10},{10,8},{12,14},{14,12},{1,3},{3,1},... | collective-permute-start | bytes 786440 | tf_op jit(solution)/shard_map/ppermute | solution.py:368
  31.7 16.2 %collective-permute-start.7 = (bf16[256,512]{1,0:T(8,128)(2,1)S(1)}, bf16[256,512]{1,0:T(8,128)(2,1)S(1)}, u32[]{:S(2)}, u32[]{:S(2)}) collective-permute-start(bf16[256,512]{1,0:T(8,128)(2,1)S(1)} %collective-permute-done.4.refs_1_), channel_id=1, source_target_pairs={{0,2},{2,0},{4,6},{6,4},{8,10},{10,8},{12,14},{14,12},{1,3},{3,1},... | collective-permute-start | bytes 786440 | tf_op jit(solution)/shard_map/ppermute | solution.py:368
  38.5 15.1 %collective-permute-start.6 = (bf16[256,512]{1,0:T(8,128)(2,1)S(1)}, bf16[256,512]{1,0:T(8,128)(2,1)S(1)}, u32[]{:S(2)}, u32[]{:S(2)}) collective-permute-start(bf16[256,512]{1,0:T(8,128)(2,1)S(1)} %collective-permute-done.5.refs_1_), channel_id=1, source_target_pairs={{0,2},{2,0},{4,6},{6,4},{8,10},{10,8},{12,14},{14,12},{1,3},{3,1},... | collective-permute-start | bytes 786440 | tf_op jit(solution)/shard_map/ppermute | solution.py:368
  65.8 16.9 %collective-permute-start.25 = (bf16[72,2048]{1,0:T(8,128)(2,1)S(1)}, bf16[72,2048]{1,0:T(8,128)(2,1)S(1)}, u32[]{:S(2)}, u32[]{:S(2)}) collective-permute-start(bf16[72,2048]{1,0:T(8,128)(2,1)S(1)} %get-tuple-element.71), channel_id=1, source_target_pairs={{0,4},{2,6},{4,0},{6,2},{8,12},{10,14},{12,8},{14,10},{1,5},{3,7},... | collective-permute-start | bytes 884744 | tf_op jit(solution)/shard_map/ppermute | solution.py:374
  65.8 21.3 %collective-permute-start.17 = (bf16[72,2048]{1,0:T(8,128)(2,1)S(1)}, bf16[72,2048]{1,0:T(8,128)(2,1)S(1)}, u32[]{:S(2)}, u32[]{:S(2)}) collective-permute-start(bf16[72,2048]{1,0:T(8,128)(2,1)S(1)} %get-tuple-element.66), channel_id=1, source_target_pairs={{0,8},{2,10},{4,12},{6,14},{8,0},{10,2},{12,4},{14,6},{1,9},{3,11}... | collective-permute-start | bytes 884744 | tf_op jit(solution)/shard_map/ppermute | solution.py:374
  66.2 22.1 %collective-permute-start.12 = (bf16[72,2048]{1,0:T(8,128)(2,1)S(1)}, bf16[72,2048]{1,0:T(8,128)(2,1)S(1)}, u32[]{:S(2)}, u32[]{:S(2)}) collective-permute-start(bf16[72,2048]{1,0:T(8,128)(2,1)S(1)} %get-tuple-element.61.refs_0_), channel_id=1, source_target_pairs={{0,1},{1,0},{2,3},{3,2},{4,5},{5,4},{6,7},{7,6},{8,9},{9,8},{10,11... | collective-permute-start | bytes 884744 | tf_op jit(solution)/shard_map/ppermute | solution.py:365
  71.8 18.0 %collective-permute-start.34 = (bf16[72,2048]{1,0:T(8,128)(2,1)S(1)}, bf16[72,2048]{1,0:T(8,128)(2,1)S(1)}, u32[]{:S(2)}, u32[]{:S(2)}) collective-permute-start(bf16[72,2048]{1,0:T(8,128)(2,1)S(1)} %collective-permute-done.33.refs_0_), channel_id=1, source_target_pairs={{0,2},{2,0},{4,6},{6,4},{8,10},{10,8},{12,14},{14,12},{1,3},{3,1},... | collective-permute-start | bytes 884744 | tf_op jit(solution)/shard_map/ppermute | solution.py:368
  72.9 17.2 %collective-permute-start.13 = (bf16[72,2048]{1,0:T(8,128)(2,1)S(1)}, bf16[72,2048]{1,0:T(8,128)(2,1)S(1)}, u32[]{:S(2)}, u32[]{:S(2)}) collective-permute-start(bf16[72,2048]{1,0:T(8,128)(2,1)S(1)} %collective-permute-done.11.refs_1_), channel_id=1, source_target_pairs={{0,1},{1,0},{2,3},{3,2},{4,5},{5,4},{6,7},{7,6},{8,9},{9,8},{10,11... | collective-permute-start | bytes 884744 | tf_op jit(solution)/shard_map/ppermute | solution.py:365
  82.7 14.4 %collective-permute-start.35 = (bf16[72,2048]{1,0:T(8,128)(2,1)S(1)}, bf16[72,2048]{1,0:T(8,128)(2,1)S(1)}, u32[]{:S(2)}, u32[]{:S(2)}) collective-permute-start(bf16[72,2048]{1,0:T(8,128)(2,1)S(1)} %collective-permute-done.33.refs_0_), channel_id=1, source_target_pairs={{0,1},{1,0},{2,3},{3,2},{4,5},{5,4},{6,7},{7,6},{8,9},{9,8},{10,11... | collective-permute-start | bytes 884744 | tf_op jit(solution)/shard_map/ppermute | solution.py:365
  88.3 16.6 %collective-permute-start.27 = (bf16[72,2048]{1,0:T(8,128)(2,1)S(1)}, bf16[72,2048]{1,0:T(8,128)(2,1)S(1)}, u32[]{:S(2)}, u32[]{:S(2)}) collective-permute-start(bf16[72,2048]{1,0:T(8,128)(2,1)S(1)} %collective-permute-done.25.refs_0_), channel_id=1, source_target_pairs={{0,1},{1,0},{2,3},{3,2},{4,5},{5,4},{6,7},{7,6},{8,9},{9,8},{10,11... | collective-permute-start | bytes 884744 | tf_op jit(solution)/shard_map/ppermute | solution.py:365
  89.8 15.6 %collective-permute-start.18 = (bf16[72,2048]{1,0:T(8,128)(2,1)S(1)}, bf16[72,2048]{1,0:T(8,128)(2,1)S(1)}, u32[]{:S(2)}, u32[]{:S(2)}) collective-permute-start(bf16[72,2048]{1,0:T(8,128)(2,1)S(1)} %collective-permute-done.17.refs_0_), channel_id=1, source_target_pairs={{0,2},{2,0},{4,6},{6,4},{8,10},{10,8},{12,14},{14,12},{1,3},{3,1},... | collective-permute-start | bytes 884744 | tf_op jit(solution)/shard_map/ppermute | solution.py:368
  97.1 15.7 %collective-permute-start.19 = (bf16[72,2048]{1,0:T(8,128)(2,1)S(1)}, bf16[72,2048]{1,0:T(8,128)(2,1)S(1)}, u32[]{:S(2)}, u32[]{:S(2)}) collective-permute-start(bf16[72,2048]{1,0:T(8,128)(2,1)S(1)} %collective-permute-done.17.refs_0_), channel_id=1, source_target_pairs={{0,1},{1,0},{2,3},{3,2},{4,5},{5,4},{6,7},{7,6},{8,9},{9,8},{10,11... | collective-permute-start | bytes 884744 | tf_op jit(solution)/shard_map/ppermute | solution.py:365
  97.3 22.7 %collective-permute-start.15 = (bf16[72,2048]{1,0:T(8,128)(2,1)S(1)}, bf16[72,2048]{1,0:T(8,128)(2,1)S(1)}, u32[]{:S(2)}, u32[]{:S(2)}) collective-permute-start(bf16[72,2048]{1,0:T(8,128)(2,1)S(1)} %get-tuple-element.65), channel_id=1, source_target_pairs={{0,1},{1,0},{2,3},{3,2},{4,5},{5,4},{6,7},{7,6},{8,9},{9,8},{10,11... | collective-permute-start | bytes 884744 | tf_op jit(solution)/shard_map/ppermute | solution.py:365
  104.9 44.7 %collective-permute-start.14 = (bf16[72,2048]{1,0:T(8,128)(2,1)S(1)}, bf16[72,2048]{1,0:T(8,128)(2,1)S(1)}, u32[]{:S(2)}, u32[]{:S(2)}) collective-permute-start(bf16[72,2048]{1,0:T(8,128)(2,1)S(1)} %get-tuple-element.63), channel_id=1, source_target_pairs={{0,1},{1,0},{2,3},{3,2},{4,5},{5,4},{6,7},{7,6},{8,9},{9,8},{10,11... | collective-permute-start | bytes 884744 | tf_op jit(solution)/shard_map/ppermute | solution.py:365
  105.5 14.7 %collective-permute-start.38 = (bf16[72,2048]{1,0:T(8,128)(2,1)S(1)}, bf16[72,2048]{1,0:T(8,128)(2,1)S(1)}, u32[]{:S(2)}, u32[]{:S(2)}) collective-permute-start(bf16[72,2048]{1,0:T(8,128)(2,1)S(1)} %get-tuple-element.80), channel_id=1, source_target_pairs={{0,1},{1,0},{2,3},{3,2},{4,5},{5,4},{6,7},{7,6},{8,9},{9,8},{10,11... | collective-permute-start | bytes 884744 | tf_op jit(solution)/shard_map/ppermute | solution.py:365
  120.0 11.7 %collective-permute-start.29 = (bf16[72,2048]{1,0:T(8,128)(2,1)S(1)}, bf16[72,2048]{1,0:T(8,128)(2,1)S(1)}, u32[]{:S(2)}, u32[]{:S(2)}) collective-permute-start(bf16[72,2048]{1,0:T(8,128)(2,1)S(1)} %get-tuple-element.73), channel_id=1, source_target_pairs={{0,1},{1,0},{2,3},{3,2},{4,5},{5,4},{6,7},{7,6},{8,9},{9,8},{10,11... | collective-permute-start | bytes 884744 | tf_op jit(solution)/shard_map/ppermute | solution.py:365
  120.8 24.6 %collective-permute-start.21 = (bf16[72,2048]{1,0:T(8,128)(2,1)S(1)}, bf16[72,2048]{1,0:T(8,128)(2,1)S(1)}, u32[]{:S(2)}, u32[]{:S(2)}) collective-permute-start(bf16[72,2048]{1,0:T(8,128)(2,1)S(1)} %get-tuple-element.68), channel_id=1, source_target_pairs={{0,1},{1,0},{2,3},{3,2},{4,5},{5,4},{6,7},{7,6},{8,9},{9,8},{10,11... | collective-permute-start | bytes 884744 | tf_op jit(solution)/shard_map/ppermute | solution.py:365
  123.3 26.3 %collective-permute-start.16 = (bf16[72,2048]{1,0:T(8,128)(2,1)S(1)}, bf16[72,2048]{1,0:T(8,128)(2,1)S(1)}, u32[]{:S(2)}, u32[]{:S(2)}) collective-permute-start(bf16[72,2048]{1,0:T(8,128)(2,1)S(1)} %add_convert_fusion.10), channel_id=1, source_target_pairs={{0,2},{2,0},{4,6},{6,4},{8,10},{10,8},{12,14},{14,12},{1,3},{3,1},... | collective-permute-start | bytes 884744 | tf_op jit(solution)/shard_map/ppermute | solution.py:368
  130.4 12.6 %collective-permute-start.31 = (bf16[72,2048]{1,0:T(8,128)(2,1)S(1)}, bf16[72,2048]{1,0:T(8,128)(2,1)S(1)}, u32[]{:S(2)}, u32[]{:S(2)}) collective-permute-start(bf16[72,2048]{1,0:T(8,128)(2,1)S(1)} %add_convert_fusion.4), channel_id=1, source_target_pairs={{0,2},{2,0},{4,6},{6,4},{8,10},{10,8},{12,14},{14,12},{1,3},{3,1},... | collective-permute-start | bytes 884744 | tf_op jit(solution)/shard_map/ppermute | solution.py:368
  131.6 17.7 %collective-permute-start.23 = (bf16[72,2048]{1,0:T(8,128)(2,1)S(1)}, bf16[72,2048]{1,0:T(8,128)(2,1)S(1)}, u32[]{:S(2)}, u32[]{:S(2)}) collective-permute-start(bf16[72,2048]{1,0:T(8,128)(2,1)S(1)} %add_convert_fusion.7), channel_id=1, source_target_pairs={{0,2},{2,0},{4,6},{6,4},{8,10},{10,8},{12,14},{14,12},{1,3},{3,1},... | collective-permute-start | bytes 884744 | tf_op jit(solution)/shard_map/ppermute | solution.py:368
  143.0 25.9 %collective-permute-start.40 = (bf16[72,2048]{1,0:T(8,128)(2,1)S(1)}, bf16[72,2048]{1,0:T(8,128)(2,1)S(1)}, u32[]{:S(2)}, u32[]{:S(2)}) collective-permute-start(bf16[72,2048]{1,0:T(8,128)(2,1)S(1)} %add_convert_fusion), channel_id=1, source_target_pairs={{0,12},{2,14},{4,8},{6,10},{8,4},{10,6},{12,0},{14,2},{1,13},{3,15... | collective-permute-start | bytes 884744 | tf_op jit(solution)/shard_map/ppermute | solution.py:374
  145.3 23.6 %collective-permute-start.32 = (bf16[72,2048]{1,0:T(8,128)(2,1)S(1)}, bf16[72,2048]{1,0:T(8,128)(2,1)S(1)}, u32[]{:S(2)}, u32[]{:S(2)}) collective-permute-start(bf16[72,2048]{1,0:T(8,128)(2,1)S(1)} %add_convert_fusion.3), channel_id=1, source_target_pairs={{0,4},{2,6},{4,0},{6,2},{8,12},{10,14},{12,8},{14,10},{1,5},{3,7},... | collective-permute-start | bytes 884744 | tf_op jit(solution)/shard_map/ppermute | solution.py:374
  149.5 18.4 %collective-permute-start.24 = (bf16[72,2048]{1,0:T(8,128)(2,1)S(1)}, bf16[72,2048]{1,0:T(8,128)(2,1)S(1)}, u32[]{:S(2)}, u32[]{:S(2)}) collective-permute-start(bf16[72,2048]{1,0:T(8,128)(2,1)S(1)} %add_convert_fusion.6), channel_id=1, source_target_pairs={{0,8},{2,10},{4,12},{6,14},{8,0},{10,2},{12,4},{14,6},{1,9},{3,11}... | collective-permute-start | bytes 884744 | tf_op jit(solution)/shard_map/ppermute | solution.py:374
  (32 other events, 352.2 us)

commit v4 on v3

--- a/solution.py
+++ b/solution.py
@@ -16,7 +16,7 @@
 
 HIDDEN_STEP = 256
 DOWN_STEP = 256
-ORDER = (0, 1, 2, 3)
+ORDER = (0, 2, 3, 1)
 
 epsilon = 1e-05
 base_theta = 1000000.0
@@ -317,18 +317,38 @@
     )
 
 
-def combine_kernel(along, steps, base_ref, choice_ref, weight_ref, *refs):
-    row_refs, out_ref = refs[:-1], refs[-1]
+def early_kernel(along, early, late, base_ref, choice_ref, weight_ref, *refs):
+    refs = list(refs)
+    row_refs = [refs.pop(0) for _ in early]
+    out_ref = refs.pop(0)
     plane = lax.axis_index("expert") // along
     choice = as_columns(choice_ref).astype(jnp.int32)
     weights = as_columns(weight_ref)
     total = base_ref[...].astype(f32)
     routings = placed(choice, plane)
-    for step, row_ref in zip(steps, row_refs):
-        expert = plane ^ step
-        weight = jnp.sum(jnp.where(choice == expert, weights, 0.0), axis=1, keepdims=True)
-        total = total + weight * dot(routings[step], row_ref[...])
-    out_ref[...] = total.astype(out_ref.dtype)
+
+    def weight(step):
+        return jnp.sum(jnp.where(choice == (plane ^ step), weights, 0.0), axis=1, keepdims=True)
+
+    for step, row_ref in zip(early, row_refs):
+        total = total + weight(step) * dot(routings[step], row_ref[...])
+    out_ref[...] = total
+    for index, step in enumerate(late):
+        refs[2 * index][...] = routings[step]
+        refs[2 * index + 1][...] = jnp.broadcast_to(weight(step), refs[2 * index + 1].shape)
+
+
+def late_kernel(base_ref, *refs):
+    total_ref, out_ref = base_ref, refs[-1]
+    width = 128
+    for start in range(0, out_ref.shape[1], 4 * width):
+        columns = slice(start, start + 4 * width)
+        total = total_ref[:, columns]
+        for index in range(0, len(refs) - 1, 3):
+            routing_ref, weight_ref, row_ref = refs[index : index + 3]
+            weight = jnp.concatenate([weight_ref[...]] * 4, axis=1)
+            total = total + weight * dot(routing_ref[...], row_ref[:, columns])
+        out_ref[:, columns] = total.astype(out_ref.dtype)
 
 
 def add(*terms):
@@ -429,7 +449,7 @@
     line = keyval
     for back in range(EXPERTS):
         if back:
-            line = upward(line)
+            line = planes(line, 1) if back == EXPERTS - 1 else upward(line)
         part.append((line, (back, 0)))
         if back:
             parts.append(part)
@@ -488,19 +508,31 @@
         others = [beside(near[turn], turn) for turn in range(1, along)]
         reduced = add(near[0], *others)
         collected[step] = planes(reduced, step) if step else reduced
-
-    def combined(base, steps, kind):
-        return call(
-            functools.partial(combine_kernel, along, steps),
-            shape((local_rows, model_width), kind),
-            (base, expert_choice.T, gate_weights.T, *[collected[step] for step in steps]),
-            flops=2 * len(steps) * ROWS * local_rows * model_width,
-            moved=8 * local_rows * model_width,
-        )
-
     a, b, c, d = ORDER
-    early = combined(residual, (a, c), f32)
-    return combined(early, (b, d), bf16)
+    early, late = (a, b), (c, d)
+    prepared = [shape((local_rows, ROWS), bf16), shape((local_rows, 128), f32)] * len(late)
+    total, *prepared = call(
+        functools.partial(early_kernel, along, early, late),
+        [shape((local_rows, model_width), f32), *prepared],
+        (
+            residual,
+            expert_choice.T,
+            gate_weights.T,
+            *[collected[step] for step in early],
+        ),
+        flops=2 * len(early) * ROWS * local_rows * model_width,
+        moved=8 * local_rows * model_width,
+    )
+    operands = [total]
+    for index, step in enumerate(late):
+        operands += [*prepared[2 * index : 2 * index + 2], collected[step]]
+    return call(
+        late_kernel,
+        shape((local_rows, model_width), bf16),
+        operands,
+        flops=2 * len(late) * ROWS * local_rows * model_width,
+        moved=8 * local_rows * model_width,
+    )
 
 
 def solution(mesh):

time: 174 us -> 179 us (1.029)
  waiting for transfers between devices: 82.9 us -> 86.1 us
  starting transfers between devices: 30.3 us -> 33.4 us
    ppermute x6 -> x7, waiting for transfers between devices: 30.1 us -> 36.6 us  [planes(): lax.ppermute(x, 'expert', [(i, i ^ step * along) for i in range(chips)])]
    ppermute x3 -> x2, waiting for transfers between devices: 23.7 us -> 17.8 us  [upward(): lax.ppermute(x, 'expert', [(i, (i + along) % chips) for i in range(chips)])]
    ppermute x20, starting transfers between devices: 12.5 us -> 17.8 us  [across(): return lax.ppermute(x, 'dp', [(i, i ^ 1) for i in range(cores)])]
    ppermute x12, waiting for transfers between devices: 26.5 us -> 29.1 us  [beside(): return lax.ppermute(x, 'expert', [(i, i ^ turn) for i in range(chips)])]
    ppermute x6 -> x7, starting transfers between devices: 6.04 us -> 3.88 us  [planes(): lax.ppermute(x, 'expert', [(i, i ^ step * along) for i in range(chips)])]
  transfers between devices with their start and end apart: 41 -> 41, of which waited for: 15 -> 14; matrix products, arithmetic and copies ran while one was open for 1% -> 1% of each run, Pallas kernels for 24% -> 23%
where the time goes in v4:
time: 179 us; the launch traced here: 176 us
  waiting for transfers between devices  86.1 us (48%)
  Pallas kernels  47.3 us (26%)
  starting transfers between devices  33.4 us (19%)
  local copies, waits for them, and re-layouts  7.75 us (4%)
    pallas_call x16, Pallas kernels, call(): pl.pallas_call(kernel, out_shape=outs, in_specs=[VMEM] * len(operands), o...  45.3 us
    ppermute x7, waiting for transfers between devices, planes(): lax.ppermute(x, 'expert', [(i, i ^ step * along) for i in range(chips)])  36.6 us
    ppermute x12, waiting for transfers between devices, beside(): return lax.ppermute(x, 'expert', [(i, i ^ turn) for i in range(chips)])  29.1 us
    ppermute x20, starting transfers between devices, across(): return lax.ppermute(x, 'dp', [(i, i ^ 1) for i in range(cores)])  17.8 us
    ppermute x2, waiting for transfers between devices, upward(): lax.ppermute(x, 'expert', [(i, (i + along) % chips) for i in range(chips)])  17.8 us
    ppermute x12, starting transfers between devices, beside(): return lax.ppermute(x, 'expert', [(i, i ^ turn) for i in range(chips)])  8.94 us
    unnamed x30, local copies, waits for them, and re-layouts  7.75 us
    ppermute x7, starting transfers between devices, planes(): lax.ppermute(x, 'expert', [(i, i ^ step * along) for i in range(chips)])  3.88 us
  transfers between devices with their start and end apart: 41, of which 14 were waited for; matrix products, arithmetic and copies ran while one was open for 1% of the time, Pallas kernels for 23%

profile of v4, /device:TPU:1, one launch (start us, length us, event | category | flops | bytes accessed | tf_op | source)
XLA Modules:
  0.0 176.4 jit_solution(13886699800611768728)
XLA Ops:
  5.2 2.2 %copy-done = bf16[1024,2048]{1,0:T(8,128)(2,1)S(1)} copy-done((bf16[1024,2048]{1,0:T(8,128)(2,1)S(1)}, bf16[1024,2048]{1,0:T(8,128)(2,1)}, u32[]{:S(2)}) %copy-start) | copy-done | bytes 4194328
  9.7 2.8 %collective-permute-start.3 = (bf16[256,512]{1,0:T(8,128)(2,1)S(1)}, bf16[256,512]{1,0:T(8,128)(2,1)S(1)}, u32[]{:S(2)}, u32[]{:S(2)}) collective-permute-start(bf16[256,512]{1,0:T(8,128)(2,1)S(1)} %shard_map.113.refs_0_), channel_id=1, source_target_pairs={{0,4},{2,6},{4,8},{6,10},{8,12},{10,14},{12,0},{14,2},{1,5},{3,7},... | collective-permute-start | bytes 786440 | tf_op jit(solution)/shard_map/ppermute | solution.py:391
  12.5 8.7 %collective-permute-done.3.refs_2_ = bf16[256,512]{1,0:T(8,128)(2,1)S(1)} collective-permute-done((bf16[256,512]{1,0:T(8,128)(2,1)S(1)}, bf16[256,512]{1,0:T(8,128)(2,1)S(1)}, u32[]{:S(2)}, u32[]{:S(2)}) %collective-permute-start.3) | collective-permute-done | bytes 262176 | tf_op jit(solution)/shard_map/ppermute | solution.py:391
  21.2 9.1 %collective-permute-done.4.refs_1_ = bf16[256,512]{1,0:T(8,128)(2,1)S(1)} collective-permute-done((bf16[256,512]{1,0:T(8,128)(2,1)S(1)}, bf16[256,512]{1,0:T(8,128)(2,1)S(1)}, u32[]{:S(2)}, u32[]{:S(2)}) %collective-permute-start.4) | collective-permute-done | bytes 262176 | tf_op jit(solution)/shard_map/ppermute | solution.py:391
  32.5 3.6 %collective-permute-done.5.refs_1_ = bf16[256,512]{1,0:T(8,128)(2,1)S(1)} collective-permute-done((bf16[256,512]{1,0:T(8,128)(2,1)S(1)}, bf16[256,512]{1,0:T(8,128)(2,1)S(1)}, u32[]{:S(2)}, u32[]{:S(2)}) %collective-permute-start.5) | collective-permute-done | bytes 262176 | tf_op jit(solution)/shard_map/ppermute | solution.py:394
  37.3 3.6 %shard_map.114 = (f32[8,256,128]{2,1,0:T(8,128)S(1)}, f32[8,256,128]{2,1,0:T(8,128)S(1)}, f32[8,256,128]{2,1,0:T(8,128)S(1)}) custom-call(bf16[8,256,128]{2,1,0:T(8,128)(2,1)S(1)} %shard_map.111.query_ref, bf16[256,512]{1,0:T(8,128)(2,1)S(1)} %shard_map.113.refs_0_, bf16[256,512]{1,0:T(8,128)(2,1)S(1)} %collective-permute-done.9.refs_1_, ...), custom_call_target="tpu_custom_call" | custom-call | flops 805306368 | bytes 2097152 | tf_op jit(solution)/shard_map/pallas_call | solution.py:35
  41.8 2.9 %shard_map.115 = (f32[8,256,128]{2,1,0:T(8,128)S(1)}, f32[8,256,128]{2,1,0:T(8,128)S(1)}, f32[8,256,128]{2,1,0:T(8,128)S(1)}) custom-call(bf16[8,256,128]{2,1,0:T(8,128)(2,1)S(1)} %shard_map.111.query_ref, bf16[256,512]{1,0:T(8,128)(2,1)S(1)} %collective-permute-done.8.refs_0_, bf16[256,512]{1,0:T(8,128)(2,1)S(1)} %collective-permute-done.4.refs_1_, ...), custom_call_target="tpu_custom_call" | custom-call | flops 536870912 | bytes 2097152 | tf_op jit(solution)/shard_map/pallas_call | solution.py:35
  44.7 2.7 %collective-permute-done.7.refs_0_ = bf16[256,512]{1,0:T(8,128)(2,1)S(1)} collective-permute-done((bf16[256,512]{1,0:T(8,128)(2,1)S(1)}, bf16[256,512]{1,0:T(8,128)(2,1)S(1)}, u32[]{:S(2)}, u32[]{:S(2)}) %collective-permute-start.7) | collective-permute-done | bytes 262176 | tf_op jit(solution)/shard_map/ppermute | solution.py:388
  47.4 2.9 %shard_map.116 = (f32[8,256,128]{2,1,0:T(8,128)S(1)}, f32[8,256,128]{2,1,0:T(8,128)S(1)}, f32[8,256,128]{2,1,0:T(8,128)S(1)}) custom-call(bf16[8,256,128]{2,1,0:T(8,128)(2,1)S(1)} %shard_map.111.query_ref, bf16[256,512]{1,0:T(8,128)(2,1)S(1)} %collective-permute-done.7.refs_0_, bf16[256,512]{1,0:T(8,128)(2,1)S(1)} %collective-permute-done.5.refs_1_, ...), custom_call_target="tpu_custom_call" | custom-call | flops 536870912 | bytes 2097152 | tf_op jit(solution)/shard_map/pallas_call | solution.py:35
  50.3 2.7 %collective-permute-done.6.refs_0_ = bf16[256,512]{1,0:T(8,128)(2,1)S(1)} collective-permute-done((bf16[256,512]{1,0:T(8,128)(2,1)S(1)}, bf16[256,512]{1,0:T(8,128)(2,1)S(1)}, u32[]{:S(2)}, u32[]{:S(2)}) %collective-permute-start.6) | collective-permute-done | bytes 262176 | tf_op jit(solution)/shard_map/ppermute | solution.py:388
  53.0 3.0 %shard_map.117 = (bf16[128,2048]{1,0:T(8,128)(2,1)S(1)}, f32[128,2048]{1,0:T(8,128)S(1)}) custom-call(bf16[8,256,128]{2,1,0:T(8,128)(2,1)S(1)} %shard_map.111.query_ref, bf16[256,512]{1,0:T(8,128)(2,1)S(1)} %collective-permute-done.6.refs_0_, f32[8,256,128]{2,1,0:T(8,128)S(1)} %get-tuple-element.60.refs_1_, f32[8,256,128]{2,1,0:T(8,128)S(1)} %get-tuple-element.61.refs_2_, ...), custom_call_target="tpu_custom_call" | custom-call | flops 1342177280 | bytes 2097152 | tf_op jit(solution)/shard_map/pallas_call | solution.py:35
  56.0 2.9 %collective-permute-start.10 = (bf16[128,2048]{1,0:T(8,128)(2,1)S(1)}, bf16[128,2048]{1,0:T(8,128)(2,1)S(1)}, u32[]{:S(2)}, u32[]{:S(2)}) collective-permute-start(bf16[128,2048]{1,0:T(8,128)(2,1)S(1)} %get-tuple-element.64), channel_id=1, source_target_pairs={{0,1},{1,0},{2,3},{3,2},{4,5},{5,4},{6,7},{7,6},{8,9},{9,8},{10,11... | collective-permute-start | bytes 1572872 | tf_op jit(solution)/shard_map/ppermute | solution.py:385
  66.7 4.1 %collective-permute-done.33.refs_0_ = bf16[72,2048]{1,0:T(8,128)(2,1)S(1)} collective-permute-done((bf16[72,2048]{1,0:T(8,128)(2,1)S(1)}, bf16[72,2048]{1,0:T(8,128)(2,1)S(1)}, u32[]{:S(2)}, u32[]{:S(2)}) %collective-permute-start.33) | collective-permute-done | bytes 294944 | tf_op jit(solution)/shard_map/ppermute | solution.py:394
  71.4 6.8 %collective-permute-start.13 = (bf16[72,2048]{1,0:T(8,128)(2,1)S(1)}, bf16[72,2048]{1,0:T(8,128)(2,1)S(1)}, u32[]{:S(2)}, u32[]{:S(2)}) collective-permute-start(bf16[72,2048]{1,0:T(8,128)(2,1)S(1)} %collective-permute-done.11.refs_1_), channel_id=1, source_target_pairs={{0,1},{1,0},{2,3},{3,2},{4,5},{5,4},{6,7},{7,6},{8,9},{9,8},{10,11... | collective-permute-start | bytes 884744 | tf_op jit(solution)/shard_map/ppermute | solution.py:385
  82.3 8.2 %collective-permute-done.17.refs_0_ = bf16[72,2048]{1,0:T(8,128)(2,1)S(1)} collective-permute-done((bf16[72,2048]{1,0:T(8,128)(2,1)S(1)}, bf16[72,2048]{1,0:T(8,128)(2,1)S(1)}, u32[]{:S(2)}, u32[]{:S(2)}) %collective-permute-start.17) | collective-permute-done | bytes 294944 | tf_op jit(solution)/shard_map/ppermute | solution.py:394
  91.2 2.0 %collective-permute-start.27 = (bf16[72,2048]{1,0:T(8,128)(2,1)S(1)}, bf16[72,2048]{1,0:T(8,128)(2,1)S(1)}, u32[]{:S(2)}, u32[]{:S(2)}) collective-permute-start(bf16[72,2048]{1,0:T(8,128)(2,1)S(1)} %collective-permute-done.25.refs_0_), channel_id=1, source_target_pairs={{0,1},{1,0},{2,3},{3,2},{4,5},{5,4},{6,7},{7,6},{8,9},{9,8},{10,11... | collective-permute-start | bytes 884744 | tf_op jit(solution)/shard_map/ppermute | solution.py:385
  94.3 6.6 %shard_map.119 = (bf16[72,2048]{1,0:T(8,128)(2,1)S(1)}, bf16[72,2048]{1,0:T(8,128)(2,1)S(1)}, bf16[72,2048]{1,0:T(8,128)(2,1)S(1)}, bf16[72,2048]{1,0:T(8,128)(2,1)S(1)}) custom-call(bf16[2048,1792]{1,0:T(8,128)(2,1)S(1)} %fetch.5.gate_ref, bf16[2048,1792]{1,0:T(8,128)(2,1)S(1)} %fetch.6.up_ref, bf16[1792,2048]{1,0:T(8,128)(2,1)S(1)} %fetch.7.down_ref, ...), custom_call_target="tpu_custom_call" | custom-call | flops 6341787648 | bytes 22020096 | tf_op jit(solution)/shard_map/pallas_call | solution.py:35
  102.1 6.6 %shard_map.123 = (bf16[72,2048]{1,0:T(8,128)(2,1)S(1)}, bf16[72,2048]{1,0:T(8,128)(2,1)S(1)}, bf16[72,2048]{1,0:T(8,128)(2,1)S(1)}, bf16[72,2048]{1,0:T(8,128)(2,1)S(1)}) custom-call(bf16[2048,1792]{1,0:T(8,128)(2,1)S(1)} %fetch.5.gate_ref, bf16[2048,1792]{1,0:T(8,128)(2,1)S(1)} %fetch.6.up_ref, bf16[1792,2048]{1,0:T(8,128)(2,1)S(1)} %fetch.7.down_ref, ...), custom_call_target="tpu_custom_call" | custom-call | flops 6341787648 | bytes 22020096 | tf_op jit(solution)/shard_map/pallas_call | solution.py:35
  109.8 6.8 %shard_map.122 = (bf16[72,2048]{1,0:T(8,128)(2,1)S(1)}, bf16[72,2048]{1,0:T(8,128)(2,1)S(1)}, bf16[72,2048]{1,0:T(8,128)(2,1)S(1)}, bf16[72,2048]{1,0:T(8,128)(2,1)S(1)}) custom-call(bf16[2048,1792]{1,0:T(8,128)(2,1)S(1)} %fetch.5.gate_ref, bf16[2048,1792]{1,0:T(8,128)(2,1)S(1)} %fetch.6.up_ref, bf16[1792,2048]{1,0:T(8,128)(2,1)S(1)} %fetch.7.down_ref, ...), custom_call_target="tpu_custom_call" | custom-call | flops 6341787648 | bytes 22020096 | tf_op jit(solution)/shard_map/pallas_call | solution.py:35
  117.2 6.6 %shard_map.120 = (bf16[72,2048]{1,0:T(8,128)(2,1)S(1)}, bf16[72,2048]{1,0:T(8,128)(2,1)S(1)}, bf16[72,2048]{1,0:T(8,128)(2,1)S(1)}, bf16[72,2048]{1,0:T(8,128)(2,1)S(1)}) custom-call(bf16[2048,1792]{1,0:T(8,128)(2,1)S(1)} %fetch.5.gate_ref, bf16[2048,1792]{1,0:T(8,128)(2,1)S(1)} %fetch.6.up_ref, bf16[1792,2048]{1,0:T(8,128)(2,1)S(1)} %fetch.7.down_ref, ...), custom_call_target="tpu_custom_call" | custom-call | flops 6341787648 | bytes 22020096 | tf_op jit(solution)/shard_map/pallas_call | solution.py:35
  127.5 6.7 %collective-permute-done.39 = bf16[72,2048]{1,0:T(8,128)(2,1)S(1)} collective-permute-done((bf16[72,2048]{1,0:T(8,128)(2,1)S(1)}, bf16[72,2048]{1,0:T(8,128)(2,1)S(1)}, u32[]{:S(2)}, u32[]{:S(2)}) %collective-permute-start.39) | collective-permute-done | bytes 294944 | tf_op jit(solution)/shard_map/ppermute | solution.py:388
  135.9 11.0 %collective-permute-done.31 = bf16[72,2048]{1,0:T(8,128)(2,1)S(1)} collective-permute-done((bf16[72,2048]{1,0:T(8,128)(2,1)S(1)}, bf16[72,2048]{1,0:T(8,128)(2,1)S(1)}, u32[]{:S(2)}, u32[]{:S(2)}) %collective-permute-start.31) | collective-permute-done | bytes 294944 | tf_op jit(solution)/shard_map/ppermute | solution.py:388
  147.9 5.2 %collective-permute-done.23 = bf16[72,2048]{1,0:T(8,128)(2,1)S(1)} collective-permute-done((bf16[72,2048]{1,0:T(8,128)(2,1)S(1)}, bf16[72,2048]{1,0:T(8,128)(2,1)S(1)}, u32[]{:S(2)}, u32[]{:S(2)}) %collective-permute-start.23) | collective-permute-done | bytes 294944 | tf_op jit(solution)/shard_map/ppermute | solution.py:388
  153.5 20.6 %collective-permute-done.24.refs_1_ = bf16[72,2048]{1,0:T(8,128)(2,1)S(1)} collective-permute-done((bf16[72,2048]{1,0:T(8,128)(2,1)S(1)}, bf16[72,2048]{1,0:T(8,128)(2,1)S(1)}, u32[]{:S(2)}, u32[]{:S(2)}) %collective-permute-start.24) | collective-permute-done | bytes 294944 | tf_op jit(solution)/shard_map/ppermute | solution.py:394
  (123 shorter events, 37.7 us)
Async XLA Ops:
  8.7 28.2 %collective-permute-start.1 = (f32[256,1024]{1,0:T(8,128)S(1)}, f32[256,1024]{1,0:T(8,128)S(1)}, u32[]{:S(2)}, u32[]{:S(2)}) collective-permute-start(f32[256,1024]{1,0:T(8,128)S(1)} %get-tuple-element.51), channel_id=1, source_target_pairs={{0,1},{1,0},{2,3},{3,2},{4,5},{5,4},{6,7},{7,6},{8,9},{9,8},{10,11... | collective-permute-start | bytes 3145736 | tf_op jit(solution)/shard_map/ppermute | solution.py:385
  9.7 11.5 %collective-permute-start.3 = (bf16[256,512]{1,0:T(8,128)(2,1)S(1)}, bf16[256,512]{1,0:T(8,128)(2,1)S(1)}, u32[]{:S(2)}, u32[]{:S(2)}) collective-permute-start(bf16[256,512]{1,0:T(8,128)(2,1)S(1)} %shard_map.113.refs_0_), channel_id=1, source_target_pairs={{0,4},{2,6},{4,8},{6,10},{8,12},{10,14},{12,0},{14,2},{1,5},{3,7},... | collective-permute-start | bytes 786440 | tf_op jit(solution)/shard_map/ppermute | solution.py:391
  31.7 15.6 %collective-permute-start.7 = (bf16[256,512]{1,0:T(8,128)(2,1)S(1)}, bf16[256,512]{1,0:T(8,128)(2,1)S(1)}, u32[]{:S(2)}, u32[]{:S(2)}) collective-permute-start(bf16[256,512]{1,0:T(8,128)(2,1)S(1)} %collective-permute-done.4.refs_1_), channel_id=1, source_target_pairs={{0,2},{2,0},{4,6},{6,4},{8,10},{10,8},{12,14},{14,12},{1,3},{3,1},... | collective-permute-start | bytes 786440 | tf_op jit(solution)/shard_map/ppermute | solution.py:388
  36.1 16.9 %collective-permute-start.6 = (bf16[256,512]{1,0:T(8,128)(2,1)S(1)}, bf16[256,512]{1,0:T(8,128)(2,1)S(1)}, u32[]{:S(2)}, u32[]{:S(2)}) collective-permute-start(bf16[256,512]{1,0:T(8,128)(2,1)S(1)} %collective-permute-done.5.refs_1_), channel_id=1, source_target_pairs={{0,2},{2,0},{4,6},{6,4},{8,10},{10,8},{12,14},{14,12},{1,3},{3,1},... | collective-permute-start | bytes 786440 | tf_op jit(solution)/shard_map/ppermute | solution.py:388
  64.1 18.2 %collective-permute-start.25 = (bf16[72,2048]{1,0:T(8,128)(2,1)S(1)}, bf16[72,2048]{1,0:T(8,128)(2,1)S(1)}, u32[]{:S(2)}, u32[]{:S(2)}) collective-permute-start(bf16[72,2048]{1,0:T(8,128)(2,1)S(1)} %get-tuple-element.79), channel_id=1, source_target_pairs={{0,12},{2,14},{4,8},{6,10},{8,4},{10,6},{12,0},{14,2},{1,13},{3,15... | collective-permute-start | bytes 884744 | tf_op jit(solution)/shard_map/ppermute | solution.py:394
  64.1 26.5 %collective-permute-start.17 = (bf16[72,2048]{1,0:T(8,128)(2,1)S(1)}, bf16[72,2048]{1,0:T(8,128)(2,1)S(1)}, u32[]{:S(2)}, u32[]{:S(2)}) collective-permute-start(bf16[72,2048]{1,0:T(8,128)(2,1)S(1)} %get-tuple-element.71), channel_id=1, source_target_pairs={{0,8},{2,10},{4,12},{6,14},{8,0},{10,2},{12,4},{14,6},{1,9},{3,11}... | collective-permute-start | bytes 884744 | tf_op jit(solution)/shard_map/ppermute | solution.py:394
  65.3 25.9 %collective-permute-start.12 = (bf16[72,2048]{1,0:T(8,128)(2,1)S(1)}, bf16[72,2048]{1,0:T(8,128)(2,1)S(1)}, u32[]{:S(2)}, u32[]{:S(2)}) collective-permute-start(bf16[72,2048]{1,0:T(8,128)(2,1)S(1)} %get-tuple-element.66.refs_0_), channel_id=1, source_target_pairs={{0,1},{1,0},{2,3},{3,2},{4,5},{5,4},{6,7},{7,6},{8,9},{9,8},{10,11... | collective-permute-start | bytes 884744 | tf_op jit(solution)/shard_map/ppermute | solution.py:385
  70.8 22.4 %collective-permute-start.34 = (bf16[72,2048]{1,0:T(8,128)(2,1)S(1)}, bf16[72,2048]{1,0:T(8,128)(2,1)S(1)}, u32[]{:S(2)}, u32[]{:S(2)}) collective-permute-start(bf16[72,2048]{1,0:T(8,128)(2,1)S(1)} %collective-permute-done.33.refs_0_), channel_id=1, source_target_pairs={{0,2},{2,0},{4,6},{6,4},{8,10},{10,8},{12,14},{14,12},{1,3},{3,1},... | collective-permute-start | bytes 884744 | tf_op jit(solution)/shard_map/ppermute | solution.py:388
  71.4 22.6 %collective-permute-start.13 = (bf16[72,2048]{1,0:T(8,128)(2,1)S(1)}, bf16[72,2048]{1,0:T(8,128)(2,1)S(1)}, u32[]{:S(2)}, u32[]{:S(2)}) collective-permute-start(bf16[72,2048]{1,0:T(8,128)(2,1)S(1)} %collective-permute-done.11.refs_1_), channel_id=1, source_target_pairs={{0,1},{1,0},{2,3},{3,2},{4,5},{5,4},{6,7},{7,6},{8,9},{9,8},{10,11... | collective-permute-start | bytes 884744 | tf_op jit(solution)/shard_map/ppermute | solution.py:385
  82.2 18.7 %collective-permute-start.35 = (bf16[72,2048]{1,0:T(8,128)(2,1)S(1)}, bf16[72,2048]{1,0:T(8,128)(2,1)S(1)}, u32[]{:S(2)}, u32[]{:S(2)}) collective-permute-start(bf16[72,2048]{1,0:T(8,128)(2,1)S(1)} %collective-permute-done.33.refs_0_), channel_id=1, source_target_pairs={{0,1},{1,0},{2,3},{3,2},{4,5},{5,4},{6,7},{7,6},{8,9},{9,8},{10,11... | collective-permute-start | bytes 884744 | tf_op jit(solution)/shard_map/ppermute | solution.py:385
  91.2 17.5 %collective-permute-start.27 = (bf16[72,2048]{1,0:T(8,128)(2,1)S(1)}, bf16[72,2048]{1,0:T(8,128)(2,1)S(1)}, u32[]{:S(2)}, u32[]{:S(2)}) collective-permute-start(bf16[72,2048]{1,0:T(8,128)(2,1)S(1)} %collective-permute-done.25.refs_0_), channel_id=1, source_target_pairs={{0,1},{1,0},{2,3},{3,2},{4,5},{5,4},{6,7},{7,6},{8,9},{9,8},{10,11... | collective-permute-start | bytes 884744 | tf_op jit(solution)/shard_map/ppermute | solution.py:385
  93.2 16.1 %collective-permute-start.18 = (bf16[72,2048]{1,0:T(8,128)(2,1)S(1)}, bf16[72,2048]{1,0:T(8,128)(2,1)S(1)}, u32[]{:S(2)}, u32[]{:S(2)}) collective-permute-start(bf16[72,2048]{1,0:T(8,128)(2,1)S(1)} %collective-permute-done.17.refs_0_), channel_id=1, source_target_pairs={{0,2},{2,0},{4,6},{6,4},{8,10},{10,8},{12,14},{14,12},{1,3},{3,1},... | collective-permute-start | bytes 884744 | tf_op jit(solution)/shard_map/ppermute | solution.py:388
  100.9 15.7 %collective-permute-start.19 = (bf16[72,2048]{1,0:T(8,128)(2,1)S(1)}, bf16[72,2048]{1,0:T(8,128)(2,1)S(1)}, u32[]{:S(2)}, u32[]{:S(2)}) collective-permute-start(bf16[72,2048]{1,0:T(8,128)(2,1)S(1)} %collective-permute-done.17.refs_0_), channel_id=1, source_target_pairs={{0,1},{1,0},{2,3},{3,2},{4,5},{5,4},{6,7},{7,6},{8,9},{9,8},{10,11... | collective-permute-start | bytes 884744 | tf_op jit(solution)/shard_map/ppermute | solution.py:385
  101.2 22.6 %collective-permute-start.15 = (bf16[72,2048]{1,0:T(8,128)(2,1)S(1)}, bf16[72,2048]{1,0:T(8,128)(2,1)S(1)}, u32[]{:S(2)}, u32[]{:S(2)}) collective-permute-start(bf16[72,2048]{1,0:T(8,128)(2,1)S(1)} %get-tuple-element.70), channel_id=1, source_target_pairs={{0,1},{1,0},{2,3},{3,2},{4,5},{5,4},{6,7},{7,6},{8,9},{9,8},{10,11... | collective-permute-start | bytes 884744 | tf_op jit(solution)/shard_map/ppermute | solution.py:385
  108.7 44.7 %collective-permute-start.14 = (bf16[72,2048]{1,0:T(8,128)(2,1)S(1)}, bf16[72,2048]{1,0:T(8,128)(2,1)S(1)}, u32[]{:S(2)}, u32[]{:S(2)}) collective-permute-start(bf16[72,2048]{1,0:T(8,128)(2,1)S(1)} %get-tuple-element.68), channel_id=1, source_target_pairs={{0,1},{1,0},{2,3},{3,2},{4,5},{5,4},{6,7},{7,6},{8,9},{9,8},{10,11... | collective-permute-start | bytes 884744 | tf_op jit(solution)/shard_map/ppermute | solution.py:385
  109.4 14.7 %collective-permute-start.38 = (bf16[72,2048]{1,0:T(8,128)(2,1)S(1)}, bf16[72,2048]{1,0:T(8,128)(2,1)S(1)}, u32[]{:S(2)}, u32[]{:S(2)}) collective-permute-start(bf16[72,2048]{1,0:T(8,128)(2,1)S(1)} %get-tuple-element.90), channel_id=1, source_target_pairs={{0,1},{1,0},{2,3},{3,2},{4,5},{5,4},{6,7},{7,6},{8,9},{9,8},{10,11... | collective-permute-start | bytes 884744 | tf_op jit(solution)/shard_map/ppermute | solution.py:385
  123.8 11.2 %collective-permute-start.29 = (bf16[72,2048]{1,0:T(8,128)(2,1)S(1)}, bf16[72,2048]{1,0:T(8,128)(2,1)S(1)}, u32[]{:S(2)}, u32[]{:S(2)}) collective-permute-start(bf16[72,2048]{1,0:T(8,128)(2,1)S(1)} %get-tuple-element.81), channel_id=1, source_target_pairs={{0,1},{1,0},{2,3},{3,2},{4,5},{5,4},{6,7},{7,6},{8,9},{9,8},{10,11... | collective-permute-start | bytes 884744 | tf_op jit(solution)/shard_map/ppermute | solution.py:385
  124.6 22.3 %collective-permute-start.21 = (bf16[72,2048]{1,0:T(8,128)(2,1)S(1)}, bf16[72,2048]{1,0:T(8,128)(2,1)S(1)}, u32[]{:S(2)}, u32[]{:S(2)}) collective-permute-start(bf16[72,2048]{1,0:T(8,128)(2,1)S(1)} %get-tuple-element.73), channel_id=1, source_target_pairs={{0,1},{1,0},{2,3},{3,2},{4,5},{5,4},{6,7},{7,6},{8,9},{9,8},{10,11... | collective-permute-start | bytes 884744 | tf_op jit(solution)/shard_map/ppermute | solution.py:385
  126.6 26.7 %collective-permute-start.16 = (bf16[72,2048]{1,0:T(8,128)(2,1)S(1)}, bf16[72,2048]{1,0:T(8,128)(2,1)S(1)}, u32[]{:S(2)}, u32[]{:S(2)}) collective-permute-start(bf16[72,2048]{1,0:T(8,128)(2,1)S(1)} %add_convert_fusion.10), channel_id=1, source_target_pairs={{0,2},{2,0},{4,6},{6,4},{8,10},{10,8},{12,14},{14,12},{1,3},{3,1},... | collective-permute-start | bytes 884744 | tf_op jit(solution)/shard_map/ppermute | solution.py:388
  134.2 12.6 %collective-permute-start.31 = (bf16[72,2048]{1,0:T(8,128)(2,1)S(1)}, bf16[72,2048]{1,0:T(8,128)(2,1)S(1)}, u32[]{:S(2)}, u32[]{:S(2)}) collective-permute-start(bf16[72,2048]{1,0:T(8,128)(2,1)S(1)} %add_convert_fusion.4), channel_id=1, source_target_pairs={{0,2},{2,0},{4,6},{6,4},{8,10},{10,8},{12,14},{14,12},{1,3},{3,1},... | collective-permute-start | bytes 884744 | tf_op jit(solution)/shard_map/ppermute | solution.py:388
  135.0 18.2 %collective-permute-start.23 = (bf16[72,2048]{1,0:T(8,128)(2,1)S(1)}, bf16[72,2048]{1,0:T(8,128)(2,1)S(1)}, u32[]{:S(2)}, u32[]{:S(2)}) collective-permute-start(bf16[72,2048]{1,0:T(8,128)(2,1)S(1)} %add_convert_fusion.7), channel_id=1, source_target_pairs={{0,2},{2,0},{4,6},{6,4},{8,10},{10,8},{12,14},{14,12},{1,3},{3,1},... | collective-permute-start | bytes 884744 | tf_op jit(solution)/shard_map/ppermute | solution.py:388
  146.9 28.3 %collective-permute-start.40 = (bf16[72,2048]{1,0:T(8,128)(2,1)S(1)}, bf16[72,2048]{1,0:T(8,128)(2,1)S(1)}, u32[]{:S(2)}, u32[]{:S(2)}) collective-permute-start(bf16[72,2048]{1,0:T(8,128)(2,1)S(1)} %add_convert_fusion), channel_id=1, source_target_pairs={{0,4},{2,6},{4,0},{6,2},{8,12},{10,14},{12,8},{14,10},{1,5},{3,7},... | collective-permute-start | bytes 884744 | tf_op jit(solution)/shard_map/ppermute | solution.py:394
  147.0 28.2 %collective-permute-start.32 = (bf16[72,2048]{1,0:T(8,128)(2,1)S(1)}, bf16[72,2048]{1,0:T(8,128)(2,1)S(1)}, u32[]{:S(2)}, u32[]{:S(2)}) collective-permute-start(bf16[72,2048]{1,0:T(8,128)(2,1)S(1)} %add_convert_fusion.3), channel_id=1, source_target_pairs={{0,12},{2,14},{4,8},{6,10},{8,4},{10,6},{12,0},{14,2},{1,13},{3,15... | collective-permute-start | bytes 884744 | tf_op jit(solution)/shard_map/ppermute | solution.py:394
  153.3 20.8 %collective-permute-start.24 = (bf16[72,2048]{1,0:T(8,128)(2,1)S(1)}, bf16[72,2048]{1,0:T(8,128)(2,1)S(1)}, u32[]{:S(2)}, u32[]{:S(2)}) collective-permute-start(bf16[72,2048]{1,0:T(8,128)(2,1)S(1)} %add_convert_fusion.6), channel_id=1, source_target_pairs={{0,8},{2,10},{4,12},{6,14},{8,0},{10,2},{12,4},{14,6},{1,9},{3,11}... | collective-permute-start | bytes 884744 | tf_op jit(solution)/shard_map/ppermute | solution.py:394
  (32 other events, 370.9 us)

commit v5 on v3

--- a/solution.py
+++ b/solution.py
@@ -16,7 +16,7 @@
 
 HIDDEN_STEP = 256
 DOWN_STEP = 256
-ORDER = (0, 1, 2, 3)
+ORDER = (0, 2, 3, 1)
 
 epsilon = 1e-05
 base_theta = 1000000.0
@@ -244,16 +244,27 @@
     ]
 
 
-def pack_kernel(along, keep_ref, came_ref, tokens_ref, gain_ref, choice_ref, residual_ref, *out_refs):
+def route_kernel(along, choice_ref, weight_ref, *out_refs):
+    plane = lax.axis_index("expert") // along
+    choice = as_columns(choice_ref).astype(jnp.int32)
+    weights = as_columns(weight_ref)
+    for step, routing in enumerate(placed(choice, plane)):
+        weight = jnp.where(choice == (plane ^ step), weights, 0.0)
+        out_refs[2 * step][...] = routing
+        out_refs[2 * step + 1][...] = jnp.broadcast_to(
+            jnp.sum(weight, axis=1, keepdims=True), out_refs[2 * step + 1].shape
+        )
+
+
+def pack_kernel(keep_ref, came_ref, tokens_ref, gain_ref, *refs):
+    routing_refs, residual_ref, out_refs = refs[:EXPERTS], refs[EXPERTS], refs[EXPERTS + 1 :]
     attention = keep_ref[...] + came_ref[...].astype(f32)
     residual = (tokens_ref[...].astype(f32) + attention).astype(bf16)
     residual_ref[...] = residual
     mixed_in = normalized(residual.astype(f32), gain_ref[...])
-    plane = lax.axis_index("expert") // along
-    choice = as_columns(choice_ref).astype(jnp.int32)
-    for out_ref, routing in zip(out_refs, placed(choice, plane)):
+    for routing_ref, out_ref in zip(routing_refs, out_refs):
         out_ref[...] = lax.dot_general(
-            routing, mixed_in, (((0,), (0,)), ((), ())), preferred_element_type=f32
+            routing_ref[...], mixed_in, (((0,), (0,)), ((), ())), preferred_element_type=f32
         ).astype(bf16)
 
 
@@ -317,18 +328,17 @@
     )
 
 
-def combine_kernel(along, steps, base_ref, choice_ref, weight_ref, *refs):
-    row_refs, out_ref = refs[:-1], refs[-1]
-    plane = lax.axis_index("expert") // along
-    choice = as_columns(choice_ref).astype(jnp.int32)
-    weights = as_columns(weight_ref)
-    total = base_ref[...].astype(f32)
-    routings = placed(choice, plane)
-    for step, row_ref in zip(steps, row_refs):
-        expert = plane ^ step
-        weight = jnp.sum(jnp.where(choice == expert, weights, 0.0), axis=1, keepdims=True)
-        total = total + weight * dot(routings[step], row_ref[...])
-    out_ref[...] = total.astype(out_ref.dtype)
+def combine_kernel(base_ref, *refs):
+    total_ref, out_ref = base_ref, refs[-1]
+    width = 128
+    for start in range(0, out_ref.shape[1], 4 * width):
+        columns = slice(start, start + 4 * width)
+        total = total_ref[:, columns].astype(f32)
+        for index in range(0, len(refs) - 1, 3):
+            routing_ref, weight_ref, row_ref = refs[index : index + 3]
+            weight = jnp.concatenate([weight_ref[...]] * 4, axis=1)
+            total = total + weight * dot(routing_ref[...], row_ref[:, columns])
+        out_ref[:, columns] = total.astype(out_ref.dtype)
 
 
 def add(*terms):
@@ -429,7 +439,7 @@
     line = keyval
     for back in range(EXPERTS):
         if back:
-            line = upward(line)
+            line = planes(line, 1) if back == EXPERTS - 1 else upward(line)
         part.append((line, (back, 0)))
         if back:
             parts.append(part)
@@ -459,15 +469,23 @@
         )
     attention_send, attention_keep = state
     attention_came = across(attention_send)
+    routes = [shape((local_rows, ROWS), bf16), shape((local_rows, 128), f32)] * EXPERTS
+    routes = call(
+        functools.partial(route_kernel, along),
+        routes,
+        (expert_choice.T, gate_weights.T),
+        flops=4 * local_rows * local_rows * 128,
+        moved=4 * EXPERTS * local_rows * 256,
+    )
     residual, *packed = call(
-        functools.partial(pack_kernel, along),
+        pack_kernel,
         [shape((local_rows, model_width), bf16)] + [shape((ROWS, model_width), bf16)] * EXPERTS,
         (
             attention_keep,
             attention_came,
             tokens,
             feedforward_gain.reshape(1, -1),
-            expert_choice.T,
+            *routes[::2],
         ),
         flops=2 * EXPERTS * ROWS * local_rows * model_width,
         moved=12 * local_rows * model_width,
@@ -488,19 +506,23 @@
         others = [beside(near[turn], turn) for turn in range(1, along)]
         reduced = add(near[0], *others)
         collected[step] = planes(reduced, step) if step else reduced
+    a, b, c, d = ORDER
+    early, late = (a, b), (c, d)
 
     def combined(base, steps, kind):
+        operands = [base]
+        for step in steps:
+            operands += [*routes[2 * step : 2 * step + 2], collected[step]]
         return call(
-            functools.partial(combine_kernel, along, steps),
+            combine_kernel,
             shape((local_rows, model_width), kind),
-            (base, expert_choice.T, gate_weights.T, *[collected[step] for step in steps]),
+            operands,
             flops=2 * len(steps) * ROWS * local_rows * model_width,
             moved=8 * local_rows * model_width,
         )
 
-    a, b, c, d = ORDER
-    early = combined(residual, (a, c), f32)
-    return combined(early, (b, d), bf16)
+    total = combined(residual, early, f32)
+    return combined(total, late, bf16)
 
 
 def solution(mesh):

time: 174 us -> 178 us (1.023)
  starting transfers between devices: 30.3 us -> 33.4 us
  waiting for transfers between devices: 82.9 us -> 85.3 us
    ppermute x6 -> x7, waiting for transfers between devices: 30.1 us -> 36.6 us  [planes(): lax.ppermute(x, 'expert', [(i, i ^ step * along) for i in range(chips)])]
    ppermute x3 -> x2, waiting for transfers between devices: 23.7 us -> 17.8 us  [upward(): lax.ppermute(x, 'expert', [(i, (i + along) % chips) for i in range(chips)])]
    ppermute x20, starting transfers between devices: 12.5 us -> 17.7 us  [across(): return lax.ppermute(x, 'dp', [(i, i ^ 1) for i in range(cores)])]
    ppermute x12, waiting for transfers between devices: 26.5 us -> 29.1 us  [beside(): return lax.ppermute(x, 'expert', [(i, i ^ turn) for i in range(chips)])]
    ppermute x6 -> x7, starting transfers between devices: 6.04 us -> 3.85 us  [planes(): lax.ppermute(x, 'expert', [(i, i ^ step * along) for i in range(chips)])]
    pallas_call x16 -> x17, Pallas kernels: 45.9 us -> 45 us  [call(): pl.pallas_call(kernel, out_shape=outs, in_specs=[VMEM] * len(operands), o...]
  transfers between devices with their start and end apart: 41 -> 41, of which waited for: 15 -> 14; matrix products, arithmetic and copies ran while one was open for 1% -> 1% of each run, Pallas kernels for 24% -> 23%
where the time goes in v5:
time: 178 us; the launch traced here: 175 us
  waiting for transfers between devices  85.3 us (48%)
  Pallas kernels  47 us (26%)
  starting transfers between devices  33.4 us (19%)
  local copies, waits for them, and re-layouts  7.74 us (4%)
    pallas_call x17, Pallas kernels, call(): pl.pallas_call(kernel, out_shape=outs, in_specs=[VMEM] * len(operands), o...  45 us
    ppermute x7, waiting for transfers between devices, planes(): lax.ppermute(x, 'expert', [(i, i ^ step * along) for i in range(chips)])  36.6 us
    ppermute x12, waiting for transfers between devices, beside(): return lax.ppermute(x, 'expert', [(i, i ^ turn) for i in range(chips)])  29.1 us
    ppermute x2, waiting for transfers between devices, upward(): lax.ppermute(x, 'expert', [(i, (i + along) % chips) for i in range(chips)])  17.8 us
    ppermute x20, starting transfers between devices, across(): return lax.ppermute(x, 'dp', [(i, i ^ 1) for i in range(cores)])  17.7 us
    ppermute x12, starting transfers between devices, beside(): return lax.ppermute(x, 'expert', [(i, i ^ turn) for i in range(chips)])  8.96 us
    unnamed x30, local copies, waits for them, and re-layouts  7.74 us
    ppermute x7, starting transfers between devices, planes(): lax.ppermute(x, 'expert', [(i, i ^ step * along) for i in range(chips)])  3.85 us
  transfers between devices with their start and end apart: 41, of which 14 were waited for; matrix products, arithmetic and copies ran while one was open for 1% of the time, Pallas kernels for 23%

profile of v5, /device:TPU:1, one launch (start us, length us, event | category | flops | bytes accessed | tf_op | source)
XLA Modules:
  0.0 175.3 jit_solution(7990670260347926695)
XLA Ops:
  5.2 2.2 %copy-done = bf16[1024,2048]{1,0:T(8,128)(2,1)S(1)} copy-done((bf16[1024,2048]{1,0:T(8,128)(2,1)S(1)}, bf16[1024,2048]{1,0:T(8,128)(2,1)}, u32[]{:S(2)}) %copy-start) | copy-done | bytes 4194328
  9.7 2.8 %collective-permute-start.3 = (bf16[256,512]{1,0:T(8,128)(2,1)S(1)}, bf16[256,512]{1,0:T(8,128)(2,1)S(1)}, u32[]{:S(2)}, u32[]{:S(2)}) collective-permute-start(bf16[256,512]{1,0:T(8,128)(2,1)S(1)} %shard_map.113.refs_0_), channel_id=1, source_target_pairs={{0,4},{2,6},{4,8},{6,10},{8,12},{10,14},{12,0},{14,2},{1,5},{3,7},... | collective-permute-start | bytes 786440 | tf_op jit(solution)/shard_map/ppermute | solution.py:381
  12.5 8.7 %collective-permute-done.3.refs_2_ = bf16[256,512]{1,0:T(8,128)(2,1)S(1)} collective-permute-done((bf16[256,512]{1,0:T(8,128)(2,1)S(1)}, bf16[256,512]{1,0:T(8,128)(2,1)S(1)}, u32[]{:S(2)}, u32[]{:S(2)}) %collective-permute-start.3) | collective-permute-done | bytes 262176 | tf_op jit(solution)/shard_map/ppermute | solution.py:381
  21.2 9.1 %collective-permute-done.4.refs_1_ = bf16[256,512]{1,0:T(8,128)(2,1)S(1)} collective-permute-done((bf16[256,512]{1,0:T(8,128)(2,1)S(1)}, bf16[256,512]{1,0:T(8,128)(2,1)S(1)}, u32[]{:S(2)}, u32[]{:S(2)}) %collective-permute-start.4) | collective-permute-done | bytes 262176 | tf_op jit(solution)/shard_map/ppermute | solution.py:381
  32.5 3.6 %collective-permute-done.5.refs_1_ = bf16[256,512]{1,0:T(8,128)(2,1)S(1)} collective-permute-done((bf16[256,512]{1,0:T(8,128)(2,1)S(1)}, bf16[256,512]{1,0:T(8,128)(2,1)S(1)}, u32[]{:S(2)}, u32[]{:S(2)}) %collective-permute-start.5) | collective-permute-done | bytes 262176 | tf_op jit(solution)/shard_map/ppermute | solution.py:384
  37.3 3.6 %shard_map.114 = (f32[8,256,128]{2,1,0:T(8,128)S(1)}, f32[8,256,128]{2,1,0:T(8,128)S(1)}, f32[8,256,128]{2,1,0:T(8,128)S(1)}) custom-call(bf16[8,256,128]{2,1,0:T(8,128)(2,1)S(1)} %shard_map.111.query_ref, bf16[256,512]{1,0:T(8,128)(2,1)S(1)} %shard_map.113.refs_0_, bf16[256,512]{1,0:T(8,128)(2,1)S(1)} %collective-permute-done.9.refs_1_, ...), custom_call_target="tpu_custom_call" | custom-call | flops 805306368 | bytes 2097152 | tf_op jit(solution)/shard_map/pallas_call | solution.py:35
  41.8 2.9 %shard_map.115 = (f32[8,256,128]{2,1,0:T(8,128)S(1)}, f32[8,256,128]{2,1,0:T(8,128)S(1)}, f32[8,256,128]{2,1,0:T(8,128)S(1)}) custom-call(bf16[8,256,128]{2,1,0:T(8,128)(2,1)S(1)} %shard_map.111.query_ref, bf16[256,512]{1,0:T(8,128)(2,1)S(1)} %collective-permute-done.8.refs_0_, bf16[256,512]{1,0:T(8,128)(2,1)S(1)} %collective-permute-done.4.refs_1_, ...), custom_call_target="tpu_custom_call" | custom-call | flops 536870912 | bytes 2097152 | tf_op jit(solution)/shard_map/pallas_call | solution.py:35
  44.7 2.7 %collective-permute-done.7.refs_0_ = bf16[256,512]{1,0:T(8,128)(2,1)S(1)} collective-permute-done((bf16[256,512]{1,0:T(8,128)(2,1)S(1)}, bf16[256,512]{1,0:T(8,128)(2,1)S(1)}, u32[]{:S(2)}, u32[]{:S(2)}) %collective-permute-start.7) | collective-permute-done | bytes 262176 | tf_op jit(solution)/shard_map/ppermute | solution.py:378
  47.4 2.9 %shard_map.116 = (f32[8,256,128]{2,1,0:T(8,128)S(1)}, f32[8,256,128]{2,1,0:T(8,128)S(1)}, f32[8,256,128]{2,1,0:T(8,128)S(1)}) custom-call(bf16[8,256,128]{2,1,0:T(8,128)(2,1)S(1)} %shard_map.111.query_ref, bf16[256,512]{1,0:T(8,128)(2,1)S(1)} %collective-permute-done.7.refs_0_, bf16[256,512]{1,0:T(8,128)(2,1)S(1)} %collective-permute-done.5.refs_1_, ...), custom_call_target="tpu_custom_call" | custom-call | flops 536870912 | bytes 2097152 | tf_op jit(solution)/shard_map/pallas_call | solution.py:35
  50.3 2.7 %collective-permute-done.6.refs_0_ = bf16[256,512]{1,0:T(8,128)(2,1)S(1)} collective-permute-done((bf16[256,512]{1,0:T(8,128)(2,1)S(1)}, bf16[256,512]{1,0:T(8,128)(2,1)S(1)}, u32[]{:S(2)}, u32[]{:S(2)}) %collective-permute-start.6) | collective-permute-done | bytes 262176 | tf_op jit(solution)/shard_map/ppermute | solution.py:378
  53.0 3.0 %shard_map.117 = (bf16[128,2048]{1,0:T(8,128)(2,1)S(1)}, f32[128,2048]{1,0:T(8,128)S(1)}) custom-call(bf16[8,256,128]{2,1,0:T(8,128)(2,1)S(1)} %shard_map.111.query_ref, bf16[256,512]{1,0:T(8,128)(2,1)S(1)} %collective-permute-done.6.refs_0_, f32[8,256,128]{2,1,0:T(8,128)S(1)} %get-tuple-element.63.refs_1_, f32[8,256,128]{2,1,0:T(8,128)S(1)} %get-tuple-element.64.refs_2_, ...), custom_call_target="tpu_custom_call" | custom-call | flops 1342177280 | bytes 2097152 | tf_op jit(solution)/shard_map/pallas_call | solution.py:35
  56.0 2.9 %collective-permute-start.10 = (bf16[128,2048]{1,0:T(8,128)(2,1)S(1)}, bf16[128,2048]{1,0:T(8,128)(2,1)S(1)}, u32[]{:S(2)}, u32[]{:S(2)}) collective-permute-start(bf16[128,2048]{1,0:T(8,128)(2,1)S(1)} %get-tuple-element.67), channel_id=1, source_target_pairs={{0,1},{1,0},{2,3},{3,2},{4,5},{5,4},{6,7},{7,6},{8,9},{9,8},{10,11... | collective-permute-start | bytes 1572872 | tf_op jit(solution)/shard_map/ppermute | solution.py:375
  66.2 4.1 %collective-permute-done.33.refs_0_ = bf16[72,2048]{1,0:T(8,128)(2,1)S(1)} collective-permute-done((bf16[72,2048]{1,0:T(8,128)(2,1)S(1)}, bf16[72,2048]{1,0:T(8,128)(2,1)S(1)}, u32[]{:S(2)}, u32[]{:S(2)}) %collective-permute-start.33) | collective-permute-done | bytes 294944 | tf_op jit(solution)/shard_map/ppermute | solution.py:384
  71.0 6.7 %collective-permute-start.13 = (bf16[72,2048]{1,0:T(8,128)(2,1)S(1)}, bf16[72,2048]{1,0:T(8,128)(2,1)S(1)}, u32[]{:S(2)}, u32[]{:S(2)}) collective-permute-start(bf16[72,2048]{1,0:T(8,128)(2,1)S(1)} %collective-permute-done.11.refs_1_), channel_id=1, source_target_pairs={{0,1},{1,0},{2,3},{3,2},{4,5},{5,4},{6,7},{7,6},{8,9},{9,8},{10,11... | collective-permute-start | bytes 884744 | tf_op jit(solution)/shard_map/ppermute | solution.py:375
  81.9 8.3 %collective-permute-done.17.refs_0_ = bf16[72,2048]{1,0:T(8,128)(2,1)S(1)} collective-permute-done((bf16[72,2048]{1,0:T(8,128)(2,1)S(1)}, bf16[72,2048]{1,0:T(8,128)(2,1)S(1)}, u32[]{:S(2)}, u32[]{:S(2)}) %collective-permute-start.17) | collective-permute-done | bytes 294944 | tf_op jit(solution)/shard_map/ppermute | solution.py:384
  90.8 1.9 %collective-permute-start.27 = (bf16[72,2048]{1,0:T(8,128)(2,1)S(1)}, bf16[72,2048]{1,0:T(8,128)(2,1)S(1)}, u32[]{:S(2)}, u32[]{:S(2)}) collective-permute-start(bf16[72,2048]{1,0:T(8,128)(2,1)S(1)} %collective-permute-done.25.refs_0_), channel_id=1, source_target_pairs={{0,1},{1,0},{2,3},{3,2},{4,5},{5,4},{6,7},{7,6},{8,9},{9,8},{10,11... | collective-permute-start | bytes 884744 | tf_op jit(solution)/shard_map/ppermute | solution.py:375
  93.9 6.6 %shard_map.120 = (bf16[72,2048]{1,0:T(8,128)(2,1)S(1)}, bf16[72,2048]{1,0:T(8,128)(2,1)S(1)}, bf16[72,2048]{1,0:T(8,128)(2,1)S(1)}, bf16[72,2048]{1,0:T(8,128)(2,1)S(1)}) custom-call(bf16[2048,1792]{1,0:T(8,128)(2,1)S(1)} %fetch.5.gate_ref, bf16[2048,1792]{1,0:T(8,128)(2,1)S(1)} %fetch.6.up_ref, bf16[1792,2048]{1,0:T(8,128)(2,1)S(1)} %fetch.7.down_ref, ...), custom_call_target="tpu_custom_call" | custom-call | flops 6341787648 | bytes 22020096 | tf_op jit(solution)/shard_map/pallas_call | solution.py:35
  101.7 6.6 %shard_map.124 = (bf16[72,2048]{1,0:T(8,128)(2,1)S(1)}, bf16[72,2048]{1,0:T(8,128)(2,1)S(1)}, bf16[72,2048]{1,0:T(8,128)(2,1)S(1)}, bf16[72,2048]{1,0:T(8,128)(2,1)S(1)}) custom-call(bf16[2048,1792]{1,0:T(8,128)(2,1)S(1)} %fetch.5.gate_ref, bf16[2048,1792]{1,0:T(8,128)(2,1)S(1)} %fetch.6.up_ref, bf16[1792,2048]{1,0:T(8,128)(2,1)S(1)} %fetch.7.down_ref, ...), custom_call_target="tpu_custom_call" | custom-call | flops 6341787648 | bytes 22020096 | tf_op jit(solution)/shard_map/pallas_call | solution.py:35
  109.3 6.8 %shard_map.123 = (bf16[72,2048]{1,0:T(8,128)(2,1)S(1)}, bf16[72,2048]{1,0:T(8,128)(2,1)S(1)}, bf16[72,2048]{1,0:T(8,128)(2,1)S(1)}, bf16[72,2048]{1,0:T(8,128)(2,1)S(1)}) custom-call(bf16[2048,1792]{1,0:T(8,128)(2,1)S(1)} %fetch.5.gate_ref, bf16[2048,1792]{1,0:T(8,128)(2,1)S(1)} %fetch.6.up_ref, bf16[1792,2048]{1,0:T(8,128)(2,1)S(1)} %fetch.7.down_ref, ...), custom_call_target="tpu_custom_call" | custom-call | flops 6341787648 | bytes 22020096 | tf_op jit(solution)/shard_map/pallas_call | solution.py:35
  116.8 6.6 %shard_map.121 = (bf16[72,2048]{1,0:T(8,128)(2,1)S(1)}, bf16[72,2048]{1,0:T(8,128)(2,1)S(1)}, bf16[72,2048]{1,0:T(8,128)(2,1)S(1)}, bf16[72,2048]{1,0:T(8,128)(2,1)S(1)}) custom-call(bf16[2048,1792]{1,0:T(8,128)(2,1)S(1)} %fetch.5.gate_ref, bf16[2048,1792]{1,0:T(8,128)(2,1)S(1)} %fetch.6.up_ref, bf16[1792,2048]{1,0:T(8,128)(2,1)S(1)} %fetch.7.down_ref, ...), custom_call_target="tpu_custom_call" | custom-call | flops 6341787648 | bytes 22020096 | tf_op jit(solution)/shard_map/pallas_call | solution.py:35
  127.0 6.7 %collective-permute-done.39 = bf16[72,2048]{1,0:T(8,128)(2,1)S(1)} collective-permute-done((bf16[72,2048]{1,0:T(8,128)(2,1)S(1)}, bf16[72,2048]{1,0:T(8,128)(2,1)S(1)}, u32[]{:S(2)}, u32[]{:S(2)}) %collective-permute-start.39) | collective-permute-done | bytes 294944 | tf_op jit(solution)/shard_map/ppermute | solution.py:378
  135.4 11.0 %collective-permute-done.31 = bf16[72,2048]{1,0:T(8,128)(2,1)S(1)} collective-permute-done((bf16[72,2048]{1,0:T(8,128)(2,1)S(1)}, bf16[72,2048]{1,0:T(8,128)(2,1)S(1)}, u32[]{:S(2)}, u32[]{:S(2)}) %collective-permute-start.31) | collective-permute-done | bytes 294944 | tf_op jit(solution)/shard_map/ppermute | solution.py:378
  147.5 5.2 %collective-permute-done.23 = bf16[72,2048]{1,0:T(8,128)(2,1)S(1)} collective-permute-done((bf16[72,2048]{1,0:T(8,128)(2,1)S(1)}, bf16[72,2048]{1,0:T(8,128)(2,1)S(1)}, u32[]{:S(2)}, u32[]{:S(2)}) %collective-permute-start.23) | collective-permute-done | bytes 294944 | tf_op jit(solution)/shard_map/ppermute | solution.py:378
  153.0 20.6 %collective-permute-done.24.refs_5_ = bf16[72,2048]{1,0:T(8,128)(2,1)S(1)} collective-permute-done((bf16[72,2048]{1,0:T(8,128)(2,1)S(1)}, bf16[72,2048]{1,0:T(8,128)(2,1)S(1)}, u32[]{:S(2)}, u32[]{:S(2)}) %collective-permute-start.24) | collective-permute-done | bytes 294944 | tf_op jit(solution)/shard_map/ppermute | solution.py:384
  (124 shorter events, 36.6 us)
Async XLA Ops:
  8.7 28.2 %collective-permute-start.1 = (f32[256,1024]{1,0:T(8,128)S(1)}, f32[256,1024]{1,0:T(8,128)S(1)}, u32[]{:S(2)}, u32[]{:S(2)}) collective-permute-start(f32[256,1024]{1,0:T(8,128)S(1)} %get-tuple-element.54), channel_id=1, source_target_pairs={{0,1},{1,0},{2,3},{3,2},{4,5},{5,4},{6,7},{7,6},{8,9},{9,8},{10,11... | collective-permute-start | bytes 3145736 | tf_op jit(solution)/shard_map/ppermute | solution.py:375
  9.7 11.5 %collective-permute-start.3 = (bf16[256,512]{1,0:T(8,128)(2,1)S(1)}, bf16[256,512]{1,0:T(8,128)(2,1)S(1)}, u32[]{:S(2)}, u32[]{:S(2)}) collective-permute-start(bf16[256,512]{1,0:T(8,128)(2,1)S(1)} %shard_map.113.refs_0_), channel_id=1, source_target_pairs={{0,4},{2,6},{4,8},{6,10},{8,12},{10,14},{12,0},{14,2},{1,5},{3,7},... | collective-permute-start | bytes 786440 | tf_op jit(solution)/shard_map/ppermute | solution.py:381
  31.7 15.6 %collective-permute-start.7 = (bf16[256,512]{1,0:T(8,128)(2,1)S(1)}, bf16[256,512]{1,0:T(8,128)(2,1)S(1)}, u32[]{:S(2)}, u32[]{:S(2)}) collective-permute-start(bf16[256,512]{1,0:T(8,128)(2,1)S(1)} %collective-permute-done.4.refs_1_), channel_id=1, source_target_pairs={{0,2},{2,0},{4,6},{6,4},{8,10},{10,8},{12,14},{14,12},{1,3},{3,1},... | collective-permute-start | bytes 786440 | tf_op jit(solution)/shard_map/ppermute | solution.py:378
  36.1 16.9 %collective-permute-start.6 = (bf16[256,512]{1,0:T(8,128)(2,1)S(1)}, bf16[256,512]{1,0:T(8,128)(2,1)S(1)}, u32[]{:S(2)}, u32[]{:S(2)}) collective-permute-start(bf16[256,512]{1,0:T(8,128)(2,1)S(1)} %collective-permute-done.5.refs_1_), channel_id=1, source_target_pairs={{0,2},{2,0},{4,6},{6,4},{8,10},{10,8},{12,14},{14,12},{1,3},{3,1},... | collective-permute-start | bytes 786440 | tf_op jit(solution)/shard_map/ppermute | solution.py:378
  63.6 18.2 %collective-permute-start.25 = (bf16[72,2048]{1,0:T(8,128)(2,1)S(1)}, bf16[72,2048]{1,0:T(8,128)(2,1)S(1)}, u32[]{:S(2)}, u32[]{:S(2)}) collective-permute-start(bf16[72,2048]{1,0:T(8,128)(2,1)S(1)} %get-tuple-element.86), channel_id=1, source_target_pairs={{0,12},{2,14},{4,8},{6,10},{8,4},{10,6},{12,0},{14,2},{1,13},{3,15... | collective-permute-start | bytes 884744 | tf_op jit(solution)/shard_map/ppermute | solution.py:384
  63.6 26.5 %collective-permute-start.17 = (bf16[72,2048]{1,0:T(8,128)(2,1)S(1)}, bf16[72,2048]{1,0:T(8,128)(2,1)S(1)}, u32[]{:S(2)}, u32[]{:S(2)}) collective-permute-start(bf16[72,2048]{1,0:T(8,128)(2,1)S(1)} %get-tuple-element.80), channel_id=1, source_target_pairs={{0,8},{2,10},{4,12},{6,14},{8,0},{10,2},{12,4},{14,6},{1,9},{3,11}... | collective-permute-start | bytes 884744 | tf_op jit(solution)/shard_map/ppermute | solution.py:384
  64.9 25.9 %collective-permute-start.12 = (bf16[72,2048]{1,0:T(8,128)(2,1)S(1)}, bf16[72,2048]{1,0:T(8,128)(2,1)S(1)}, u32[]{:S(2)}, u32[]{:S(2)}) collective-permute-start(bf16[72,2048]{1,0:T(8,128)(2,1)S(1)} %get-tuple-element.74.refs_0_), channel_id=1, source_target_pairs={{0,1},{1,0},{2,3},{3,2},{4,5},{5,4},{6,7},{7,6},{8,9},{9,8},{10,11... | collective-permute-start | bytes 884744 | tf_op jit(solution)/shard_map/ppermute | solution.py:375
  70.4 22.4 %collective-permute-start.34 = (bf16[72,2048]{1,0:T(8,128)(2,1)S(1)}, bf16[72,2048]{1,0:T(8,128)(2,1)S(1)}, u32[]{:S(2)}, u32[]{:S(2)}) collective-permute-start(bf16[72,2048]{1,0:T(8,128)(2,1)S(1)} %collective-permute-done.33.refs_0_), channel_id=1, source_target_pairs={{0,2},{2,0},{4,6},{6,4},{8,10},{10,8},{12,14},{14,12},{1,3},{3,1},... | collective-permute-start | bytes 884744 | tf_op jit(solution)/shard_map/ppermute | solution.py:378
  71.0 22.6 %collective-permute-start.13 = (bf16[72,2048]{1,0:T(8,128)(2,1)S(1)}, bf16[72,2048]{1,0:T(8,128)(2,1)S(1)}, u32[]{:S(2)}, u32[]{:S(2)}) collective-permute-start(bf16[72,2048]{1,0:T(8,128)(2,1)S(1)} %collective-permute-done.11.refs_1_), channel_id=1, source_target_pairs={{0,1},{1,0},{2,3},{3,2},{4,5},{5,4},{6,7},{7,6},{8,9},{9,8},{10,11... | collective-permute-start | bytes 884744 | tf_op jit(solution)/shard_map/ppermute | solution.py:375
  81.8 18.7 %collective-permute-start.35 = (bf16[72,2048]{1,0:T(8,128)(2,1)S(1)}, bf16[72,2048]{1,0:T(8,128)(2,1)S(1)}, u32[]{:S(2)}, u32[]{:S(2)}) collective-permute-start(bf16[72,2048]{1,0:T(8,128)(2,1)S(1)} %collective-permute-done.33.refs_0_), channel_id=1, source_target_pairs={{0,1},{1,0},{2,3},{3,2},{4,5},{5,4},{6,7},{7,6},{8,9},{9,8},{10,11... | collective-permute-start | bytes 884744 | tf_op jit(solution)/shard_map/ppermute | solution.py:375
  90.8 17.5 %collective-permute-start.27 = (bf16[72,2048]{1,0:T(8,128)(2,1)S(1)}, bf16[72,2048]{1,0:T(8,128)(2,1)S(1)}, u32[]{:S(2)}, u32[]{:S(2)}) collective-permute-start(bf16[72,2048]{1,0:T(8,128)(2,1)S(1)} %collective-permute-done.25.refs_0_), channel_id=1, source_target_pairs={{0,1},{1,0},{2,3},{3,2},{4,5},{5,4},{6,7},{7,6},{8,9},{9,8},{10,11... | collective-permute-start | bytes 884744 | tf_op jit(solution)/shard_map/ppermute | solution.py:375
  92.7 16.1 %collective-permute-start.18 = (bf16[72,2048]{1,0:T(8,128)(2,1)S(1)}, bf16[72,2048]{1,0:T(8,128)(2,1)S(1)}, u32[]{:S(2)}, u32[]{:S(2)}) collective-permute-start(bf16[72,2048]{1,0:T(8,128)(2,1)S(1)} %collective-permute-done.17.refs_0_), channel_id=1, source_target_pairs={{0,2},{2,0},{4,6},{6,4},{8,10},{10,8},{12,14},{14,12},{1,3},{3,1},... | collective-permute-start | bytes 884744 | tf_op jit(solution)/shard_map/ppermute | solution.py:378
  100.5 15.7 %collective-permute-start.19 = (bf16[72,2048]{1,0:T(8,128)(2,1)S(1)}, bf16[72,2048]{1,0:T(8,128)(2,1)S(1)}, u32[]{:S(2)}, u32[]{:S(2)}) collective-permute-start(bf16[72,2048]{1,0:T(8,128)(2,1)S(1)} %collective-permute-done.17.refs_0_), channel_id=1, source_target_pairs={{0,1},{1,0},{2,3},{3,2},{4,5},{5,4},{6,7},{7,6},{8,9},{9,8},{10,11... | collective-permute-start | bytes 884744 | tf_op jit(solution)/shard_map/ppermute | solution.py:375
  100.7 22.6 %collective-permute-start.15 = (bf16[72,2048]{1,0:T(8,128)(2,1)S(1)}, bf16[72,2048]{1,0:T(8,128)(2,1)S(1)}, u32[]{:S(2)}, u32[]{:S(2)}) collective-permute-start(bf16[72,2048]{1,0:T(8,128)(2,1)S(1)} %get-tuple-element.78), channel_id=1, source_target_pairs={{0,1},{1,0},{2,3},{3,2},{4,5},{5,4},{6,7},{7,6},{8,9},{9,8},{10,11... | collective-permute-start | bytes 884744 | tf_op jit(solution)/shard_map/ppermute | solution.py:375
  108.3 44.7 %collective-permute-start.14 = (bf16[72,2048]{1,0:T(8,128)(2,1)S(1)}, bf16[72,2048]{1,0:T(8,128)(2,1)S(1)}, u32[]{:S(2)}, u32[]{:S(2)}) collective-permute-start(bf16[72,2048]{1,0:T(8,128)(2,1)S(1)} %get-tuple-element.76), channel_id=1, source_target_pairs={{0,1},{1,0},{2,3},{3,2},{4,5},{5,4},{6,7},{7,6},{8,9},{9,8},{10,11... | collective-permute-start | bytes 884744 | tf_op jit(solution)/shard_map/ppermute | solution.py:375
  108.9 14.7 %collective-permute-start.38 = (bf16[72,2048]{1,0:T(8,128)(2,1)S(1)}, bf16[72,2048]{1,0:T(8,128)(2,1)S(1)}, u32[]{:S(2)}, u32[]{:S(2)}) collective-permute-start(bf16[72,2048]{1,0:T(8,128)(2,1)S(1)} %get-tuple-element.96), channel_id=1, source_target_pairs={{0,1},{1,0},{2,3},{3,2},{4,5},{5,4},{6,7},{7,6},{8,9},{9,8},{10,11... | collective-permute-start | bytes 884744 | tf_op jit(solution)/shard_map/ppermute | solution.py:375
  123.4 11.2 %collective-permute-start.29 = (bf16[72,2048]{1,0:T(8,128)(2,1)S(1)}, bf16[72,2048]{1,0:T(8,128)(2,1)S(1)}, u32[]{:S(2)}, u32[]{:S(2)}) collective-permute-start(bf16[72,2048]{1,0:T(8,128)(2,1)S(1)} %get-tuple-element.88), channel_id=1, source_target_pairs={{0,1},{1,0},{2,3},{3,2},{4,5},{5,4},{6,7},{7,6},{8,9},{9,8},{10,11... | collective-permute-start | bytes 884744 | tf_op jit(solution)/shard_map/ppermute | solution.py:375
  124.2 22.3 %collective-permute-start.21 = (bf16[72,2048]{1,0:T(8,128)(2,1)S(1)}, bf16[72,2048]{1,0:T(8,128)(2,1)S(1)}, u32[]{:S(2)}, u32[]{:S(2)}) collective-permute-start(bf16[72,2048]{1,0:T(8,128)(2,1)S(1)} %get-tuple-element.82), channel_id=1, source_target_pairs={{0,1},{1,0},{2,3},{3,2},{4,5},{5,4},{6,7},{7,6},{8,9},{9,8},{10,11... | collective-permute-start | bytes 884744 | tf_op jit(solution)/shard_map/ppermute | solution.py:375
  126.2 26.7 %collective-permute-start.16 = (bf16[72,2048]{1,0:T(8,128)(2,1)S(1)}, bf16[72,2048]{1,0:T(8,128)(2,1)S(1)}, u32[]{:S(2)}, u32[]{:S(2)}) collective-permute-start(bf16[72,2048]{1,0:T(8,128)(2,1)S(1)} %add_convert_fusion.10), channel_id=1, source_target_pairs={{0,2},{2,0},{4,6},{6,4},{8,10},{10,8},{12,14},{14,12},{1,3},{3,1},... | collective-permute-start | bytes 884744 | tf_op jit(solution)/shard_map/ppermute | solution.py:378
  133.7 12.6 %collective-permute-start.31 = (bf16[72,2048]{1,0:T(8,128)(2,1)S(1)}, bf16[72,2048]{1,0:T(8,128)(2,1)S(1)}, u32[]{:S(2)}, u32[]{:S(2)}) collective-permute-start(bf16[72,2048]{1,0:T(8,128)(2,1)S(1)} %add_convert_fusion.4), channel_id=1, source_target_pairs={{0,2},{2,0},{4,6},{6,4},{8,10},{10,8},{12,14},{14,12},{1,3},{3,1},... | collective-permute-start | bytes 884744 | tf_op jit(solution)/shard_map/ppermute | solution.py:378
  134.6 18.2 %collective-permute-start.23 = (bf16[72,2048]{1,0:T(8,128)(2,1)S(1)}, bf16[72,2048]{1,0:T(8,128)(2,1)S(1)}, u32[]{:S(2)}, u32[]{:S(2)}) collective-permute-start(bf16[72,2048]{1,0:T(8,128)(2,1)S(1)} %add_convert_fusion.7), channel_id=1, source_target_pairs={{0,2},{2,0},{4,6},{6,4},{8,10},{10,8},{12,14},{14,12},{1,3},{3,1},... | collective-permute-start | bytes 884744 | tf_op jit(solution)/shard_map/ppermute | solution.py:378
  146.4 27.7 %collective-permute-start.40 = (bf16[72,2048]{1,0:T(8,128)(2,1)S(1)}, bf16[72,2048]{1,0:T(8,128)(2,1)S(1)}, u32[]{:S(2)}, u32[]{:S(2)}) collective-permute-start(bf16[72,2048]{1,0:T(8,128)(2,1)S(1)} %add_convert_fusion), channel_id=1, source_target_pairs={{0,4},{2,6},{4,0},{6,2},{8,12},{10,14},{12,8},{14,10},{1,5},{3,7},... | collective-permute-start | bytes 884744 | tf_op jit(solution)/shard_map/ppermute | solution.py:384
  146.5 27.6 %collective-permute-start.32 = (bf16[72,2048]{1,0:T(8,128)(2,1)S(1)}, bf16[72,2048]{1,0:T(8,128)(2,1)S(1)}, u32[]{:S(2)}, u32[]{:S(2)}) collective-permute-start(bf16[72,2048]{1,0:T(8,128)(2,1)S(1)} %add_convert_fusion.3), channel_id=1, source_target_pairs={{0,12},{2,14},{4,8},{6,10},{8,4},{10,6},{12,0},{14,2},{1,13},{3,15... | collective-permute-start | bytes 884744 | tf_op jit(solution)/shard_map/ppermute | solution.py:384
  152.8 20.8 %collective-permute-start.24 = (bf16[72,2048]{1,0:T(8,128)(2,1)S(1)}, bf16[72,2048]{1,0:T(8,128)(2,1)S(1)}, u32[]{:S(2)}, u32[]{:S(2)}) collective-permute-start(bf16[72,2048]{1,0:T(8,128)(2,1)S(1)} %add_convert_fusion.6), channel_id=1, source_target_pairs={{0,8},{2,10},{4,12},{6,14},{8,0},{10,2},{12,4},{14,6},{1,9},{3,11}... | collective-permute-start | bytes 884744 | tf_op jit(solution)/shard_map/ppermute | solution.py:384
  (32 other events, 335.1 us)

commit v6 on v5

--- a/solution.py
+++ b/solution.py
@@ -341,6 +341,32 @@
         out_ref[:, columns] = total.astype(out_ref.dtype)
 
 
+def last_kernel(total_ref, *refs):
+    refs = list(refs)
+    sem = refs.pop()
+    held_ref = refs.pop()
+    out_ref = refs.pop()
+    width = 128
+    step = 4 * width
+    copies = []
+    for start in range(0, held_ref.shape[1], step):
+        columns = slice(start, start + step)
+        total = total_ref[:, columns].astype(f32)
+        for index in range(0, len(refs), 3):
+            routing_ref, weight_ref, row_ref = refs[index : index + 3]
+            weight = jnp.concatenate([weight_ref[...]] * 4, axis=1)
+            total = total + weight * dot(routing_ref[...], row_ref[:, columns])
+        held_ref[:, columns] = total.astype(held_ref.dtype)
+        block = pl.ds(start, step)
+        copy = pltpu.make_async_copy(
+            held_ref.at[:, block], out_ref.at[:, block], sem.at[start // step]
+        )
+        copy.start()
+        copies.append(copy)
+    for copy in copies:
+        copy.wait()
+
+
 def add(*terms):
     return sum(term.astype(f32) for term in terms).astype(bf16)
 
@@ -509,20 +535,34 @@
     a, b, c, d = ORDER
     early, late = (a, b), (c, d)
 
-    def combined(base, steps, kind):
+    def combined(base, steps, kind, last=False):
         operands = [base]
         for step in steps:
             operands += [*routes[2 * step : 2 * step + 2], collected[step]]
+        out = shape((local_rows, model_width), kind)
+        if last:
+            return pl.pallas_call(
+                last_kernel,
+                out_shape=out,
+                in_specs=[VMEM] * len(operands),
+                out_specs=pl.BlockSpec(memory_space=pl.ANY),
+                scratch_shapes=[
+                    pltpu.VMEM(out.shape, kind),
+                    pltpu.SemaphoreType.DMA((model_width // 512,)),
+                ],
+                compiler_params=pltpu.CompilerParams(vmem_limit_bytes=16 << 20),
+                name="combine",
+            )(*operands)
         return call(
             combine_kernel,
-            shape((local_rows, model_width), kind),
+            out,
             operands,
             flops=2 * len(steps) * ROWS * local_rows * model_width,
             moved=8 * local_rows * model_width,
         )
 
     total = combined(residual, early, f32)
-    return combined(total, late, bf16)
+    return combined(total, late, bf16, last=True)
 
 
 def solution(mesh):

time: 178 us -> 178 us (level)
    pallas_call x17 -> x16, Pallas kernels: 45 us -> 43.8 us  [call(): pl.pallas_call(kernel, out_shape=outs, in_specs=[VMEM] * len(operands), o...]
where the time goes in v6:
time: 178 us; the launch traced here: 175 us
  waiting for transfers between devices  85.3 us (48%)
  Pallas kernels  46.9 us (26%)
  starting transfers between devices  33.4 us (19%)
  local copies, waits for them, and re-layouts  7.74 us (4%)
    pallas_call x16, Pallas kernels, call(): pl.pallas_call(kernel, out_shape=outs, in_specs=[VMEM] * len(operands), o...  43.8 us
    ppermute x7, waiting for transfers between devices, planes(): lax.ppermute(x, 'expert', [(i, i ^ step * along) for i in range(chips)])  36.6 us
    ppermute x12, waiting for transfers between devices, beside(): return lax.ppermute(x, 'expert', [(i, i ^ turn) for i in range(chips)])  29.1 us
    ppermute x2, waiting for transfers between devices, upward(): lax.ppermute(x, 'expert', [(i, (i + along) % chips) for i in range(chips)])  17.8 us
    ppermute x20, starting transfers between devices, across(): return lax.ppermute(x, 'dp', [(i, i ^ 1) for i in range(cores)])  17.7 us
    ppermute x12, starting transfers between devices, beside(): return lax.ppermute(x, 'expert', [(i, i ^ turn) for i in range(chips)])  8.96 us
    unnamed x30, local copies, waits for them, and re-layouts  7.74 us
    ppermute x7, starting transfers between devices, planes(): lax.ppermute(x, 'expert', [(i, i ^ step * along) for i in range(chips)])  3.85 us
  transfers between devices with their start and end apart: 41, of which 14 were waited for; matrix products, arithmetic and copies ran while one was open for 1% of the time, Pallas kernels for 23%

profile of v6, /device:TPU:1, one launch (start us, length us, event | category | flops | bytes accessed | tf_op | source)
XLA Modules:
  0.0 175.4 jit_solution(5601846154658383145)
XLA Ops:
  5.2 2.2 %copy-done = bf16[1024,2048]{1,0:T(8,128)(2,1)S(1)} copy-done((bf16[1024,2048]{1,0:T(8,128)(2,1)S(1)}, bf16[1024,2048]{1,0:T(8,128)(2,1)}, u32[]{:S(2)}) %copy-start) | copy-done | bytes 4194328
  9.7 2.8 %collective-permute-start.3 = (bf16[256,512]{1,0:T(8,128)(2,1)S(1)}, bf16[256,512]{1,0:T(8,128)(2,1)S(1)}, u32[]{:S(2)}, u32[]{:S(2)}) collective-permute-start(bf16[256,512]{1,0:T(8,128)(2,1)S(1)} %shard_map.113.refs_0_), channel_id=1, source_target_pairs={{0,4},{2,6},{4,8},{6,10},{8,12},{10,14},{12,0},{14,2},{1,5},{3,7},... | collective-permute-start | bytes 786440 | tf_op jit(solution)/shard_map/ppermute | solution.py:407
  12.5 8.7 %collective-permute-done.3.refs_2_ = bf16[256,512]{1,0:T(8,128)(2,1)S(1)} collective-permute-done((bf16[256,512]{1,0:T(8,128)(2,1)S(1)}, bf16[256,512]{1,0:T(8,128)(2,1)S(1)}, u32[]{:S(2)}, u32[]{:S(2)}) %collective-permute-start.3) | collective-permute-done | bytes 262176 | tf_op jit(solution)/shard_map/ppermute | solution.py:407
  21.2 9.1 %collective-permute-done.4.refs_1_ = bf16[256,512]{1,0:T(8,128)(2,1)S(1)} collective-permute-done((bf16[256,512]{1,0:T(8,128)(2,1)S(1)}, bf16[256,512]{1,0:T(8,128)(2,1)S(1)}, u32[]{:S(2)}, u32[]{:S(2)}) %collective-permute-start.4) | collective-permute-done | bytes 262176 | tf_op jit(solution)/shard_map/ppermute | solution.py:407
  32.5 3.6 %collective-permute-done.5.refs_1_ = bf16[256,512]{1,0:T(8,128)(2,1)S(1)} collective-permute-done((bf16[256,512]{1,0:T(8,128)(2,1)S(1)}, bf16[256,512]{1,0:T(8,128)(2,1)S(1)}, u32[]{:S(2)}, u32[]{:S(2)}) %collective-permute-start.5) | collective-permute-done | bytes 262176 | tf_op jit(solution)/shard_map/ppermute | solution.py:410
  37.3 3.6 %shard_map.114 = (f32[8,256,128]{2,1,0:T(8,128)S(1)}, f32[8,256,128]{2,1,0:T(8,128)S(1)}, f32[8,256,128]{2,1,0:T(8,128)S(1)}) custom-call(bf16[8,256,128]{2,1,0:T(8,128)(2,1)S(1)} %shard_map.111.query_ref, bf16[256,512]{1,0:T(8,128)(2,1)S(1)} %shard_map.113.refs_0_, bf16[256,512]{1,0:T(8,128)(2,1)S(1)} %collective-permute-done.9.refs_1_, ...), custom_call_target="tpu_custom_call" | custom-call | flops 805306368 | bytes 2097152 | tf_op jit(solution)/shard_map/pallas_call | solution.py:35
  41.8 2.9 %shard_map.115 = (f32[8,256,128]{2,1,0:T(8,128)S(1)}, f32[8,256,128]{2,1,0:T(8,128)S(1)}, f32[8,256,128]{2,1,0:T(8,128)S(1)}) custom-call(bf16[8,256,128]{2,1,0:T(8,128)(2,1)S(1)} %shard_map.111.query_ref, bf16[256,512]{1,0:T(8,128)(2,1)S(1)} %collective-permute-done.8.refs_0_, bf16[256,512]{1,0:T(8,128)(2,1)S(1)} %collective-permute-done.4.refs_1_, ...), custom_call_target="tpu_custom_call" | custom-call | flops 536870912 | bytes 2097152 | tf_op jit(solution)/shard_map/pallas_call | solution.py:35
  44.7 2.7 %collective-permute-done.7.refs_0_ = bf16[256,512]{1,0:T(8,128)(2,1)S(1)} collective-permute-done((bf16[256,512]{1,0:T(8,128)(2,1)S(1)}, bf16[256,512]{1,0:T(8,128)(2,1)S(1)}, u32[]{:S(2)}, u32[]{:S(2)}) %collective-permute-start.7) | collective-permute-done | bytes 262176 | tf_op jit(solution)/shard_map/ppermute | solution.py:404
  47.4 2.9 %shard_map.116 = (f32[8,256,128]{2,1,0:T(8,128)S(1)}, f32[8,256,128]{2,1,0:T(8,128)S(1)}, f32[8,256,128]{2,1,0:T(8,128)S(1)}) custom-call(bf16[8,256,128]{2,1,0:T(8,128)(2,1)S(1)} %shard_map.111.query_ref, bf16[256,512]{1,0:T(8,128)(2,1)S(1)} %collective-permute-done.7.refs_0_, bf16[256,512]{1,0:T(8,128)(2,1)S(1)} %collective-permute-done.5.refs_1_, ...), custom_call_target="tpu_custom_call" | custom-call | flops 536870912 | bytes 2097152 | tf_op jit(solution)/shard_map/pallas_call | solution.py:35
  50.3 2.7 %collective-permute-done.6.refs_0_ = bf16[256,512]{1,0:T(8,128)(2,1)S(1)} collective-permute-done((bf16[256,512]{1,0:T(8,128)(2,1)S(1)}, bf16[256,512]{1,0:T(8,128)(2,1)S(1)}, u32[]{:S(2)}, u32[]{:S(2)}) %collective-permute-start.6) | collective-permute-done | bytes 262176 | tf_op jit(solution)/shard_map/ppermute | solution.py:404
  53.0 3.0 %shard_map.117 = (bf16[128,2048]{1,0:T(8,128)(2,1)S(1)}, f32[128,2048]{1,0:T(8,128)S(1)}) custom-call(bf16[8,256,128]{2,1,0:T(8,128)(2,1)S(1)} %shard_map.111.query_ref, bf16[256,512]{1,0:T(8,128)(2,1)S(1)} %collective-permute-done.6.refs_0_, f32[8,256,128]{2,1,0:T(8,128)S(1)} %get-tuple-element.63.refs_1_, f32[8,256,128]{2,1,0:T(8,128)S(1)} %get-tuple-element.64.refs_2_, ...), custom_call_target="tpu_custom_call" | custom-call | flops 1342177280 | bytes 2097152 | tf_op jit(solution)/shard_map/pallas_call | solution.py:35
  56.0 2.9 %collective-permute-start.10 = (bf16[128,2048]{1,0:T(8,128)(2,1)S(1)}, bf16[128,2048]{1,0:T(8,128)(2,1)S(1)}, u32[]{:S(2)}, u32[]{:S(2)}) collective-permute-start(bf16[128,2048]{1,0:T(8,128)(2,1)S(1)} %get-tuple-element.67), channel_id=1, source_target_pairs={{0,1},{1,0},{2,3},{3,2},{4,5},{5,4},{6,7},{7,6},{8,9},{9,8},{10,11... | collective-permute-start | bytes 1572872 | tf_op jit(solution)/shard_map/ppermute | solution.py:401
  66.2 4.1 %collective-permute-done.33.refs_0_ = bf16[72,2048]{1,0:T(8,128)(2,1)S(1)} collective-permute-done((bf16[72,2048]{1,0:T(8,128)(2,1)S(1)}, bf16[72,2048]{1,0:T(8,128)(2,1)S(1)}, u32[]{:S(2)}, u32[]{:S(2)}) %collective-permute-start.33) | collective-permute-done | bytes 294944 | tf_op jit(solution)/shard_map/ppermute | solution.py:410
  71.0 6.7 %collective-permute-start.13 = (bf16[72,2048]{1,0:T(8,128)(2,1)S(1)}, bf16[72,2048]{1,0:T(8,128)(2,1)S(1)}, u32[]{:S(2)}, u32[]{:S(2)}) collective-permute-start(bf16[72,2048]{1,0:T(8,128)(2,1)S(1)} %collective-permute-done.11.refs_1_), channel_id=1, source_target_pairs={{0,1},{1,0},{2,3},{3,2},{4,5},{5,4},{6,7},{7,6},{8,9},{9,8},{10,11... | collective-permute-start | bytes 884744 | tf_op jit(solution)/shard_map/ppermute | solution.py:401
  81.9 8.3 %collective-permute-done.17.refs_0_ = bf16[72,2048]{1,0:T(8,128)(2,1)S(1)} collective-permute-done((bf16[72,2048]{1,0:T(8,128)(2,1)S(1)}, bf16[72,2048]{1,0:T(8,128)(2,1)S(1)}, u32[]{:S(2)}, u32[]{:S(2)}) %collective-permute-start.17) | collective-permute-done | bytes 294944 | tf_op jit(solution)/shard_map/ppermute | solution.py:410
  90.8 1.9 %collective-permute-start.27 = (bf16[72,2048]{1,0:T(8,128)(2,1)S(1)}, bf16[72,2048]{1,0:T(8,128)(2,1)S(1)}, u32[]{:S(2)}, u32[]{:S(2)}) collective-permute-start(bf16[72,2048]{1,0:T(8,128)(2,1)S(1)} %collective-permute-done.25.refs_0_), channel_id=1, source_target_pairs={{0,1},{1,0},{2,3},{3,2},{4,5},{5,4},{6,7},{7,6},{8,9},{9,8},{10,11... | collective-permute-start | bytes 884744 | tf_op jit(solution)/shard_map/ppermute | solution.py:401
  93.9 6.6 %shard_map.120 = (bf16[72,2048]{1,0:T(8,128)(2,1)S(1)}, bf16[72,2048]{1,0:T(8,128)(2,1)S(1)}, bf16[72,2048]{1,0:T(8,128)(2,1)S(1)}, bf16[72,2048]{1,0:T(8,128)(2,1)S(1)}) custom-call(bf16[2048,1792]{1,0:T(8,128)(2,1)S(1)} %fetch.5.gate_ref, bf16[2048,1792]{1,0:T(8,128)(2,1)S(1)} %fetch.6.up_ref, bf16[1792,2048]{1,0:T(8,128)(2,1)S(1)} %fetch.7.down_ref, ...), custom_call_target="tpu_custom_call" | custom-call | flops 6341787648 | bytes 22020096 | tf_op jit(solution)/shard_map/pallas_call | solution.py:35
  101.7 6.6 %shard_map.124 = (bf16[72,2048]{1,0:T(8,128)(2,1)S(1)}, bf16[72,2048]{1,0:T(8,128)(2,1)S(1)}, bf16[72,2048]{1,0:T(8,128)(2,1)S(1)}, bf16[72,2048]{1,0:T(8,128)(2,1)S(1)}) custom-call(bf16[2048,1792]{1,0:T(8,128)(2,1)S(1)} %fetch.5.gate_ref, bf16[2048,1792]{1,0:T(8,128)(2,1)S(1)} %fetch.6.up_ref, bf16[1792,2048]{1,0:T(8,128)(2,1)S(1)} %fetch.7.down_ref, ...), custom_call_target="tpu_custom_call" | custom-call | flops 6341787648 | bytes 22020096 | tf_op jit(solution)/shard_map/pallas_call | solution.py:35
  109.3 6.8 %shard_map.123 = (bf16[72,2048]{1,0:T(8,128)(2,1)S(1)}, bf16[72,2048]{1,0:T(8,128)(2,1)S(1)}, bf16[72,2048]{1,0:T(8,128)(2,1)S(1)}, bf16[72,2048]{1,0:T(8,128)(2,1)S(1)}) custom-call(bf16[2048,1792]{1,0:T(8,128)(2,1)S(1)} %fetch.5.gate_ref, bf16[2048,1792]{1,0:T(8,128)(2,1)S(1)} %fetch.6.up_ref, bf16[1792,2048]{1,0:T(8,128)(2,1)S(1)} %fetch.7.down_ref, ...), custom_call_target="tpu_custom_call" | custom-call | flops 6341787648 | bytes 22020096 | tf_op jit(solution)/shard_map/pallas_call | solution.py:35
  116.8 6.6 %shard_map.121 = (bf16[72,2048]{1,0:T(8,128)(2,1)S(1)}, bf16[72,2048]{1,0:T(8,128)(2,1)S(1)}, bf16[72,2048]{1,0:T(8,128)(2,1)S(1)}, bf16[72,2048]{1,0:T(8,128)(2,1)S(1)}) custom-call(bf16[2048,1792]{1,0:T(8,128)(2,1)S(1)} %fetch.5.gate_ref, bf16[2048,1792]{1,0:T(8,128)(2,1)S(1)} %fetch.6.up_ref, bf16[1792,2048]{1,0:T(8,128)(2,1)S(1)} %fetch.7.down_ref, ...), custom_call_target="tpu_custom_call" | custom-call | flops 6341787648 | bytes 22020096 | tf_op jit(solution)/shard_map/pallas_call | solution.py:35
  127.0 6.7 %collective-permute-done.39 = bf16[72,2048]{1,0:T(8,128)(2,1)S(1)} collective-permute-done((bf16[72,2048]{1,0:T(8,128)(2,1)S(1)}, bf16[72,2048]{1,0:T(8,128)(2,1)S(1)}, u32[]{:S(2)}, u32[]{:S(2)}) %collective-permute-start.39) | collective-permute-done | bytes 294944 | tf_op jit(solution)/shard_map/ppermute | solution.py:404
  135.4 11.0 %collective-permute-done.31 = bf16[72,2048]{1,0:T(8,128)(2,1)S(1)} collective-permute-done((bf16[72,2048]{1,0:T(8,128)(2,1)S(1)}, bf16[72,2048]{1,0:T(8,128)(2,1)S(1)}, u32[]{:S(2)}, u32[]{:S(2)}) %collective-permute-start.31) | collective-permute-done | bytes 294944 | tf_op jit(solution)/shard_map/ppermute | solution.py:404
  147.5 5.2 %collective-permute-done.23 = bf16[72,2048]{1,0:T(8,128)(2,1)S(1)} collective-permute-done((bf16[72,2048]{1,0:T(8,128)(2,1)S(1)}, bf16[72,2048]{1,0:T(8,128)(2,1)S(1)}, u32[]{:S(2)}, u32[]{:S(2)}) %collective-permute-start.23) | collective-permute-done | bytes 294944 | tf_op jit(solution)/shard_map/ppermute | solution.py:404
  153.0 20.6 %collective-permute-done.24.refs_5_ = bf16[72,2048]{1,0:T(8,128)(2,1)S(1)} collective-permute-done((bf16[72,2048]{1,0:T(8,128)(2,1)S(1)}, bf16[72,2048]{1,0:T(8,128)(2,1)S(1)}, u32[]{:S(2)}, u32[]{:S(2)}) %collective-permute-start.24) | collective-permute-done | bytes 294944 | tf_op jit(solution)/shard_map/ppermute | solution.py:410
  (124 shorter events, 36.5 us)
Async XLA Ops:
  8.7 28.2 %collective-permute-start.1 = (f32[256,1024]{1,0:T(8,128)S(1)}, f32[256,1024]{1,0:T(8,128)S(1)}, u32[]{:S(2)}, u32[]{:S(2)}) collective-permute-start(f32[256,1024]{1,0:T(8,128)S(1)} %get-tuple-element.54), channel_id=1, source_target_pairs={{0,1},{1,0},{2,3},{3,2},{4,5},{5,4},{6,7},{7,6},{8,9},{9,8},{10,11... | collective-permute-start | bytes 3145736 | tf_op jit(solution)/shard_map/ppermute | solution.py:401
  9.7 11.5 %collective-permute-start.3 = (bf16[256,512]{1,0:T(8,128)(2,1)S(1)}, bf16[256,512]{1,0:T(8,128)(2,1)S(1)}, u32[]{:S(2)}, u32[]{:S(2)}) collective-permute-start(bf16[256,512]{1,0:T(8,128)(2,1)S(1)} %shard_map.113.refs_0_), channel_id=1, source_target_pairs={{0,4},{2,6},{4,8},{6,10},{8,12},{10,14},{12,0},{14,2},{1,5},{3,7},... | collective-permute-start | bytes 786440 | tf_op jit(solution)/shard_map/ppermute | solution.py:407
  31.7 15.6 %collective-permute-start.7 = (bf16[256,512]{1,0:T(8,128)(2,1)S(1)}, bf16[256,512]{1,0:T(8,128)(2,1)S(1)}, u32[]{:S(2)}, u32[]{:S(2)}) collective-permute-start(bf16[256,512]{1,0:T(8,128)(2,1)S(1)} %collective-permute-done.4.refs_1_), channel_id=1, source_target_pairs={{0,2},{2,0},{4,6},{6,4},{8,10},{10,8},{12,14},{14,12},{1,3},{3,1},... | collective-permute-start | bytes 786440 | tf_op jit(solution)/shard_map/ppermute | solution.py:404
  36.1 16.9 %collective-permute-start.6 = (bf16[256,512]{1,0:T(8,128)(2,1)S(1)}, bf16[256,512]{1,0:T(8,128)(2,1)S(1)}, u32[]{:S(2)}, u32[]{:S(2)}) collective-permute-start(bf16[256,512]{1,0:T(8,128)(2,1)S(1)} %collective-permute-done.5.refs_1_), channel_id=1, source_target_pairs={{0,2},{2,0},{4,6},{6,4},{8,10},{10,8},{12,14},{14,12},{1,3},{3,1},... | collective-permute-start | bytes 786440 | tf_op jit(solution)/shard_map/ppermute | solution.py:404
  63.6 18.2 %collective-permute-start.25 = (bf16[72,2048]{1,0:T(8,128)(2,1)S(1)}, bf16[72,2048]{1,0:T(8,128)(2,1)S(1)}, u32[]{:S(2)}, u32[]{:S(2)}) collective-permute-start(bf16[72,2048]{1,0:T(8,128)(2,1)S(1)} %get-tuple-element.86), channel_id=1, source_target_pairs={{0,12},{2,14},{4,8},{6,10},{8,4},{10,6},{12,0},{14,2},{1,13},{3,15... | collective-permute-start | bytes 884744 | tf_op jit(solution)/shard_map/ppermute | solution.py:410
  63.6 26.5 %collective-permute-start.17 = (bf16[72,2048]{1,0:T(8,128)(2,1)S(1)}, bf16[72,2048]{1,0:T(8,128)(2,1)S(1)}, u32[]{:S(2)}, u32[]{:S(2)}) collective-permute-start(bf16[72,2048]{1,0:T(8,128)(2,1)S(1)} %get-tuple-element.80), channel_id=1, source_target_pairs={{0,8},{2,10},{4,12},{6,14},{8,0},{10,2},{12,4},{14,6},{1,9},{3,11}... | collective-permute-start | bytes 884744 | tf_op jit(solution)/shard_map/ppermute | solution.py:410
  64.9 25.9 %collective-permute-start.12 = (bf16[72,2048]{1,0:T(8,128)(2,1)S(1)}, bf16[72,2048]{1,0:T(8,128)(2,1)S(1)}, u32[]{:S(2)}, u32[]{:S(2)}) collective-permute-start(bf16[72,2048]{1,0:T(8,128)(2,1)S(1)} %get-tuple-element.74.refs_0_), channel_id=1, source_target_pairs={{0,1},{1,0},{2,3},{3,2},{4,5},{5,4},{6,7},{7,6},{8,9},{9,8},{10,11... | collective-permute-start | bytes 884744 | tf_op jit(solution)/shard_map/ppermute | solution.py:401
  70.4 22.4 %collective-permute-start.34 = (bf16[72,2048]{1,0:T(8,128)(2,1)S(1)}, bf16[72,2048]{1,0:T(8,128)(2,1)S(1)}, u32[]{:S(2)}, u32[]{:S(2)}) collective-permute-start(bf16[72,2048]{1,0:T(8,128)(2,1)S(1)} %collective-permute-done.33.refs_0_), channel_id=1, source_target_pairs={{0,2},{2,0},{4,6},{6,4},{8,10},{10,8},{12,14},{14,12},{1,3},{3,1},... | collective-permute-start | bytes 884744 | tf_op jit(solution)/shard_map/ppermute | solution.py:404
  71.0 22.6 %collective-permute-start.13 = (bf16[72,2048]{1,0:T(8,128)(2,1)S(1)}, bf16[72,2048]{1,0:T(8,128)(2,1)S(1)}, u32[]{:S(2)}, u32[]{:S(2)}) collective-permute-start(bf16[72,2048]{1,0:T(8,128)(2,1)S(1)} %collective-permute-done.11.refs_1_), channel_id=1, source_target_pairs={{0,1},{1,0},{2,3},{3,2},{4,5},{5,4},{6,7},{7,6},{8,9},{9,8},{10,11... | collective-permute-start | bytes 884744 | tf_op jit(solution)/shard_map/ppermute | solution.py:401
  81.8 18.7 %collective-permute-start.35 = (bf16[72,2048]{1,0:T(8,128)(2,1)S(1)}, bf16[72,2048]{1,0:T(8,128)(2,1)S(1)}, u32[]{:S(2)}, u32[]{:S(2)}) collective-permute-start(bf16[72,2048]{1,0:T(8,128)(2,1)S(1)} %collective-permute-done.33.refs_0_), channel_id=1, source_target_pairs={{0,1},{1,0},{2,3},{3,2},{4,5},{5,4},{6,7},{7,6},{8,9},{9,8},{10,11... | collective-permute-start | bytes 884744 | tf_op jit(solution)/shard_map/ppermute | solution.py:401
  90.8 17.5 %collective-permute-start.27 = (bf16[72,2048]{1,0:T(8,128)(2,1)S(1)}, bf16[72,2048]{1,0:T(8,128)(2,1)S(1)}, u32[]{:S(2)}, u32[]{:S(2)}) collective-permute-start(bf16[72,2048]{1,0:T(8,128)(2,1)S(1)} %collective-permute-done.25.refs_0_), channel_id=1, source_target_pairs={{0,1},{1,0},{2,3},{3,2},{4,5},{5,4},{6,7},{7,6},{8,9},{9,8},{10,11... | collective-permute-start | bytes 884744 | tf_op jit(solution)/shard_map/ppermute | solution.py:401
  92.7 16.1 %collective-permute-start.18 = (bf16[72,2048]{1,0:T(8,128)(2,1)S(1)}, bf16[72,2048]{1,0:T(8,128)(2,1)S(1)}, u32[]{:S(2)}, u32[]{:S(2)}) collective-permute-start(bf16[72,2048]{1,0:T(8,128)(2,1)S(1)} %collective-permute-done.17.refs_0_), channel_id=1, source_target_pairs={{0,2},{2,0},{4,6},{6,4},{8,10},{10,8},{12,14},{14,12},{1,3},{3,1},... | collective-permute-start | bytes 884744 | tf_op jit(solution)/shard_map/ppermute | solution.py:404
  100.5 15.7 %collective-permute-start.19 = (bf16[72,2048]{1,0:T(8,128)(2,1)S(1)}, bf16[72,2048]{1,0:T(8,128)(2,1)S(1)}, u32[]{:S(2)}, u32[]{:S(2)}) collective-permute-start(bf16[72,2048]{1,0:T(8,128)(2,1)S(1)} %collective-permute-done.17.refs_0_), channel_id=1, source_target_pairs={{0,1},{1,0},{2,3},{3,2},{4,5},{5,4},{6,7},{7,6},{8,9},{9,8},{10,11... | collective-permute-start | bytes 884744 | tf_op jit(solution)/shard_map/ppermute | solution.py:401
  100.7 22.6 %collective-permute-start.15 = (bf16[72,2048]{1,0:T(8,128)(2,1)S(1)}, bf16[72,2048]{1,0:T(8,128)(2,1)S(1)}, u32[]{:S(2)}, u32[]{:S(2)}) collective-permute-start(bf16[72,2048]{1,0:T(8,128)(2,1)S(1)} %get-tuple-element.78), channel_id=1, source_target_pairs={{0,1},{1,0},{2,3},{3,2},{4,5},{5,4},{6,7},{7,6},{8,9},{9,8},{10,11... | collective-permute-start | bytes 884744 | tf_op jit(solution)/shard_map/ppermute | solution.py:401
  108.3 44.7 %collective-permute-start.14 = (bf16[72,2048]{1,0:T(8,128)(2,1)S(1)}, bf16[72,2048]{1,0:T(8,128)(2,1)S(1)}, u32[]{:S(2)}, u32[]{:S(2)}) collective-permute-start(bf16[72,2048]{1,0:T(8,128)(2,1)S(1)} %get-tuple-element.76), channel_id=1, source_target_pairs={{0,1},{1,0},{2,3},{3,2},{4,5},{5,4},{6,7},{7,6},{8,9},{9,8},{10,11... | collective-permute-start | bytes 884744 | tf_op jit(solution)/shard_map/ppermute | solution.py:401
  108.9 14.7 %collective-permute-start.38 = (bf16[72,2048]{1,0:T(8,128)(2,1)S(1)}, bf16[72,2048]{1,0:T(8,128)(2,1)S(1)}, u32[]{:S(2)}, u32[]{:S(2)}) collective-permute-start(bf16[72,2048]{1,0:T(8,128)(2,1)S(1)} %get-tuple-element.96), channel_id=1, source_target_pairs={{0,1},{1,0},{2,3},{3,2},{4,5},{5,4},{6,7},{7,6},{8,9},{9,8},{10,11... | collective-permute-start | bytes 884744 | tf_op jit(solution)/shard_map/ppermute | solution.py:401
  123.4 11.2 %collective-permute-start.29 = (bf16[72,2048]{1,0:T(8,128)(2,1)S(1)}, bf16[72,2048]{1,0:T(8,128)(2,1)S(1)}, u32[]{:S(2)}, u32[]{:S(2)}) collective-permute-start(bf16[72,2048]{1,0:T(8,128)(2,1)S(1)} %get-tuple-element.88), channel_id=1, source_target_pairs={{0,1},{1,0},{2,3},{3,2},{4,5},{5,4},{6,7},{7,6},{8,9},{9,8},{10,11... | collective-permute-start | bytes 884744 | tf_op jit(solution)/shard_map/ppermute | solution.py:401
  124.2 22.3 %collective-permute-start.21 = (bf16[72,2048]{1,0:T(8,128)(2,1)S(1)}, bf16[72,2048]{1,0:T(8,128)(2,1)S(1)}, u32[]{:S(2)}, u32[]{:S(2)}) collective-permute-start(bf16[72,2048]{1,0:T(8,128)(2,1)S(1)} %get-tuple-element.82), channel_id=1, source_target_pairs={{0,1},{1,0},{2,3},{3,2},{4,5},{5,4},{6,7},{7,6},{8,9},{9,8},{10,11... | collective-permute-start | bytes 884744 | tf_op jit(solution)/shard_map/ppermute | solution.py:401
  126.2 26.7 %collective-permute-start.16 = (bf16[72,2048]{1,0:T(8,128)(2,1)S(1)}, bf16[72,2048]{1,0:T(8,128)(2,1)S(1)}, u32[]{:S(2)}, u32[]{:S(2)}) collective-permute-start(bf16[72,2048]{1,0:T(8,128)(2,1)S(1)} %add_convert_fusion.10), channel_id=1, source_target_pairs={{0,2},{2,0},{4,6},{6,4},{8,10},{10,8},{12,14},{14,12},{1,3},{3,1},... | collective-permute-start | bytes 884744 | tf_op jit(solution)/shard_map/ppermute | solution.py:404
  133.7 12.6 %collective-permute-start.31 = (bf16[72,2048]{1,0:T(8,128)(2,1)S(1)}, bf16[72,2048]{1,0:T(8,128)(2,1)S(1)}, u32[]{:S(2)}, u32[]{:S(2)}) collective-permute-start(bf16[72,2048]{1,0:T(8,128)(2,1)S(1)} %add_convert_fusion.4), channel_id=1, source_target_pairs={{0,2},{2,0},{4,6},{6,4},{8,10},{10,8},{12,14},{14,12},{1,3},{3,1},... | collective-permute-start | bytes 884744 | tf_op jit(solution)/shard_map/ppermute | solution.py:404
  134.6 18.2 %collective-permute-start.23 = (bf16[72,2048]{1,0:T(8,128)(2,1)S(1)}, bf16[72,2048]{1,0:T(8,128)(2,1)S(1)}, u32[]{:S(2)}, u32[]{:S(2)}) collective-permute-start(bf16[72,2048]{1,0:T(8,128)(2,1)S(1)} %add_convert_fusion.7), channel_id=1, source_target_pairs={{0,2},{2,0},{4,6},{6,4},{8,10},{10,8},{12,14},{14,12},{1,3},{3,1},... | collective-permute-start | bytes 884744 | tf_op jit(solution)/shard_map/ppermute | solution.py:404
  146.4 27.7 %collective-permute-start.40 = (bf16[72,2048]{1,0:T(8,128)(2,1)S(1)}, bf16[72,2048]{1,0:T(8,128)(2,1)S(1)}, u32[]{:S(2)}, u32[]{:S(2)}) collective-permute-start(bf16[72,2048]{1,0:T(8,128)(2,1)S(1)} %add_convert_fusion), channel_id=1, source_target_pairs={{0,4},{2,6},{4,0},{6,2},{8,12},{10,14},{12,8},{14,10},{1,5},{3,7},... | collective-permute-start | bytes 884744 | tf_op jit(solution)/shard_map/ppermute | solution.py:410
  146.5 27.6 %collective-permute-start.32 = (bf16[72,2048]{1,0:T(8,128)(2,1)S(1)}, bf16[72,2048]{1,0:T(8,128)(2,1)S(1)}, u32[]{:S(2)}, u32[]{:S(2)}) collective-permute-start(bf16[72,2048]{1,0:T(8,128)(2,1)S(1)} %add_convert_fusion.3), channel_id=1, source_target_pairs={{0,12},{2,14},{4,8},{6,10},{8,4},{10,6},{12,0},{14,2},{1,13},{3,15... | collective-permute-start | bytes 884744 | tf_op jit(solution)/shard_map/ppermute | solution.py:410
  152.8 20.8 %collective-permute-start.24 = (bf16[72,2048]{1,0:T(8,128)(2,1)S(1)}, bf16[72,2048]{1,0:T(8,128)(2,1)S(1)}, u32[]{:S(2)}, u32[]{:S(2)}) collective-permute-start(bf16[72,2048]{1,0:T(8,128)(2,1)S(1)} %add_convert_fusion.6), channel_id=1, source_target_pairs={{0,8},{2,10},{4,12},{6,14},{8,0},{10,2},{12,4},{14,6},{1,9},{3,11}... | collective-permute-start | bytes 884744 | tf_op jit(solution)/shard_map/ppermute | solution.py:410
  (32 other events, 335.1 us)
